TPU v7x, 32 devices: a whole 2x2x4 slice. The times are simulated.
32 devices in a mesh: emb: 32 (over z, y, x, core).
Axes of the slice: x: 2, y: 2, z: 4, core: 2. Of those that a mesh axis runs over, the one named last changes fastest.
Arguments:
- x_start: bfloat16 [65536, 1024], P('emb')
- d_out: bfloat16 [65536, 1024], P('emb')
- token_ids: int32 [2, 65536, 4], P(None, 'emb')
- w_up: bfloat16 [4, 1024, 4096], replicated
- w_down: bfloat16 [4, 4096, 1024], replicated
- w_gate: bfloat16 [2, 1024, 1024], replicated
- w_proj: bfloat16 [2, 1024, 1024], replicated
- tables: bfloat16 [2, 131072, 256], P(None, 'emb')
Outputs:
- output 1: bfloat16 [65536, 1024], P('emb')
- output 2: float32 [2, 131072, 256], P(None, 'emb')
All inputs are finite; a program needn't handle non-finite values.
Results may differ from a plain program's by a relative error of at most 0.0153688.
Values are sent between devices in bfloat16 or wider.
A program may use at most 1 GiB of HBM per device.

v0:
```python
import jax
import jax.numpy as jnp
from jax import lax
from jax.sharding import PartitionSpec as P

EPS = 1e-6


def gelu_fn(pre_act):
    return jax.nn.gelu(pre_act, approximate=True)


def gelu_grad(pre_act, cotangent):
    _, pullback = jax.vjp(gelu_fn, pre_act.astype(jnp.float32))
    return pullback(cotangent)[0]


def norm_fwd(x_res):
    x_f = x_res.astype(jnp.float32)
    inv_rms = lax.rsqrt(jnp.mean(x_f * x_f, axis=-1, keepdims=True) + EPS)
    return (x_f * inv_rms).astype(jnp.bfloat16), inv_rms


def norm_bwd(x_res, inv_rms, d_norm):
    x_f = x_res.astype(jnp.float32)
    mean_dot = jnp.mean(x_f * d_norm, axis=-1, keepdims=True)
    return inv_rms * d_norm - x_f * (inv_rms * inv_rms * inv_rms) * mean_dot


def slot_map(layers):
    return {1: 0, layers - 1: 1}


def stack_forward(x_start, w_up, w_down, w_gate, w_proj, fetch_rows):
    layers = w_up.shape[0]
    slot_of = slot_map(layers)
    saved_acts = []
    x_cur = x_start
    for layer_idx in range(layers):
        normed, inv_rms = norm_fwd(x_cur)
        hidden = jnp.dot(normed, w_up[layer_idx], preferred_element_type=jnp.float32).astype(jnp.bfloat16)
        activated = gelu_fn(hidden.astype(jnp.float32)).astype(jnp.bfloat16)
        mlp_out = jnp.dot(activated, w_down[layer_idx], preferred_element_type=jnp.float32).astype(jnp.bfloat16)
        new_res = x_cur.astype(jnp.float32) + mlp_out.astype(jnp.float32)
        gate_saved = None
        if layer_idx in slot_of:
            which = slot_of[layer_idx]
            emb_rows = fetch_rows(which)
            pre_gate = jnp.dot(normed, w_gate[which], preferred_element_type=jnp.float32).astype(jnp.bfloat16)
            gate_val = gelu_fn(pre_gate.astype(jnp.float32)).astype(jnp.bfloat16)
            mixed_val = (gate_val.astype(jnp.float32) * emb_rows.astype(jnp.float32)).astype(jnp.bfloat16)
            proj_out = jnp.dot(mixed_val, w_proj[which], preferred_element_type=jnp.float32).astype(jnp.bfloat16)
            new_res = new_res + proj_out.astype(jnp.float32)
            gate_saved = (pre_gate, gate_val, emb_rows)
        saved_acts.append((x_cur, inv_rms, hidden, gate_saved))
        x_cur = new_res.astype(jnp.bfloat16)
    return x_cur, saved_acts


def stack_backward(d_out, w_up, w_down, w_gate, w_proj, saved_acts, return_rows):
    layers = w_up.shape[0]
    slot_of = slot_map(layers)
    table_grads = [None, None]
    d_res = d_out.astype(jnp.float32)
    for layer_idx in reversed(range(1, layers)):
        x_prev, inv_rms, hidden, gate_saved = saved_acts[layer_idx]
        d_low = d_res.astype(jnp.bfloat16)
        if gate_saved is not None:
            which = slot_of[layer_idx]
            pre_gate, gate_val, emb_rows = gate_saved
            d_mix = jnp.einsum('td,ed->te', d_low, w_proj[which], preferred_element_type=jnp.float32)
            table_grads[which] = return_rows(which, gate_val.astype(jnp.float32) * d_mix)
        if layer_idx > 1:
            d_act = jnp.einsum('td,fd->tf', d_low, w_down[layer_idx], preferred_element_type=jnp.float32)
            d_hid = gelu_grad(hidden, d_act)
            d_norm = jnp.einsum('tf,df->td', d_hid.astype(jnp.bfloat16), w_up[layer_idx], preferred_element_type=jnp.float32)
            if gate_saved is not None:
                d_gate = gelu_grad(pre_gate, d_mix * emb_rows.astype(jnp.float32))
                d_norm = d_norm + jnp.einsum('te,de->td', d_gate.astype(jnp.bfloat16), w_gate[which], preferred_element_type=jnp.float32)
            d_res = d_res + norm_bwd(x_prev, inv_rms, d_norm)
    return table_grads


def route_plan(flat_ids, rows_dev, n_dev, capacity):
    owner_ids = flat_ids // rows_dev
    sort_order = jnp.argsort(owner_ids, stable=True)
    sorted_owner = owner_ids[sort_order]
    counts = jax.ops.segment_sum(jnp.ones_like(owner_ids), owner_ids, num_segments=n_dev)
    starts = jnp.cumsum(counts) - counts
    sorted_slot = sorted_owner * capacity + jnp.arange(flat_ids.shape[0], dtype=jnp.int32) - starts[sorted_owner]
    return jnp.zeros_like(flat_ids).at[sort_order].set(sorted_slot)


def solution(mesh):
    n_dev = mesh.shape['emb']
    tok_spec = P('emb', None)
    tab_spec = P(None, 'emb', None)

    def local_program(x_start, d_out, token_ids, w_up, w_down, w_gate, w_proj, tables):
        n_tok, n_heads = token_ids.shape[1], token_ids.shape[2]
        rows_dev, row_width = tables.shape[1], tables.shape[2]
        capacity = max(8, (4 * n_tok * n_heads) // n_dev)
        my_base = lax.axis_index('emb') * rows_dev
        pad_ids = (jnp.arange(n_dev * capacity, dtype=jnp.int32) // capacity) * rows_dev
        routes = {}

        def fetch_rows(which):
            flat_ids = token_ids[which].reshape(n_tok * n_heads)
            dest_slot = route_plan(flat_ids, rows_dev, n_dev, capacity)
            send_ids = pad_ids.at[dest_slot].set(flat_ids)
            recv_ids = lax.all_to_all(send_ids, 'emb', 0, 0, tiled=True)
            local_ids = recv_ids - my_base
            served = tables[which][local_ids]
            back_rows = lax.all_to_all(served, 'emb', 0, 0, tiled=True)
            routes[which] = (dest_slot, local_ids)
            return back_rows[dest_slot].reshape(n_tok, n_heads * row_width)

        def return_rows(which, grad_rows):
            dest_slot, local_ids = routes[which]
            send_grad = jnp.zeros((n_dev * capacity, row_width), jnp.float32).at[dest_slot].set(grad_rows.reshape(n_tok * n_heads, row_width))
            recv_grad = lax.all_to_all(send_grad, 'emb', 0, 0, tiled=True)
            return jax.ops.segment_sum(recv_grad, local_ids, num_segments=rows_dev)

        x_end, saved_acts = stack_forward(x_start, w_up, w_down, w_gate, w_proj, fetch_rows)
        table_grads = stack_backward(d_out, w_up, w_down, w_gate, w_proj, saved_acts, return_rows)
        return x_end, jnp.stack(table_grads)

    return jax.shard_map(local_program, mesh=mesh, in_specs=(tok_spec, tok_spec, tab_spec, P(), P(), P(), P(), tab_spec), out_specs=(tok_spec, tab_spec), check_vma=False)
```

profile of v0, /device:TPU:21, one launch (start us, length us, event | category | flops | bytes accessed | tf_op | source)
XLA Modules:
  0.0 3009.7 jit_solution(12008186083212391853)
XLA Ops:
  4.0 57.0 %scatter_custom_fusion = s32[32]{0:T(128)S(1)} fusion(s32[8192]{0:T(1024)S(1)} %bitcast.246, s32[8192]{0:T(1024)S(1)} %ne.86, s32[]{:T(128)} %constant.80.clone.1), kind=kCustom, calls=%fused_computation.333 | custom fusion | flops 8192 | bytes 132 | tf_op jit(solution)/shard_map/scatter-add | solution.py:88
  71.1 45.5 %gather_fusion = s32[8192]{0:T(1024)S(1)} fusion(s32[8192]{0:T(1024)S(1)} %add_select_fusion.2, s32[8192]{0:T(1024)S(1)} %get-tuple-element.76), kind=kCustom, calls=%fused_computation | custom fusion | bytes 98304 | tf_op jit(solution)/shard_map/gather | solution.py:87
  139.4 42.3 %scatter_custom_fusion.1 = s32[8192]{0:T(1024)S(1)} fusion(s32[8192]{0:T(1024)S(1)} %get-tuple-element.77, s32[8192]{0:T(1024)S(1)} %select_subtract_fusion.1, s32[]{:T(128)} %constant.80.clone.1), kind=kCustom, calls=%fused_computation.319 | custom fusion | bytes 32772 | tf_op jit(solution)/shard_map/scatter | solution.py:91
  182.3 32.0 %scatter_fusion = s32[32768]{0:T(1024)} fusion(s32[32768]{0:T(1024)} %copy.43, s32[8192]{0:T(1024)S(1)} %get-tuple-element.75, s32[8192]{0:T(1024)S(1)} %reshape.502), kind=kCustom, calls=%fused_computation.8 | custom fusion | bytes 131072 | tf_op jit(solution)/shard_map/scatter | solution.py:110
  222.4 57.0 %scatter_custom_fusion.3 = s32[32]{0:T(128)S(1)} fusion(s32[8192]{0:T(1024)S(1)} %bitcast.247, s32[8192]{0:T(1024)S(1)} %ne.86, s32[]{:T(128)} %constant.80.clone.1), kind=kCustom, calls=%fused_computation.331 | custom fusion | flops 8192 | bytes 132 | tf_op jit(solution)/shard_map/scatter-add | solution.py:88
  287.9 45.5 %gather_fusion.3 = s32[8192]{0:T(1024)S(1)} fusion(s32[8192]{0:T(1024)S(1)} %add_select_fusion.1, s32[8192]{0:T(1024)S(1)} %get-tuple-element.72), kind=kCustom, calls=%fused_computation.3 | custom fusion | bytes 98304 | tf_op jit(solution)/shard_map/gather | solution.py:87
  390.9 32.0 %scatter_fusion.1 = s32[32768]{0:T(1024)} fusion(s32[32768]{0:T(1024)} %fusion.199, s32[8192]{0:T(1024)S(1)} %get-tuple-element.71, s32[8192]{0:T(1024)S(1)} %reshape.526), kind=kCustom, calls=%fused_computation.11 | custom fusion | bytes 131072 | tf_op jit(solution)/shard_map/scatter | solution.py:110
  429.6 122.6 %gather_fusion.1 = bf16[32768,256]{1,0:T(8,128)(2,1)} fusion(bf16[4096,256]{1,0:T(8,128)(2,1)} %get-tuple-element.67, s32[32768]{0:T(1024)S(1)} %broadcast_clamp_fusion.1), kind=kCustom, calls=%fused_computation.1 | custom fusion | bytes 33685504 | tf_op jit(solution)/shard_map/gather | solution.py:113
  558.9 128.7 %gather_fusion.4 = bf16[32768,256]{1,0:T(8,128)(2,1)} fusion(bf16[4096,256]{1,0:T(8,128)(2,1)S(1)} %get-tuple-element.66, s32[32768]{0:T(1024)S(1)} %broadcast_clamp_fusion), kind=kCustom, calls=%fused_computation.4 | custom fusion | bytes 33685504 | tf_op jit(solution)/shard_map/gather | solution.py:113
  687.6 230.2 %all-to-all-done.1 = bf16[32,1024,256]{2,1,0:T(8,128)(2,1)} async-done(((bf16[32,1024,256]{2,1,0:T(8,128)(2,1)}), bf16[32,1024,256]{2,1,0:T(8,128)(2,1)}, u32[]{:S(2)}, u32[]{:S(2)}) %all-to-all-start.1) | async-done | bytes 16777248 | tf_op jit(solution)/shard_map/all_to_all | solution.py:114
  944.1 32.7 %fusion.157.clone.5 = bf16[2048,4096]{1,0:T(8,128)(2,1)} fusion(bf16[4,1024,4096]{2,1,0:T(8,128)(2,1)} %param.11, bf16[2048,1024]{0,1:T(8,128)(2,1)} %copy.28, f32[2048]{0:T(1024)S(1)} %add_rsqrt_fusion.3), kind=kOutput, calls=%fused_computation.47.clone.clone.clone.clone.clone.clone.2 | convolution fusion | flops 17278435328 | bytes 29368320 | tf_op jit(solution)/shard_map/dot_general | solution.py:41
  1011.9 32.7 %fusion.161.clone.5 = bf16[2048,4096]{1,0:T(8,128)(2,1)} fusion(bf16[4,1024,4096]{2,1,0:T(8,128)(2,1)} %param.11, bf16[2048,1024]{0,1:T(8,128)(2,1)} %get-tuple-element.147, f32[2048]{0:T(1024)S(1)} %add_rsqrt_fusion.2), kind=kOutput, calls=%fused_computation.53.clone.clone.clone.clone.clone.clone.2 | convolution fusion | flops 17278435328 | bytes 29368320 | tf_op jit(solution)/shard_map/dot_general | solution.py:41
  1044.6 39.1 %gather_fusion.2 = bf16[8192,256]{1,0:T(8,128)(2,1)} fusion(bf16[32768,256]{1,0:T(8,128)(2,1)} %bitcast.46, s32[8192]{0:T(1024)S(1)} %copy-done.6), kind=kCustom, calls=%fused_computation.2 | custom fusion | bytes 8421376 | tf_op jit(solution)/shard_map/gather | solution.py:116
  1206.5 47.7 %scatter_custom_fusion.8 = f32[32768,256]{1,0:T(8,128)} fusion(s32[8192]{0:T(1024)} %copy-done.5, f32[8192,256]{1,0:T(8,128)} %reshape.550, f32[]{:T(128)} %constant.71.clone.1), kind=kCustom, calls=%fused_computation.66 | custom fusion | bytes 33554944 | tf_op jit(solution)/shard_map/scatter | solution.py:120
  1254.3 40.0 %all-to-all-done.3 = bf16[32,1024,256]{2,1,0:T(8,128)(2,1)} async-done(((bf16[32,1024,256]{2,1,0:T(8,128)(2,1)}), bf16[32,1024,256]{2,1,0:T(8,128)(2,1)}, u32[]{:S(2)}, u32[]{:S(2)}) %all-to-all-start.3) | async-done | bytes 16777248 | tf_op jit(solution)/shard_map/all_to_all | solution.py:114
  1318.1 38.8 %gather_fusion.5 = bf16[8192,256]{1,0:T(8,128)(2,1)} fusion(bf16[32768,256]{1,0:T(8,128)(2,1)} %bitcast.94, s32[8192]{0:T(1024)S(1)} %copy-done.7), kind=kCustom, calls=%fused_computation.5 | custom fusion | bytes 8421376 | tf_op jit(solution)/shard_map/gather | solution.py:116
  1389.8 44.4 %fusion.301 = bf16[2048,4096]{1,0:T(8,128)(2,1)} fusion(bf16[2048,4096]{1,0:T(8,128)(2,1)} %convolution_convert_fusion, bf16[2048,1024]{1,0:T(8,128)(2,1)} %param.9, bf16[4,4096,1024]{2,1,0:T(8,128)(2,1)} %param.12), kind=kOutput, calls=%fused_computation.38.clone.clone.2 | convolution fusion | flops 17356029952 | bytes 46137344 | tf_op jit(solution)/shard_map/td,fd->tf/dot_general | solution.py:74
  1475.3 47.2 %fusion.45.clone.5 = bf16[2048,4096]{1,0:T(8,128)(2,1)} fusion(bf16[2048,4096]{1,0:T(8,128)(2,1)} %convolution_convert_fusion.1, bf16[4,4096,1024]{2,1,0:T(8,128)(2,1)} %param.12, bf16[2048,1024]{0,1:T(8,128)(2,1)} %get-tuple-element.151, f32[2048,1024]{0,1:T(8,128)} %get-tuple-element.155, bf16[2048,1024]{0,1:T(8,128)(2,1)} %copy.39, ...), kind=kOutput, calls=%fused_computation.41.clone.clone.clone.clone.2 | convolution fusion | flops 17372807168 | bytes 58744832 | tf_op jit(solution)/shard_map/td,fd->tf/dot_general | solution.py:74
  1575.5 47.7 %scatter_custom_fusion.6 = f32[32768,256]{1,0:T(8,128)} fusion(s32[8192]{0:T(1024)} %copy-done.4, f32[8192,256]{1,0:T(8,128)} %reshape.534, f32[]{:T(128)} %constant.71.clone.1), kind=kCustom, calls=%fused_computation.68 | custom fusion | bytes 33554944 | tf_op jit(solution)/shard_map/scatter | solution.py:120
  1623.3 408.0 %all-to-all-done.5 = f32[32,1024,256]{2,1,0:T(8,128)} async-done(((f32[32,1024,256]{2,1,0:T(8,128)}), f32[32,1024,256]{2,1,0:T(8,128)}, u32[]{:S(2)}, u32[]{:S(2)}) %all-to-all-start.5) | async-done | bytes 33554464 | tf_op jit(solution)/shard_map/all_to_all | solution.py:121
  2031.3 34.1 %all-to-all-start.4 = ((f32[32,1024,256]{2,1,0:T(8,128)}), f32[32,1024,256]{2,1,0:T(8,128)}, u32[]{:S(2)}, u32[]{:S(2)}) async-start(f32[32,1024,256]{2,1,0:T(8,128)} %bitcast.229), calls=%async_computation.4 | async-start | bytes 67108864 | tf_op jit(solution)/shard_map/all_to_all | solution.py:121
  2108.3 216.7 %scatter_custom_fusion.9 = f32[4096,256]{1,0:T(8,128)} fusion(s32[32768]{0:T(1024)} %bitcast.238, f32[32768,256]{1,0:T(8,128)} %bitcast.102, f32[]{:T(128)} %constant.71.clone.1), kind=kCustom, calls=%fused_computation.196 | custom fusion | flops 8388608 | bytes 4194816 | tf_op jit(solution)/shard_map/scatter-add | solution.py:122
  2325.0 460.0 %all-to-all-done.4 = f32[32,1024,256]{2,1,0:T(8,128)} async-done(((f32[32,1024,256]{2,1,0:T(8,128)}), f32[32,1024,256]{2,1,0:T(8,128)}, u32[]{:S(2)}, u32[]{:S(2)}) %all-to-all-start.4) | async-done | bytes 33554464 | tf_op jit(solution)/shard_map/all_to_all | solution.py:121
  2784.9 216.9 %scatter_custom_fusion.7 = f32[4096,256]{1,0:T(8,128)} fusion(s32[32768]{0:T(1024)} %bitcast.236, f32[32768,256]{1,0:T(8,128)} %bitcast.98, f32[]{:T(128)} %constant.71.clone.1), kind=kCustom, calls=%fused_computation.198 | custom fusion | flops 8388608 | bytes 4194816 | tf_op jit(solution)/shard_map/scatter-add | solution.py:122
  (121 shorter events, 509.3 us)
Async XLA Ops:
  182.3 32.0 %copy-start.4 = (s32[8192]{0:T(1024)}, s32[8192]{0:T(1024)S(1)}, u32[]{:S(2)}) copy-start(s32[8192]{0:T(1024)S(1)} %get-tuple-element.75) | copy-start | bytes 98308
  214.3 208.6 %all-to-all-start = ((s32[32,1024,1]{1,2,0:T(1,128)}), s32[32,1024,1]{1,2,0:T(1,128)S(1)}, u32[]{:S(2)}, u32[]{:S(2)}) async-start(s32[32,1024,1]{1,2,0:T(1,128)} %bitcast.42), calls=%async_computation | async-start | bytes 262144 | tf_op jit(solution)/shard_map/all_to_all | solution.py:111
  390.9 32.0 %copy-start.5 = (s32[8192]{0:T(1024)}, s32[8192]{0:T(1024)S(1)}, u32[]{:S(2)}) copy-start(s32[8192]{0:T(1024)S(1)} %get-tuple-element.71) | copy-start | bytes 98308
  422.9 129.3 %all-to-all-start.2 = ((s32[32,1024,1]{1,2,0:T(1,128)}), s32[32,1024,1]{1,2,0:T(1,128)S(1)}, u32[]{:S(2)}, u32[]{:S(2)}) async-start(s32[32,1024,1]{1,2,0:T(1,128)} %bitcast.90), calls=%async_computation.2 | async-start | bytes 262144 | tf_op jit(solution)/shard_map/all_to_all | solution.py:111
  428.8 0.6 copy-start.2
  552.2 365.6 %all-to-all-start.1 = ((bf16[32,1024,256]{2,1,0:T(8,128)(2,1)}), bf16[32,1024,256]{2,1,0:T(8,128)(2,1)}, u32[]{:S(2)}, u32[]{:S(2)}) async-start(bf16[32,1024,256]{2,1,0:T(8,128)(2,1)} %bitcast.231), calls=%async_computation.1 | async-start | bytes 33554432 | tf_op jit(solution)/shard_map/all_to_all | solution.py:114
  558.1 0.7 copy-start.3
  917.8 376.5 %all-to-all-start.3 = ((bf16[32,1024,256]{2,1,0:T(8,128)(2,1)}), bf16[32,1024,256]{2,1,0:T(8,128)(2,1)}, u32[]{:S(2)}, u32[]{:S(2)}) async-start(bf16[32,1024,256]{2,1,0:T(8,128)(2,1)} %bitcast.230), calls=%async_computation.3 | async-start | bytes 33554432 | tf_op jit(solution)/shard_map/all_to_all | solution.py:114
  976.8 24.7 copy-start.12
  1011.9 32.7 %copy-start.6 = (s32[8192]{0:T(1024)S(1)}, s32[8192]{0:T(1024)}, u32[]{:S(2)}) copy-start(s32[8192]{0:T(1024)} %get-tuple-element.74) | copy-start | bytes 98308
  1127.3 24.8 copy-start.9
  1152.1 26.6 copy-start.13
  1178.7 7.2 copy-start
  1178.7 7.2 copy-start.15
  1185.9 10.5 copy-start.17
  1294.3 737.0 %all-to-all-start.5 = ((f32[32,1024,256]{2,1,0:T(8,128)}), f32[32,1024,256]{2,1,0:T(8,128)}, u32[]{:S(2)}, u32[]{:S(2)}) async-start(f32[32,1024,256]{2,1,0:T(8,128)} %bitcast.228), calls=%async_computation.5 | async-start | bytes 67108864 | tf_op jit(solution)/shard_map/all_to_all | solution.py:121
  1311.6 6.5 copy-start.7
  1434.2 24.5 copy-start.14
  1458.7 16.6 copy-start.11
  1522.5 24.8 copy-start.1
  1522.5 24.8 copy-start.8
  1522.5 24.8 copy-start.10
  2031.3 753.7 %all-to-all-start.4 = ((f32[32,1024,256]{2,1,0:T(8,128)}), f32[32,1024,256]{2,1,0:T(8,128)}, u32[]{:S(2)}, u32[]{:S(2)}) async-start(f32[32,1024,256]{2,1,0:T(8,128)} %bitcast.229), calls=%async_computation.4 | async-start | bytes 67108864 | tf_op jit(solution)/shard_map/all_to_all | solution.py:121
  2065.4 25.0 copy-start.16
where the time goes:
time: 3050 us; the launch traced here: 3010 us
  waiting for transfers between devices  1140 us (37%)
  local copies, waits for them, and re-layouts  722 us (24%)
  other arithmetic  621 us (20%)
  matrix products  441 us (14%)
  starting transfers between devices  86.1 us (3%)
    all_to_all x2, waiting for transfers between devices, return_rows(): recv_grad = lax.all_to_all(send_grad, 'emb', 0, 0, tiled=True)  868 us
    scatter-add x2, other arithmetic, return_rows(): return jax.ops.segment_sum(recv_grad, local_ids, num_segments=rows_dev)  434 us
    all_to_all x2, waiting for transfers between devices, fetch_rows(): back_rows = lax.all_to_all(served, 'emb', 0, 0, tiled=True)  270 us
    gather x2, local copies, waits for them, and re-layouts, fetch_rows(): served = tables[which][local_ids]  251 us
    dot_general x4, matrix products, stack_forward(): jnp.dot(normed, w_up[layer_idx], preferred_element_type=jnp.float32)  115 us
    scatter-add x2, other arithmetic, route_plan(): jax.ops.segment_sum(jnp.ones_like(owner_ids), owner_ids, num_segments=n_dev)  114 us
    dot_general x4, matrix products, stack_forward(): jnp.dot(activated, w_down[layer_idx], preferred_element_type=jnp.float32)  101 us
    scatter x2, local copies, waits for them, and re-layouts, return_rows(): jnp.zeros((n_dev * capacity, row_width), jnp.float32).at[dest_slot]  95.5 us
  transfers between devices with their start and end apart: 6, of which 4 were waited for; matrix products, arithmetic and copies ran while one was open for 45% of the time, Pallas kernels for 0%

commit v1 on v0

v1 whole, which is shorter than its diff:
```python
import jax
import jax.numpy as jnp
from jax import lax
from jax.experimental import pallas as pl
from jax.experimental.pallas import tpu as pltpu
from jax.sharding import PartitionSpec as P


EPS = 1e-6
C1 = 0.7978845608028654
C2 = C1 * 0.044715
BF16 = jnp.bfloat16
F32 = jnp.float32
VMEM_LIMIT = 62 * 1024 * 1024
MESH = pl.DeviceIdType.MESH
PLANE = 8
SLOTS = 336
IDW = 1024
UNROLL = 16

SMEM_SPEC = pl.BlockSpec(memory_space=pltpu.SMEM)
VMEM_SPEC = pl.BlockSpec(memory_space=pltpu.VMEM)
ANY_SPEC = pl.BlockSpec(memory_space=pl.ANY)


def local_params():
    return pltpu.CompilerParams(vmem_limit_bytes=VMEM_LIMIT)


def remote_params(cid):
    return pltpu.CompilerParams(vmem_limit_bytes=VMEM_LIMIT, collective_id=cid, has_side_effects=True)


def cost(us, nbytes):
    return pl.CostEstimate(flops=int(us * 9 * 10**8), bytes_accessed=nbytes, transcendentals=0)


def shape_of(shape, dtype):
    return jax.ShapeDtypeStruct(shape, dtype)


def gelu(x):
    half = 0.5 * x
    return half + half * jnp.tanh(x * (C1 + C2 * (x * x)))


def gelu_bwd(x, ct):
    x2 = x * x
    t = jnp.tanh(x * (C1 + C2 * x2))
    return ct * ((0.5 + 0.5 * t) + (x * (0.5 - (0.5 * t) * t)) * (C1 + (3 * C2) * x2))


def dot_nn(a, b):
    return jnp.dot(a, b, preferred_element_type=F32)


def dot_nt(a, b):
    return lax.dot_general(a, b, (((1,), (1,)), ((), ())), preferred_element_type=F32)


def rms(x_f):
    return lax.rsqrt(jnp.mean(x_f * x_f, axis=-1, keepdims=True) + EPS)


def token_kernel(body, tile, tokens, ins, weights, outs, scratch, us):
    n_in, n_w, n_out = len(ins), len(weights), len(outs)

    def kernel(*refs):
        in_refs = refs[:n_in]
        w_hbm = refs[n_in:n_in + n_w]
        out_refs = refs[n_in + n_w:n_in + n_w + n_out]
        w_vmem = refs[n_in + n_w + n_out:n_in + 2 * n_w + n_out]
        sem = refs[n_in + 2 * n_w + n_out]
        rest = refs[n_in + 2 * n_w + n_out + 1:]
        copies = [pltpu.make_async_copy(w_hbm[i].at[weights[i][1]], w_vmem[i], sem.at[i]) for i in range(n_w)]
        opening = pl.program_id(0) == 0

        @pl.when(opening)
        def _():
            for c in copies:
                c.start()

        def need(*which):
            @pl.when(opening)
            def _():
                for i in which:
                    copies[i].wait()

        body(need, in_refs, w_vmem, out_refs, rest)

    def tiled(shape, per):
        return pl.BlockSpec((tile * per,) + shape[1:], lambda i: (i,) + (0,) * (len(shape) - 1))

    in_specs = [tiled(a.shape, per) for a, per in ins] + [ANY_SPEC] * n_w
    out_specs = [tiled(s.shape, per) for s, per in outs]
    w_scratch = [pltpu.VMEM(w.shape[1:], w.dtype) for w, _ in weights]
    return pl.pallas_call(
        kernel, grid=(tokens // tile,), out_shape=[s for s, _ in outs], in_specs=in_specs, out_specs=out_specs,
        scratch_shapes=w_scratch + [pltpu.SemaphoreType.DMA((n_w,))] + scratch,
        compiler_params=local_params(), cost_estimate=cost(us, 2**25),
    )(*[a for a, _ in ins], *[w for w, _ in weights])


def mlp_up(u, w_up, act, h_ref, chunk=512):
    for j in range(w_up.shape[1] // chunk):
        cols = slice(j * chunk, (j + 1) * chunk)
        h = dot_nn(u, w_up[:, cols]).astype(BF16)
        if h_ref is not None:
            h_ref[:, cols] = h
        if act is not None:
            act[:, cols] = gelu(h.astype(F32)).astype(BF16)


def store_rows(ref, value):
    tokens, width = value.shape
    n = width // 128
    for c in range(n):
        ref[pl.ds(c, tokens, stride=n), :] = value[:, c * 128:(c + 1) * 128]


def layer_plain(x, w_up, w_down, layer, tile=512):
    tokens, d = x.shape

    def body(need, ins, w, outs, rest):
        need(0, 1)
        x_f = ins[0][...].astype(F32)
        u = (x_f * rms(x_f)).astype(BF16)
        mlp_up(u, w[0], rest[0], None)
        for q in range(d // 256):
            cols = slice(q * 256, (q + 1) * 256)
            m = dot_nn(rest[0][...], w[1][:, cols]).astype(BF16)
            outs[0][:, cols] = (ins[0][:, cols].astype(F32) + m.astype(F32)).astype(BF16)

    return token_kernel(body, tile, tokens, [(x, 1)], [(w_up, layer), (w_down, layer)],
                        [(shape_of(x.shape, BF16), 1)], [pltpu.VMEM((tile, w_up.shape[2]), BF16)], 44)[0]


def layer_table_head(x, w_up, w_down, w_gate, layer, which, tile=512):
    tokens, d = x.shape

    def body(need, ins, w, outs, rest):
        need(0, 1, 2)
        x_f = ins[0][...].astype(F32)
        u = (x_f * rms(x_f)).astype(BF16)
        mlp_up(u, w[0], rest[0], None)
        a = dot_nn(u, w[2][...]).astype(BF16)
        outs[1][...] = gelu(a.astype(F32)).astype(BF16)
        for q in range(d // 256):
            cols = slice(q * 256, (q + 1) * 256)
            outs[0][:, cols] = dot_nn(rest[0][...], w[1][:, cols]).astype(BF16)

    return token_kernel(body, tile, tokens, [(x, 1)],
                        [(w_up, layer), (w_down, layer), (w_gate, which)],
                        [(shape_of(x.shape, BF16), 1), (shape_of(x.shape, BF16), 1)],
                        [pltpu.VMEM((tile, w_up.shape[2]), BF16)], 50)


def layer_middle(x, m, g, e, d_out, w_up, w_down, w_gate, w_proj, layer, tile=256):
    tokens, d = x.shape
    ff = w_up.shape[2]

    def body(need, ins, w, outs, rest):
        x_ref, m_ref, g_ref, e_ref, c_ref = ins
        x2_ref, h_ref, x3_ref, a_ref, dz_ref, row_ref = outs
        act = rest[0]
        need(4, 0)
        z = (g_ref[...].astype(F32) * e_ref[...].astype(F32)).astype(BF16)
        q = dot_nn(z, w[4][...]).astype(BF16)
        x2 = ((x_ref[...].astype(F32) + m_ref[...].astype(F32)) + q.astype(F32)).astype(BF16)
        x2_ref[...] = x2
        x_f = x2.astype(F32)
        u = (x_f * rms(x_f)).astype(BF16)
        need(1)
        mlp_up(u, w[0], act, h_ref)
        for n in range(d // 256):
            cols = slice(n * 256, (n + 1) * 256)
            mm = dot_nn(act[...], w[1][:, cols]).astype(BF16)
            x3_ref[:, cols] = (x2_ref[:, cols].astype(F32) + mm.astype(F32)).astype(BF16)
        x_f = x3_ref[...].astype(F32)
        u = (x_f * rms(x_f)).astype(BF16)
        need(2, 3)
        a = dot_nn(u, w[2][...]).astype(BF16)
        a_ref[...] = a
        gate = gelu(a.astype(F32)).astype(BF16)
        dz = dot_nt(c_ref[...], w[3][...])
        dz_ref[...] = dz
        store_rows(row_ref, gate.astype(F32) * dz)

    vec = (shape_of((tokens, d), BF16), 1)
    return token_kernel(body, tile, tokens, [(x, 1), (m, 1), (g, 1), (e, 1), (d_out, 1)],
                        [(w_up, layer), (w_down, layer), (w_gate, 1), (w_proj, 1), (w_proj, 0)],
                        [vec, (shape_of((tokens, ff), BF16), 1), vec, vec, (shape_of((tokens, d), F32), 1),
                         (shape_of((tokens * d // 128, 128), F32), d // 128)],
                        [pltpu.VMEM((tile, ff), BF16)], 62)


def last_up(x, w_up, layer, tile=512):
    tokens, ff = x.shape[0], w_up.shape[2]

    def body(need, ins, w, outs, rest):
        need(0)
        x_f = ins[0][...].astype(F32)
        u = (x_f * rms(x_f)).astype(BF16)
        mlp_up(u, w[0], None, outs[0])

    return token_kernel(body, tile, tokens, [(x, 1)], [(w_up, layer)],
                        [(shape_of((tokens, ff), BF16), 1)], [], 22)[0]


def last_down(x, h, a, e, w_down, w_proj, layer, which, tile=256):
    tokens, d = x.shape
    ff = h.shape[1]

    def body(need, ins, w, outs, rest):
        x_ref, h_ref, a_ref, e_ref = ins
        act = rest[0]
        need(0, 1)
        gate = gelu(a_ref[...].astype(F32)).astype(BF16)
        z = (gate.astype(F32) * e_ref[...].astype(F32)).astype(BF16)
        for j in range(ff // 512):
            cols = slice(j * 512, (j + 1) * 512)
            act[:, cols] = gelu(h_ref[:, cols].astype(F32)).astype(BF16)
        for n in range(d // 256):
            cols = slice(n * 256, (n + 1) * 256)
            m = dot_nn(act[...], w[0][:, cols]).astype(BF16)
            q = dot_nn(z, w[1][:, cols]).astype(BF16)
            outs[0][:, cols] = ((x_ref[:, cols].astype(F32) + m.astype(F32)) + q.astype(F32)).astype(BF16)

    return token_kernel(body, tile, tokens, [(x, 1), (h, 1), (a, 1), (e, 1)],
                        [(w_down, layer), (w_proj, which)], [(shape_of(x.shape, BF16), 1)],
                        [pltpu.VMEM((tile, ff), BF16)], 30)[0]


def back_mlp(c_b, h_ref, w_up, w_down, dh):
    chunk = 512
    for j in range(h_ref.shape[1] // chunk):
        cols = slice(j * chunk, (j + 1) * chunk)
        d_act = dot_nt(c_b, w_down[cols, :])
        dh[:, cols] = gelu_bwd(h_ref[:, cols].astype(F32), d_act).astype(BF16)
    return jnp.concatenate([dot_nt(dh[...], w_up[n * 256:(n + 1) * 256, :]) for n in range(w_up.shape[0] // 256)], axis=1)


def back_norm(c_f, x_ref, du):
    x_f = x_ref[...].astype(F32)
    s = rms(x_f)
    return c_f + (s * du - x_f * (s * s * s) * jnp.mean(x_f * du, axis=-1, keepdims=True))


def back_table(c, h, x, a, dz, e, w_up, w_down, w_gate, layer, which, tile=256):
    tokens, d = x.shape
    ff = h.shape[1]

    def body(need, ins, w, outs, rest):
        c_ref, h_ref, x_ref, a_ref, dz_ref, e_ref = ins
        need(0, 1, 2)
        d_gate = gelu_bwd(a_ref[...].astype(F32), dz_ref[...] * e_ref[...].astype(F32)).astype(BF16)
        rest[1][...] = dot_nt(d_gate, w[2][...])
        du = back_mlp(c_ref[...], h_ref, w[0], w[1], rest[0]) + rest[1][...]
        outs[0][...] = back_norm(c_ref[...].astype(F32), x_ref, du)

    return token_kernel(body, tile, tokens,
                        [(c, 1), (h, 1), (x, 1), (a, 1), (dz, 1), (e, 1)],
                        [(w_up, layer), (w_down, layer), (w_gate, which)],
                        [(shape_of((tokens, d), F32), 1)],
                        [pltpu.VMEM((tile, ff), BF16), pltpu.VMEM((tile, d), F32)], 58)[0]


def back_plain(c, h, x, g, w_up, w_down, w_proj, layer, which, tile=256):
    tokens, d = x.shape
    ff = h.shape[1]

    def body(need, ins, w, outs, rest):
        c_ref, h_ref, x_ref, g_ref = ins
        need(0, 1, 2)
        du = back_mlp(c_ref[...].astype(BF16), h_ref, w[0], w[1], rest[0])
        c_low = back_norm(c_ref[...], x_ref, du).astype(BF16)
        store_rows(outs[0], g_ref[...].astype(F32) * dot_nt(c_low, w[2][...]))

    return token_kernel(body, tile, tokens, [(c, 1), (h, 1), (x, 1), (g, 1)],
                        [(w_up, layer), (w_down, layer), (w_proj, which)],
                        [(shape_of((tokens * d // 128, 128), F32), d // 128)],
                        [pltpu.VMEM((tile, ff), BF16)], 58)[0]


def split_rows(tables, place):
    n_tab, rows, width = tables.shape
    blk = rows // PLANE

    def kernel(place_ref, src, out, buf, isem, osem):
        reads = [pltpu.make_async_copy(src.at[t], buf.at[t], isem.at[t]) for t in range(n_tab)]
        for c in reads:
            c.start()
        writes = []
        for t in range(n_tab):
            reads[t].wait()
            for b in range(PLANE):
                writes.append(pltpu.make_async_copy(buf.at[t, pl.ds(b * blk, blk)], out.at[place_ref[0] ^ b, t], osem.at[t * PLANE + b]))
                writes[-1].start()
        for c in writes:
            c.wait()

    return pl.pallas_call(
        kernel, out_shape=shape_of((PLANE, n_tab, blk, width), tables.dtype), in_specs=[SMEM_SPEC, ANY_SPEC], out_specs=ANY_SPEC,
        scratch_shapes=[pltpu.VMEM(tables.shape, tables.dtype), pltpu.SemaphoreType.DMA((n_tab,)),
                        pltpu.SemaphoreType.DMA((n_tab * PLANE,))],
        compiler_params=local_params(), name="split_rows", cost_estimate=cost(4, 2**23))(place, tables)


def make_ids(uid, start, count, peak, rnd, blank):
    n_tgt = count.shape[0]
    rows = -(-SLOTS // 128)

    def kernel(uid_ref, start_ref, count_ref, peak_ref, rnd_ref, out_ref):
        lane = lax.broadcasted_iota(jnp.int32, (1, 128), 1)
        out_ref[...] = jnp.full(out_ref.shape, peak_ref[0], jnp.int32)
        for g in range(n_tgt):
            shift = rnd_ref[0] * SLOTS
            left = jnp.clip(count_ref[g] - shift, 0, SLOTS)
            at = jnp.minimum(start_ref[g] + shift, (uid_ref.shape[0] - rows - 1) * 128)
            row, off = at // 128, lax.rem(at, 128)
            turned = [pltpu.roll(uid_ref[row + i], lax.rem(128 - off, 128), axis=1) for i in range(rows + 1)]
            for i in range(rows):
                ids = jnp.where(lane < 128 - off, turned[i], turned[i + 1])
                out_ref[g, i:i + 1, :] = jnp.where(i * 128 + lane < left, ids, blank)

    return pl.pallas_call(
        kernel, out_shape=shape_of((n_tgt, IDW // 128, 128), jnp.int32),
        in_specs=[VMEM_SPEC] + [SMEM_SPEC] * 4, out_specs=VMEM_SPEC, compiler_params=local_params(), name="make_ids",
        cost_estimate=cost(3, 2**18),
    )(uid, start, count, peak, jnp.reshape(rnd, (1,)).astype(jnp.int32))


def pair_at(index):
    return pl.ds(pl.multiple_of(index, 2), 2)


def owner_gather(ids, served, which, n_src):
    blk, width = served.shape[2:]
    rows = PLANE * blk
    pieces = width // 128

    def kernel(ids_ref, served_ref, out_ref, native, flat, isem):
        reads = [pltpu.make_async_copy(served_ref.at[b, which], native.at[b], isem.at[b]) for b in range(PLANE)]
        for c in reads:
            c.start()
        for b in range(PLANE):
            reads[b].wait()
            for c in range(pieces):
                flat[pl.ds(b * blk * pieces + c, blk, stride=pieces), :] = native[b, :, c * 128:(c + 1) * 128].astype(F32)

        def src(s, c):
            def part(b, c):
                for j in range(UNROLL):
                    r = b * UNROLL + j
                    out_ref[s * SLOTS + r] = flat[pair_at(ids_ref[s * IDW + r]), :].astype(BF16)
                return c

            lax.fori_loop(0, SLOTS // UNROLL, part, 0)
            return c

        lax.fori_loop(0, n_src, src, 0)

    return pl.pallas_call(
        kernel, out_shape=shape_of((n_src * SLOTS, pieces, 128), BF16),
        in_specs=[SMEM_SPEC, ANY_SPEC], out_specs=VMEM_SPEC,
        scratch_shapes=[pltpu.VMEM((PLANE, blk, width), BF16), pltpu.VMEM((rows * pieces + 8, 128), F32),
                        pltpu.SemaphoreType.DMA((PLANE,))],
        compiler_params=local_params(), name="owner_gather", cost_estimate=cost(14, 2**22),
    )(ids, served)


def unpack_rows(idx, rec_own, rec_pair, heads):
    n = idx.shape[0]
    half, pieces = rec_own.shape[0], rec_own.shape[1]
    tokens, tile = n // heads, 256
    per = heads * pieces

    def kernel(idx_ref, own_ref, pair_ref, out_ref, rec, stage, sem):
        copies = [pltpu.make_async_copy(own_ref, rec.at[pl.ds(0, half)], sem.at[0]),
                  pltpu.make_async_copy(pair_ref, rec.at[pl.ds(half, half)], sem.at[1])]
        for c in copies:
            c.start()
        for c in copies:
            c.wait()

        def part(i, c):
            def blk(b, c):
                for j in range(UNROLL):
                    row = rec[idx_ref[i * (tile * heads) + b * UNROLL + j]]
                    stage[pl.ds(pl.multiple_of(b * UNROLL * pieces, UNROLL * pieces) + pieces * j, pieces), :] = row.astype(F32)
                return c

            lax.fori_loop(0, tile * heads // UNROLL, blk, 0)
            for c in range(per):
                out_ref[pl.ds(i * tile, tile), c * 128:(c + 1) * 128] = stage[pl.ds(c, tile, stride=per), :].astype(BF16)
            return c

        lax.fori_loop(0, tokens // tile, part, 0)

    return pl.pallas_call(
        kernel, out_shape=shape_of((tokens, per * 128), BF16),
        in_specs=[SMEM_SPEC, ANY_SPEC, ANY_SPEC], out_specs=VMEM_SPEC,
        scratch_shapes=[pltpu.VMEM((2 * half, pieces, 128), BF16), pltpu.VMEM((tile * per, 128), F32), pltpu.SemaphoreType.DMA((2,))],
        compiler_params=local_params(), name="unpack_rows", cost_estimate=cost(16, 2**23),
    )(idx, rec_own, rec_pair)


def pack_rows(pos, dst, size, grad_own, grad_pair, n_tgt):
    n = grad_own.shape[0]
    n_row = 2 * n_tgt * SLOTS
    low = jnp.iinfo(jnp.int32).max

    def kernel(pos_ref, dst_ref, size_ref, own_ref, pair_ref, out_ref, g_ref, stage, sem):
        first = pltpu.make_async_copy(own_ref, g_ref.at[pl.ds(0, n)], sem.at[0])
        second = pltpu.make_async_copy(pair_ref, g_ref.at[pl.ds(n, n)], sem.at[1])
        first.start()
        second.start()
        first.wait()
        second.wait()

        def blk(b, acc):
            for j in range(UNROLL):
                p = pos_ref[b * UNROLL + j]
                row = g_ref[pair_at(p & low), :]
                acc = row + jnp.where(jnp.full((2, 128), p, jnp.int32) < 0, acc, 0.0)
                stage[pair_at(dst_ref[b * UNROLL + j]), :] = acc
            return acc

        lax.fori_loop(0, (size_ref[0] + UNROLL - 1) // UNROLL, blk, jnp.zeros((2, 128), F32))
        done = pltpu.make_async_copy(stage.at[pl.ds(0, n_row)], out_ref, sem.at[0])
        done.start()
        done.wait()

    return pl.pallas_call(
        kernel, out_shape=shape_of((n_row, 128), F32),
        in_specs=[SMEM_SPEC, SMEM_SPEC, SMEM_SPEC, ANY_SPEC, ANY_SPEC], out_specs=ANY_SPEC,
        scratch_shapes=[pltpu.VMEM((2 * n, 128), F32), pltpu.VMEM((n_row + 8, 128), F32), pltpu.SemaphoreType.DMA((2,))],
        compiler_params=local_params(), name="pack_rows", cost_estimate=cost(26, 2**24),
    )(pos, dst, size, grad_own, grad_pair)


def owner_scatter(ids, rec, rows, place):
    n_src = rec.shape[0] // (2 * SLOTS)
    per = UNROLL

    blk_rows = 2 * rows // PLANE

    def kernel(ids_ref, place_ref, rec_ref, *refs):
        outs, (acc, buf, sem, osem) = refs[:PLANE], refs[PLANE:]
        reads = [pltpu.make_async_copy(rec_ref.at[pl.ds(s * 2 * SLOTS, 2 * SLOTS)], buf.at[pl.ds(s * 2 * SLOTS, 2 * SLOTS)], sem.at[s])
                 for s in range(n_src)]
        for c in reads:
            c.start()

        def zero(i, c):
            acc[pl.ds(i * 128, 128), :] = jnp.zeros((128, 128), F32)
            return c

        lax.fori_loop(0, 2 * rows // 128, zero, 0)
        for c in reads:
            c.wait()

        def src(s, c):
            def blk(b, c):
                at = [pair_at(ids_ref[s * IDW + b * per + j]) for j in range(per)]
                base = pl.multiple_of((s * SLOTS + b * per) * 2, 2 * per)
                new = [acc[i, :] + buf[pl.ds(base + 2 * j, 2), :] for j, i in enumerate(at)]
                for i, v in zip(at, new):
                    acc[i, :] = v
                return c

            lax.fori_loop(0, SLOTS // per, blk, 0)
            return c

        lax.fori_loop(0, n_src, src, 0)
        writes = []
        for b in range(PLANE):
            at = pl.multiple_of((place_ref[0] ^ b) * blk_rows, blk_rows)
            writes.append(pltpu.make_async_copy(acc.at[pl.ds(at, blk_rows)], outs[b], osem.at[b]))
            writes[-1].start()
        for c in writes:
            c.wait()

    return pl.pallas_call(
        kernel, out_shape=[shape_of((blk_rows, 128), F32)] * PLANE, in_specs=[SMEM_SPEC, SMEM_SPEC, ANY_SPEC],
        out_specs=[ANY_SPEC] * PLANE,
        scratch_shapes=[pltpu.VMEM((2 * rows + 8, 128), F32), pltpu.VMEM((n_src * 2 * SLOTS, 128), F32),
                        pltpu.SemaphoreType.DMA((n_src,)), pltpu.SemaphoreType.DMA((PLANE,))],
        compiler_params=local_params(), name="owner_scatter", cost_estimate=cost(20, 2**24),
    )(ids, place, rec)


def finish_table(blocks, grads, which, n_tab):
    blk_rows = blocks[0].shape[0]
    blk = blk_rows // 2
    shape = (n_tab, PLANE * blk, 256)
    first = grads is None

    def kernel(*refs):
        out, buf, stage, isem, osem = refs[-5:]
        reads = [pltpu.make_async_copy(refs[b], buf.at[b], isem.at[b]) for b in range(PLANE)]
        for c in reads:
            c.start()
        writes = []
        for b in range(PLANE):
            reads[b].wait()
            for c in range(2):
                stage[b, :, c * 128:(c + 1) * 128] = buf[b, pl.ds(c, blk, stride=2), :]
            writes.append(pltpu.make_async_copy(stage.at[b], out.at[which, pl.ds(b * blk, blk)], osem.at[b]))
            writes[-1].start()
        for c in writes:
            c.wait()

    args = list(blocks) + ([] if first else [grads])
    return pl.pallas_call(
        kernel, out_shape=shape_of(shape, F32), in_specs=[ANY_SPEC] * len(args), out_specs=ANY_SPEC,
        scratch_shapes=[pltpu.VMEM((PLANE, blk_rows, 128), F32), pltpu.VMEM((PLANE, blk, 256), F32),
                        pltpu.SemaphoreType.DMA((PLANE,)), pltpu.SemaphoreType.DMA((PLANE,))],
        input_output_aliases={} if first else {PLANE: 0},
        compiler_params=local_params(), name="finish_table", cost_estimate=cost(8, 2**23))(*args)


def swap_cores(x, n_dev):
    return lax.ppermute(x, 'emb', [(i, i ^ 1) for i in range(n_dev)])


def chip_trade(x, n_dev):
    groups = [list(range(c, n_dev, 2)) for c in range(2)]
    return lax.all_to_all(x, 'emb', 0, 0, axis_index_groups=groups, tiled=True)


def chip_exchange(blocks, cid, n_chip):
    def kernel(x_ref, o_ref, ssem, rsem, lsem):
        me = lax.axis_index('emb')
        chip = me // 2
        barrier = pltpu.get_barrier_semaphore()
        for d in range(1, n_chip):
            pl.semaphore_signal(barrier, inc=1, device_id=(me ^ (2 * d),), device_id_type=MESH)
        pl.semaphore_wait(barrier, n_chip - 1)
        copies = [pltpu.make_async_copy(x_ref.at[chip], o_ref.at[chip], lsem)]
        for d in range(1, n_chip):
            copies.append(pltpu.make_async_remote_copy(
                src_ref=x_ref.at[chip ^ d], dst_ref=o_ref.at[chip], send_sem=ssem.at[d], recv_sem=rsem.at[d],
                device_id=(me ^ (2 * d),), device_id_type=MESH))
        for c in copies:
            c.start()
        for c in copies:
            c.wait()

    return pl.pallas_call(
        kernel, out_shape=shape_of(blocks.shape, blocks.dtype), in_specs=[ANY_SPEC], out_specs=ANY_SPEC,
        scratch_shapes=[pltpu.SemaphoreType.DMA((n_chip,)), pltpu.SemaphoreType.DMA((n_chip,)), pltpu.SemaphoreType.DMA],
        compiler_params=remote_params(cid), name="chip_exchange", cost_estimate=cost(100, 2**23))(blocks)


def plane_trade(x, n_dev):
    groups = [list(range(z, z + PLANE)) for z in range(0, n_dev, PLANE)]
    return lax.all_to_all(x, 'emb', 0, 0, axis_index_groups=groups, tiled=True)


def place_trade(blocks, n_dev):
    return [blocks[0]] + [lax.ppermute(blocks[b], 'emb', [(i, i ^ b) for i in range(n_dev)]) for b in range(1, PLANE)]


def place_exchange(blocks, cid):
    def kernel(*refs):
        srcs, outs, (ssem, rsem) = refs[:PLANE - 1], refs[PLANE - 1:2 * (PLANE - 1)], refs[-2:]
        me = lax.axis_index('emb')
        barrier = pltpu.get_barrier_semaphore()
        for b in range(1, PLANE):
            pl.semaphore_signal(barrier, inc=1, device_id=(me ^ b,), device_id_type=MESH)
        pl.semaphore_wait(barrier, PLANE - 1)
        copies = [pltpu.make_async_remote_copy(
            src_ref=srcs[b - 1], dst_ref=outs[b - 1], send_sem=ssem.at[b], recv_sem=rsem.at[b],
            device_id=(me ^ b,), device_id_type=MESH) for b in range(1, PLANE)]
        for c in copies:
            c.start()
        for c in copies:
            c.wait()

    shape = shape_of(blocks[0].shape, blocks[0].dtype)
    got = pl.pallas_call(
        kernel, out_shape=[shape] * (PLANE - 1), in_specs=[ANY_SPEC] * (PLANE - 1), out_specs=[ANY_SPEC] * (PLANE - 1),
        scratch_shapes=[pltpu.SemaphoreType.DMA((PLANE,)), pltpu.SemaphoreType.DMA((PLANE,))],
        compiler_params=remote_params(cid), name="place_exchange", cost_estimate=cost(50, 2**22))(*blocks[1:])
    return [blocks[0]] + list(got)


def after(x, *deps):
    return lax.optimization_barrier((x,) + deps)[0]


def route_plan(ids_pair, n_own, rows_dev, n_dev, me):
    n = ids_pair.shape[0]
    n_chip = n_dev // 2
    blk = rows_dev // PLANE
    owner, local = ids_pair // rows_dev, lax.rem(ids_pair, rows_dev)
    server = owner ^ (local // blk)
    name = (lax.rem(server, 2) * n_chip + server // 2) * rows_dev + lax.rem(owner, PLANE) * blk + lax.rem(local, blk)
    lane = jnp.arange(n, dtype=jnp.int32)
    key = lax.sort(name * n + lane)
    sid, pos = key // n, lax.rem(key, n)
    n_low = jnp.sum((sid < n_chip * rows_dev).astype(jnp.int32))
    first = sid != jnp.concatenate([jnp.full((1,), -1, jnp.int32), sid[:-1]])
    slot = jnp.cumsum(first.astype(jnp.int32)) - 1
    tgt = sid // rows_dev
    bound = jnp.arange(n_dev + 1, dtype=jnp.int32)
    start = jnp.sum((first[None, :] & (tgt[None, :] < bound[:, None])).astype(jnp.int32), axis=1)
    rank = slot - jnp.sum(jnp.where(tgt[None, :] == bound[:-1, None], start[:-1, None], 0), axis=0)
    code = tgt * (2 * rows_dev) + rank
    count = start[1:] - start[:-1]
    core = lax.rem(me, 2)
    size = jnp.where(core == 0, n_low, n - n_low)
    begin = jnp.where(core == 0, 0, n_low)
    low = jnp.iinfo(jnp.int32).min
    both = jnp.stack([2 * pos + jnp.where(first, 0, low), code])
    both = jnp.concatenate([both, both, both[:, :UNROLL]], axis=1)
    mine = lax.dynamic_slice(both, (0, begin), (2, n + UNROLL))
    valid = jnp.arange(n + UNROLL, dtype=jnp.int32) < size
    most = jnp.iinfo(jnp.int32).max
    uid = lax.sort(jnp.where(first & (sid // (n_chip * rows_dev) == core), sid, most))
    uid = jnp.concatenate([2 * lax.rem(uid, rows_dev), jnp.zeros((512,), jnp.int32)]).reshape((n + 512) // 128, 1, 128)
    start = lax.dynamic_slice(start, (core * n_chip,), (n_chip,))
    return dict(pos=jnp.where(valid, mine[0], 0), code=jnp.where(valid, mine[1], -1), uid=uid, start=start - start[0],
                size=size.reshape(1), by_pos=jnp.where(pos < n_own, pos * (n_dev * 2 * rows_dev) + code, most),
                count=lax.dynamic_slice(count, (core * n_chip,), (n_chip,)), peak=jnp.max(count).reshape(1))


def round_slot(code, span, rnd, trash, width):
    tgt, rank = code // span, lax.rem(code, span) - rnd * SLOTS
    inside = (code >= 0) & (rank >= 0) & (rank < SLOTS)
    return jnp.where(inside, tgt * width + rank, trash)


def solution(mesh):
    n_dev = mesh.shape['emb']
    n_chip = n_dev // 2
    tok_spec = P('emb', None)
    tab_spec = P(None, 'emb', None)

    def step(x_start, d_out, token_ids, w_up, w_down, w_gate, w_proj, tables):
        n_tab, n_tok, n_heads = token_ids.shape
        rows_dev, row_width = tables.shape[1], tables.shape[2]
        n_req = n_tok * n_heads
        tail = (row_width // 128, 128)
        me = lax.axis_index('emb')
        core = lax.rem(me, 2)

        flat_ids = token_ids.reshape(n_tab, n_req)
        ids_pair = jnp.concatenate([flat_ids, swap_cores(flat_ids, n_dev)], axis=1)
        place = lax.rem(me, PLANE).reshape(1)
        split = split_rows(tables, place)
        served = plane_trade(split, n_dev)
        plans = [route_plan(after(ids_pair, split)[t], n_req, rows_dev, n_dev, me) for t in range(n_tab)]

        span = 2 * rows_dev
        in_order = lax.sort(jnp.stack([plan['by_pos'] for plan in plans]), dimension=1)
        code_own = lax.rem(in_order[:, :n_req], n_dev * span)

        def half_slot(plan, rnd, width, trash):
            code = plan['code']
            code = jnp.where(code >= 0, lax.rem(code, n_chip * span), code)
            return round_slot(code, span, rnd, trash, width)

        def id_blocks(which, rnd):
            plan = plans[which]
            return make_ids(plan['uid'], plan['start'], plan['count'], plan['peak'], rnd, 2 * rows_dev)

        blocks = jnp.stack([id_blocks(t, jnp.int32(0)) for t in range(n_tab)], axis=1)
        got = chip_trade(after(blocks, served), n_dev)
        first_ids = [got[:, t].reshape(n_chip * IDW) for t in range(n_tab)]
        got = got.reshape(n_chip, n_tab, IDW)
        rounds = (jnp.max(got[:, :, IDW - 1], axis=0) + SLOTS - 1) // SLOTS

        def more_ids(which, rnd, cid):
            return chip_exchange(id_blocks(which, rnd), cid, n_chip).reshape(n_chip * IDW)

        def own_slot(which, rnd):
            slot = round_slot(code_own[which], span, rnd, 0, SLOTS)
            return jnp.where(core == 0, slot, lax.rem(slot + n_chip * SLOTS, 2 * n_chip * SLOTS))

        def unpack(which, rnd, own):
            return unpack_rows(own_slot(which, rnd), own, swap_cores(own, n_dev), n_heads)

        def fetch_rest(which, first):
            def more(state):
                rnd, rows = state
                ids = more_ids(which, rnd, which)
                sent = owner_gather(ids, served, which, n_chip).reshape((n_chip, SLOTS) + tail)
                new = unpack(which, rnd, chip_exchange(sent, 2 + which, n_chip).reshape((n_chip * SLOTS,) + tail))
                now = lax.rem(code_own[which], span) // SLOTS == rnd
                return rnd + 1, jnp.where(jnp.repeat(now, row_width).reshape(rows.shape), new, rows)

            return lax.while_loop(lambda s: s[0] < rounds[which], more, (jnp.int32(1), first))[1]

        def packed(which, rnd, grad_own, grad_pair):
            plan = plans[which]
            dst = 2 * half_slot(plan, rnd, SLOTS, n_chip * SLOTS)
            return pack_rows(plan['pos'], dst, plan['size'], grad_own, grad_pair, n_chip)

        def pair_rows(grad_rows):
            return grad_rows, swap_cores(grad_rows, n_dev)

        def return_rest(which, first, pair):
            def more(state):
                rnd, total = state
                ids = more_ids(which, rnd, 4 + which)
                rec = chip_exchange(packed(which, rnd, *pair).reshape(n_chip, 2 * SLOTS, 128), 6 + which, n_chip)
                new = owner_scatter(ids, rec.reshape(n_chip * 2 * SLOTS, 128), rows_dev, place)
                return rnd + 1, [p + q for p, q in zip(total, new)]

            return lax.while_loop(lambda s: s[0] < rounds[which], more, (jnp.int32(1), list(first)))[1]

        x1 = layer_plain(x_start, w_up, w_down, 0)
        sent0 = owner_gather(after(first_ids[0], x1), served, 0, n_chip)
        fetched0 = chip_trade(sent0, n_dev)
        sent1 = owner_gather(after(first_ids[1], sent0), served, 1, n_chip)
        fetched1 = chip_trade(sent1, n_dev)
        m1, g1 = layer_table_head(after(x1, sent1), w_up, w_down, w_gate, 1, 0)
        e1 = fetch_rest(0, unpack(0, 0, fetched0))
        x2, h2, x3, a3, dz3, rows3 = layer_middle(x1, m1, g1, e1, d_out, w_up, w_down, w_gate, w_proj, 2)
        pair1 = pair_rows(rows3)
        h3 = last_up(x3, w_up, 3)
        sent1 = packed(1, 0, *pair1)
        returned1 = chip_trade(sent1, n_dev)
        e3 = unpack(1, 0, after(fetched1, sent1))
        e3 = fetch_rest(1, e3)
        c2 = back_table(after(d_out, sent1), h3, x3, a3, dz3, e3, w_up, w_down, w_gate, 3, 1)
        rows1 = back_plain(c2, h2, x2, g1, w_up, w_down, w_proj, 2, 0)
        pair0 = pair_rows(rows1)
        total1 = owner_scatter(first_ids[1], after(returned1, rows1), rows_dev, place)
        total1 = return_rest(1, total1, pair1)
        placed1 = place_trade(total1, n_dev)
        sent0 = packed(0, 0, pair0[0], after(pair0[1], total1[0]))
        returned0 = chip_trade(sent0, n_dev)
        x_end = last_down(after(x3, sent0), h3, a3, e3, w_down, w_proj, 3, 1)
        grads = finish_table([after(p, x_end) for p in placed1], None, 1, n_tab)
        total0 = owner_scatter(first_ids[0], after(returned0, x_end), rows_dev, place)
        total0 = return_rest(0, total0, pair0)
        grads = finish_table(place_exchange(total0, 8), grads, 0, n_tab)
        return x_end, grads

    return jax.shard_map(step, mesh=mesh, in_specs=(tok_spec, tok_spec, tab_spec, P(), P(), P(), P(), tab_spec),
                         out_specs=(tok_spec, tab_spec), check_vma=False)
```

time: 3050 us -> 865 us (0.28)
  the two profiles are of different devices: /device:TPU:21 before, /device:TPU:25 now
where the time goes in v1:
time: 865 us; the launch traced here: 856 us
  Pallas kernels  565 us (65%)
  waiting for transfers between devices  120 us (14%)
  starting transfers between devices  63 us (7%)
  other arithmetic  52.4 us (6%)
  local copies, waits for them, and re-layouts  33.9 us (4%)
  between operations  18.9 us (2%)
    pallas_call x7, Pallas kernels, token_kernel(): pl.pallas_call(kernel, grid=(tokens // tile,), out_shape=[s for s, _ in o...  348 us
    all_to_all x5, waiting for transfers between devices, chip_trade(): return lax.all_to_all(x, 'emb', 0, 0, axis_index_groups=groups, tiled=True)  68.2 us
    pallas_call x1, Pallas kernels, place_exchange(): pl.pallas_call(kernel, out_shape=[shape] * (PLANE - 1), in_specs=[ANY_SPE...  56.5 us
    pallas_call x2, Pallas kernels, pack_rows(): pl.pallas_call(kernel, out_shape=shape_of((n_row, 128), F32), in_specs=[S...  53.7 us
    ppermute x7, waiting for transfers between devices, place_trade(): lax.ppermute(blocks[b], 'emb', [(i, i ^ b) for i in range(n_dev)])  51.4 us
    all_to_all x5, starting transfers between devices, chip_trade(): return lax.all_to_all(x, 'emb', 0, 0, axis_index_groups=groups, tiled=True)  35.3 us
    pallas_call x2, Pallas kernels, unpack_rows(): pl.pallas_call(kernel, out_shape=shape_of((tokens, per * 128), BF16), in_...  34.2 us
    pallas_call x2, Pallas kernels, owner_scatter(): pl.pallas_call(kernel, out_shape=[shape_of((blk_rows, 128), F32)] * PLANE...  31.6 us
  transfers between devices with their start and end apart: 18, of which 6 were waited for; matrix products, arithmetic and copies ran while one was open for 7% of the time, Pallas kernels for 42%

profile of v1, /device:TPU:25, one launch (start us, length us, event | category | flops | bytes accessed | tf_op | source)
XLA Modules:
  0.0 855.7 jit_solution(14900424461611955261)
XLA Ops:
  19.4 46.2 %shard_map.95.refs_0_ = bf16[2048,1024]{1,0:T(8,128)(2,1)} custom-call(bf16[2048,1024]{1,0:T(8,128)(2,1)} %refs_0_.1, bf16[4,1024,4096]{2,1,0:T(8,128)(2,1)} %refs_4_.4, bf16[4,4096,1024]{2,1,0:T(8,128)(2,1)} %refs_4_.5), custom_call_target="tpu_custom_call" | custom-call | flops 39600001024 | bytes 33554432 | tf_op jit(solution)/shard_map/pallas_call | solution.py:97
  74.5 7.9 sort.63
  127.1 12.7 %owner_gather.12 = bf16[5376,2,128]{2,1,0:T(2,128)(2,1)} custom-call(s32[16384]{0:T(1024)} %get-tuple-element.944.ids_ref, bf16[8,2,512,256]{3,2,1,0:T(8,128)(2,1)} %all-to-all-done.served_ref), custom_call_target="tpu_custom_call" | custom-call | flops 12600000512 | bytes 4194304 | tf_op jit(solution)/shard_map/owner_gather/pallas_call | solution.py:363
  146.2 22.2 %sort.69.cloned.1.call-done = s32[2,16384]{1,0:T(2,128)} async-done(((s32[2,16384]{1,0:T(2,128)}), s32[2,16384]{1,0:T(2,128)}) %sort.69.cloned.1.call-update) | async-done | bytes 131088 | tf_op jit(solution)/shard_map/sort | solution.py:657
  171.2 12.7 %owner_gather.13 = bf16[5376,2,128]{2,1,0:T(2,128)(2,1)} custom-call(s32[16384]{0:T(1024)} %get-tuple-element.945.ids_ref, bf16[8,2,512,256]{3,2,1,0:T(8,128)(2,1)} %all-to-all-done.served_ref), custom_call_target="tpu_custom_call" | custom-call | flops 12600000512 | bytes 4194304 | tf_op jit(solution)/shard_map/owner_gather/pallas_call | solution.py:363
  184.9 17.0 %all-to-all-done.2.own_ref = bf16[5376,2,128]{2,1,0:T(2,128)(2,1)} async-done(((bf16[5376,2,128]{2,1,0:T(2,128)(2,1)}), bf16[5376,2,128]{2,1,0:T(2,128)(2,1)}, u32[]{:S(2)}, u32[]{:S(2)}) %all-to-all-start.2) | async-done | bytes 2752544 | tf_op jit(solution)/shard_map/all_to_all | solution.py:529
  206.3 53.0 %shard_map.96 = (bf16[2048,1024]{1,0:T(8,128)(2,1)}, bf16[2048,1024]{1,0:T(8,128)(2,1)}) custom-call(bf16[2048,1024]{1,0:T(8,128)(2,1)} %shard_map.95.refs_0_, bf16[4,1024,4096]{2,1,0:T(8,128)(2,1)} %refs_4_.4, bf16[4,4096,1024]{2,1,0:T(8,128)(2,1)} %refs_4_.5, bf16[2,1024,1024]{2,1,0:T(8,128)(2,1)} %refs_8_.3), custom_call_target="tpu_custom_call" | custom-call | flops 44999999488 | bytes 33554432 | tf_op jit(solution)/shard_map/pallas_call | solution.py:97
  259.4 17.0 %unpack_rows.12 = bf16[2048,1024]{1,0:T(8,128)(2,1)} custom-call(s32[8192]{0:T(1024)} %get-tuple-element.1187.idx_ref, bf16[5376,2,128]{2,1,0:T(2,128)(2,1)} %all-to-all-done.2.own_ref, bf16[5376,2,128]{2,1,0:T(2,128)(2,1)} %collective-permute-done.3.pair_ref), custom_call_target="tpu_custom_call" | custom-call | flops 14400000000 | bytes 8388608 | tf_op jit(solution)/shard_map/unpack_rows/pallas_call | solution.py:400
  277.3 70.2 %shard_map.97 = (bf16[2048,1024]{1,0:T(8,128)(2,1)}, bf16[2048,4096]{1,0:T(8,128)(2,1)}, bf16[2048,1024]{1,0:T(8,128)(2,1)}, bf16[2048,1024]{1,0:T(8,128)(2,1)},...) custom-call(bf16[2048,1024]{1,0:T(8,128)(2,1)} %shard_map.95.refs_0_, bf16[2048,1024]{1,0:T(8,128)(2,1)} %get-tuple-element.947.refs_1_, ...), custom_call_target="tpu_custom_call" | custom-call | flops 55800000512 | bytes 33554432 | tf_op jit(solution)/shard_map/pallas_call | solution.py:97
  366.5 27.0 %pack_rows.10 = f32[10752,128]{1,0:T(8,128)} custom-call(s32[16400]{0:T(1024)} %fusion.49.pos_ref, s32[16400]{0:T(1024)} %fusion.47.dst_ref, s32[1]{0:T(128)} %bitcast.45.size_ref, f32[16384,128]{1,0:T(8,128)} %get-tuple-element.1738.own_ref, f32[16384,128]{1,0:T(8,128)} %collective-permute-done.4.pair_ref), custom_call_target="tpu_custom_call" | custom-call | flops 23399999488 | bytes 16777216 | tf_op jit(solution)/shard_map/pack_rows/pallas_call | solution.py:434
  393.4 23.5 %all-to-all-done.3.own_ref = bf16[5376,2,128]{2,1,0:T(2,128)(2,1)} async-done(((bf16[5376,2,128]{2,1,0:T(2,128)(2,1)}), bf16[5376,2,128]{2,1,0:T(2,128)(2,1)}, u32[]{:S(2)}, u32[]{:S(2)}) %all-to-all-start.3) | async-done | bytes 2752544 | tf_op jit(solution)/shard_map/all_to_all | solution.py:529
  421.1 25.3 %shard_map.98.refs_1_ = bf16[2048,4096]{1,0:T(8,128)(2,1)} custom-call(bf16[2048,1024]{1,0:T(8,128)(2,1)} %get-tuple-element.970.refs_0_.refs_2_, bf16[4,1024,4096]{2,1,0:T(8,128)(2,1)} %refs_4_.4), custom_call_target="tpu_custom_call" | custom-call | flops 19800000512 | bytes 33554432 | tf_op jit(solution)/shard_map/pallas_call | solution.py:97
  446.5 8.1 all-to-all-start.4
  454.6 17.2 %unpack_rows.13 = bf16[2048,1024]{1,0:T(8,128)(2,1)} custom-call(s32[8192]{0:T(1024)} %get-tuple-element.1184.idx_ref, bf16[5376,2,128]{2,1,0:T(2,128)(2,1)} %all-to-all-done.3.own_ref, bf16[5376,2,128]{2,1,0:T(2,128)(2,1)} %collective-permute-done.5.pair_ref), custom_call_target="tpu_custom_call" | custom-call | flops 14400000000 | bytes 8388608 | tf_op jit(solution)/shard_map/unpack_rows/pallas_call | solution.py:400
  474.1 60.7 %shard_map.99.refs_0_ = f32[2048,1024]{1,0:T(8,128)} custom-call(bf16[2048,1024]{1,0:T(8,128)(2,1)} %refs_0_.2, bf16[2048,4096]{1,0:T(8,128)(2,1)} %shard_map.98.refs_1_, bf16[2048,1024]{1,0:T(8,128)(2,1)} %get-tuple-element.970.refs_0_.refs_2_, bf16[2048,1024]{1,0:T(8,128)(2,1)} %get-tuple-element.953.refs_3_.refs_2_, ...), custom_call_target="tpu_custom_call" | custom-call | flops 52200001536 | bytes 33554432 | tf_op jit(solution)/shard_map/pallas_call | solution.py:97
  534.9 55.0 %shard_map.100.own_ref = f32[16384,128]{1,0:T(8,128)} custom-call(f32[2048,1024]{1,0:T(8,128)} %shard_map.99.refs_0_, bf16[2048,4096]{1,0:T(8,128)(2,1)} %get-tuple-element.957.refs_1_, bf16[2048,1024]{1,0:T(8,128)(2,1)} %get-tuple-element.958.refs_2_, bf16[2048,1024]{1,0:T(8,128)(2,1)} %get-tuple-element.948.refs_2_.refs_3_, ...), custom_call_target="tpu_custom_call" | custom-call | flops 52200001536 | bytes 33554432 | tf_op jit(solution)/shard_map/pallas_call | solution.py:97
  590.5 15.7 %owner_scatter.10 = (f32[1024,128]{1,0:T(8,128)}, f32[1024,128]{1,0:T(8,128)}, f32[1024,128]{1,0:T(8,128)}, f32[1024,128]{1,0:T(8,128)}, f32[1024,128]{1,0:T(8,1...) custom-call(s32[16384]{0:T(1024)} %get-tuple-element.945.ids_ref, s32[1]{0:T(128)} %bitcast.22.place_ref, ...), custom_call_target="tpu_custom_call" | custom-call | flops 17999998976 | bytes 16777216 | tf_op jit(solution)/shard_map/owner_scatter/pallas_call | solution.py:484
  608.4 26.7 %pack_rows.11 = f32[10752,128]{1,0:T(8,128)} custom-call(s32[16400]{0:T(1024)S(1)} %copy-done.52, s32[16400]{0:T(1024)} %fusion.43.dst_ref, s32[1]{0:T(128)} %bitcast.42.size_ref, f32[16384,128]{1,0:T(8,128)} %shard_map.100.own_ref, f32[16384,128]{1,0:T(8,128)} %collective-permute-done.6.pair_ref), custom_call_target="tpu_custom_call" | custom-call | flops 23399999488 | bytes 16777216 | tf_op jit(solution)/shard_map/pack_rows/pallas_call | solution.py:434
  647.6 43.3 %collective-permute-done.13.refs_7_ = f32[1024,128]{1,0:T(8,128)S(1)} collective-permute-done((f32[1024,128]{1,0:T(8,128)S(1)}, f32[1024,128]{1,0:T(8,128)S(1)}, u32[]{:S(2)}, u32[]{:S(2)}) %collective-permute-start.13) | collective-permute-done | bytes 524320 | tf_op jit(solution)/shard_map/ppermute | solution.py:562
  698.7 8.1 collective-permute-done.12.refs_6_
  707.8 37.9 %shard_map.101 = bf16[2048,1024]{1,0:T(8,128)(2,1)} custom-call(bf16[2048,1024]{1,0:T(8,128)(2,1)} %get-tuple-element.970.refs_0_.refs_2_, bf16[2048,4096]{1,0:T(8,128)(2,1)} %shard_map.98.refs_1_, bf16[2048,1024]{1,0:T(8,128)(2,1)} %get-tuple-element.953.refs_3_.refs_2_, bf16[2048,1024]{1,0:T(8,128)(2,1)} %get-tuple-element.956.refs_5_.refs_3_, ...), custom_call_target="tpu_custom_call" | custom-call | flops 27000000512 | bytes 33554432 | tf_op jit(solution)/shard_map/pallas_call | solution.py:97
  749.0 23.3 %all-to-all-done.5 = f32[16,672,128]{2,1,0:T(8,128)} async-done(((f32[16,672,128]{2,1,0:T(8,128)}), f32[16,672,128]{2,1,0:T(8,128)}, u32[]{:S(2)}, u32[]{:S(2)}) %all-to-all-start.5) | async-done | bytes 5505056 | tf_op jit(solution)/shard_map/all_to_all | solution.py:529
  772.4 15.8 %owner_scatter.11 = (f32[1024,128]{1,0:T(8,128)}, f32[1024,128]{1,0:T(8,128)}, f32[1024,128]{1,0:T(8,128)}, f32[1024,128]{1,0:T(8,128)}, f32[1024,128]{1,0:T(8,1...) custom-call(s32[16384]{0:T(1024)} %get-tuple-element.944.ids_ref, s32[1]{0:T(128)} %bitcast.22.place_ref, ...), custom_call_target="tpu_custom_call" | custom-call | flops 17999998976 | bytes 16777216 | tf_op jit(solution)/shard_map/owner_scatter/pallas_call | solution.py:484
  788.9 56.5 %place_exchange.1 = (f32[1024,128]{1,0:T(8,128)}, f32[1024,128]{1,0:T(8,128)}, f32[1024,128]{1,0:T(8,128)}, f32[1024,128]{1,0:T(8,128)}, f32[1024,128]{1,0:T(8,1...) custom-call(f32[1024,128]{1,0:T(8,128)} %get-tuple-element.1882, f32[1024,128]{1,0:T(8,128)} %get-tuple-element.1883, ...), custom_call_target="tpu_custom_call" | custom-call | flops 44999999488 | bytes 4194304 | tf_op jit(solution)/shard_map/place_exchange/pallas_call | solution.py:582
  (162 shorter events, 136.2 us)
Async XLA Ops:
  10.3 55.2 %collective-permute-start.2 = (s32[2,8192]{1,0:T(2,128)S(1)}, s32[2,8192]{1,0:T(2,128)S(1)}, u32[]{:S(2)}, u32[]{:S(2)}) collective-permute-start(s32[2,8192]{1,0:T(2,128)S(1)} %reshape.156), channel_id=1, source_target_pairs={{0,1},{1,0},{2,3},{3,2},{4,5},{5,4},{6,7},{7,6},{8,9},{9,8},{10,11... | collective-permute-start | bytes 196616 | tf_op jit(solution)/shard_map/ppermute | solution.py:524
  14.8 99.3 %all-to-all-start = ((bf16[8,2,512,256]{3,2,1,0:T(8,128)(2,1)}), bf16[8,2,512,256]{3,2,1,0:T(8,128)(2,1)}, u32[]{:S(2)}, u32[]{:S(2)}) async-start(bf16[8,2,512,256]{3,2,1,0:T(8,128)(2,1)} %split_rows.1), calls=%async_computation | async-start | bytes 8388608 | tf_op jit(solution)/shard_map/all_to_all | solution.py:558
  114.8 11.7 %all-to-all-start.1 = ((s32[16,2,8,128]{3,2,1,0:T(8,128)}), s32[16,2,8,128]{3,2,1,0:T(8,128)S(1)}, u32[]{:S(2)}, u32[]{:S(2)}) async-start(s32[16,2,8,128]{3,2,1,0:T(8,128)} %copy.29), calls=%async_computation.1 | async-start | bytes 262144 | tf_op jit(solution)/shard_map/all_to_all | solution.py:529
  139.9 62.0 %all-to-all-start.2 = ((bf16[5376,2,128]{2,1,0:T(2,128)(2,1)}), bf16[5376,2,128]{2,1,0:T(2,128)(2,1)}, u32[]{:S(2)}, u32[]{:S(2)}) async-start(bf16[5376,2,128]{2,1,0:T(2,128)(2,1)} %owner_gather.12), calls=%async_computation.2 | async-start | bytes 5505024 | tf_op jit(solution)/shard_map/all_to_all | solution.py:529
  201.8 57.5 %collective-permute-start.3 = (bf16[5376,2,128]{2,1,0:T(2,128)(2,1)}, bf16[5376,2,128]{2,1,0:T(2,128)(2,1)}, u32[]{:S(2)}, u32[]{:S(2)}) collective-permute-start(bf16[5376,2,128]{2,1,0:T(2,128)(2,1)} %all-to-all-done.2.own_ref), channel_id=1, source_target_pairs={{0,1},{1,0},{2,3},{3,2},{4,5},{5,4},{6,7},{7,6},{8,9},{9,8},{10,11... | collective-permute-start | bytes 8257544 | tf_op jit(solution)/shard_map/ppermute | solution.py:524
  277.2 70.3 %copy-start.56 = (s32[132,1,128]{2,1,0:T(1,128)}, s32[132,1,128]{2,1,0:T(1,128)S(1)}, u32[]{:S(2)}) copy-start(s32[132,1,128]{2,1,0:T(1,128)S(1)} %get-tuple-element.1904) | copy-start | bytes 202756
  277.2 73.1 %copy-start.47 = (s32[16384]{0:T(1024)S(1)}, s32[16384]{0:T(1024)}, u32[]{:S(2)}) copy-start(s32[16384]{0:T(1024)} %get-tuple-element.1156) | copy-start | bytes 196612
  277.3 73.1 %copy-start.48 = (s32[16384]{0:T(1024)S(1)}, s32[16384]{0:T(1024)}, u32[]{:S(2)}) copy-start(s32[16384]{0:T(1024)} %get-tuple-element.1152) | copy-start | bytes 196612
  277.3 73.1 %copy-start.49 = (s32[16384]{0:T(1024)S(1)}, s32[16384]{0:T(1024)}, u32[]{:S(2)}) copy-start(s32[16384]{0:T(1024)} %get-tuple-element.1161) | copy-start | bytes 196612
  277.3 73.1 %copy-start.50 = (s32[16384]{0:T(1024)S(1)}, s32[16384]{0:T(1024)}, u32[]{:S(2)}) copy-start(s32[16384]{0:T(1024)} %get-tuple-element.1163) | copy-start | bytes 196612
  347.5 18.9 %collective-permute-start.4 = (f32[16384,128]{1,0:T(8,128)}, f32[16384,128]{1,0:T(8,128)}, u32[]{:S(2)}, u32[]{:S(2)}) collective-permute-start(f32[16384,128]{1,0:T(8,128)} %get-tuple-element.1738.own_ref), channel_id=1, source_target_pairs={{0,1},{1,0},{2,3},{3,2},{4,5},{5,4},{6,7},{7,6},{8,9},{9,8},{10,11... | collective-permute-start | bytes 25165832 | tf_op jit(solution)/shard_map/ppermute | solution.py:524
  352.2 64.7 %all-to-all-start.3 = ((bf16[5376,2,128]{2,1,0:T(2,128)(2,1)}), bf16[5376,2,128]{2,1,0:T(2,128)(2,1)}, u32[]{:S(2)}, u32[]{:S(2)}) async-start(bf16[5376,2,128]{2,1,0:T(2,128)(2,1)} %owner_gather.13), calls=%async_computation.3 | async-start | bytes 5505024 | tf_op jit(solution)/shard_map/all_to_all | solution.py:529
  416.9 37.7 %collective-permute-start.5 = (bf16[5376,2,128]{2,1,0:T(2,128)(2,1)}, bf16[5376,2,128]{2,1,0:T(2,128)(2,1)}, u32[]{:S(2)}, u32[]{:S(2)}) collective-permute-start(bf16[5376,2,128]{2,1,0:T(2,128)(2,1)} %all-to-all-done.3.own_ref), channel_id=1, source_target_pairs={{0,1},{1,0},{2,3},{3,2},{4,5},{5,4},{6,7},{7,6},{8,9},{9,8},{10,11... | collective-permute-start | bytes 8257544 | tf_op jit(solution)/shard_map/ppermute | solution.py:524
  446.5 144.0 %all-to-all-start.4 = ((f32[16,672,128]{2,1,0:T(8,128)}), f32[16,672,128]{2,1,0:T(8,128)}, u32[]{:S(2)}, u32[]{:S(2)}) async-start(f32[16,672,128]{2,1,0:T(8,128)} %bitcast.130), calls=%async_computation.4 | async-start | bytes 11010048 | tf_op jit(solution)/shard_map/all_to_all | solution.py:529
  589.9 18.5 %collective-permute-start.6 = (f32[16384,128]{1,0:T(8,128)}, f32[16384,128]{1,0:T(8,128)}, u32[]{:S(2)}, u32[]{:S(2)}) collective-permute-start(f32[16384,128]{1,0:T(8,128)} %shard_map.100.own_ref), channel_id=1, source_target_pairs={{0,1},{1,0},{2,3},{3,2},{4,5},{5,4},{6,7},{7,6},{8,9},{9,8},{10,11... | collective-permute-start | bytes 25165832 | tf_op jit(solution)/shard_map/ppermute | solution.py:524
  635.2 71.6 %copy-start.9 = (f32[1024,128]{1,0:T(8,128)S(1)}, f32[1024,128]{1,0:T(8,128)}, u32[]{:S(2)}) copy-start(f32[1024,128]{1,0:T(8,128)} %get-tuple-element.996) | copy-start | bytes 1572868
  635.2 137.2 %all-to-all-start.5 = ((f32[16,672,128]{2,1,0:T(8,128)}), f32[16,672,128]{2,1,0:T(8,128)}, u32[]{:S(2)}, u32[]{:S(2)}) async-start(f32[16,672,128]{2,1,0:T(8,128)} %bitcast.131), calls=%async_computation.5 | async-start | bytes 11010048 | tf_op jit(solution)/shard_map/all_to_all | solution.py:529
  642.0 48.9 %collective-permute-start.13 = (f32[1024,128]{1,0:T(8,128)S(1)}, f32[1024,128]{1,0:T(8,128)S(1)}, u32[]{:S(2)}, u32[]{:S(2)}) collective-permute-start(f32[1024,128]{1,0:T(8,128)S(1)} %copy-done.18), channel_id=1, source_target_pairs={{0,7},{1,6},{2,5},{3,4},{4,3},{5,2},{6,1},{7,0},{8,15},{9,14},{10,... | collective-permute-start | bytes 1572872 | tf_op jit(solution)/shard_map/ppermute | solution.py:562
  644.0 62.8 %collective-permute-start.12 = (f32[1024,128]{1,0:T(8,128)S(1)}, f32[1024,128]{1,0:T(8,128)}, u32[]{:S(2)}, u32[]{:S(2)}) collective-permute-start(f32[1024,128]{1,0:T(8,128)S(1)} %copy-done.15), channel_id=1, source_target_pairs={{0,6},{1,7},{2,4},{3,5},{4,2},{5,3},{6,0},{7,1},{8,14},{9,15},{10,... | collective-permute-start | bytes 1572872 | tf_op jit(solution)/shard_map/ppermute | solution.py:562
  644.3 101.4 %collective-permute-start.11 = (f32[1024,128]{1,0:T(8,128)}, f32[1024,128]{1,0:T(8,128)}, u32[]{:S(2)}, u32[]{:S(2)}) collective-permute-start(f32[1024,128]{1,0:T(8,128)} %get-tuple-element.1004), channel_id=1, source_target_pairs={{0,5},{1,4},{2,7},{3,6},{4,1},{5,0},{6,3},{7,2},{8,13},{9,12},{10,... | collective-permute-start | bytes 1572872 | tf_op jit(solution)/shard_map/ppermute | solution.py:562
  646.2 99.5 %collective-permute-start.10 = (f32[1024,128]{1,0:T(8,128)}, f32[1024,128]{1,0:T(8,128)}, u32[]{:S(2)}, u32[]{:S(2)}) collective-permute-start(f32[1024,128]{1,0:T(8,128)} %get-tuple-element.1002), channel_id=1, source_target_pairs={{0,4},{1,5},{2,6},{3,7},{4,0},{5,1},{6,2},{7,3},{8,12},{9,13},{10,... | collective-permute-start | bytes 1572872 | tf_op jit(solution)/shard_map/ppermute | solution.py:562
  646.5 99.3 %collective-permute-start.9 = (f32[1024,128]{1,0:T(8,128)}, f32[1024,128]{1,0:T(8,128)}, u32[]{:S(2)}, u32[]{:S(2)}) collective-permute-start(f32[1024,128]{1,0:T(8,128)} %get-tuple-element.1000), channel_id=1, source_target_pairs={{0,3},{1,2},{2,1},{3,0},{4,7},{5,6},{6,5},{7,4},{8,11},{9,10},{10,... | collective-permute-start | bytes 1572872 | tf_op jit(solution)/shard_map/ppermute | solution.py:562
  691.0 54.8 %collective-permute-start.8 = (f32[1024,128]{1,0:T(8,128)S(1)}, f32[1024,128]{1,0:T(8,128)}, u32[]{:S(2)}, u32[]{:S(2)}) collective-permute-start(f32[1024,128]{1,0:T(8,128)S(1)} %copy-done.12), channel_id=1, source_target_pairs={{0,2},{1,3},{2,0},{3,1},{4,6},{5,7},{6,4},{7,5},{8,10},{9,11},{10,... | collective-permute-start | bytes 1572872 | tf_op jit(solution)/shard_map/ppermute | solution.py:562
  706.7 39.0 %collective-permute-start.7 = (f32[1024,128]{1,0:T(8,128)S(1)}, f32[1024,128]{1,0:T(8,128)}, u32[]{:S(2)}, u32[]{:S(2)}) collective-permute-start(f32[1024,128]{1,0:T(8,128)S(1)} %copy-done.9), channel_id=1, source_target_pairs={{0,1},{1,0},{2,3},{3,2},{4,5},{5,4},{6,7},{7,6},{8,9},{9,8},{10,11... | collective-permute-start | bytes 1572872 | tf_op jit(solution)/shard_map/ppermute | solution.py:562
  (16 other events, 477.3 us)
Sparse Core Ops, SparseCore 0:
  124.5 43.6 sort.71.cloned.1.call-done
  (1 shorter events, 0.0 us)

commit v2 on v1

--- a/solution.py
+++ b/solution.py
@@ -17,6 +17,11 @@
 SLOTS = 336
 IDW = 1024
 UNROLL = 16
+LANES = 128
+COLS = 256
+CHUNK = 512
+TILE = 256
+WIDE_TILE = 512
 
 SMEM_SPEC = pl.BlockSpec(memory_space=pltpu.SMEM)
 VMEM_SPEC = pl.BlockSpec(memory_space=pltpu.VMEM)
@@ -31,8 +36,8 @@
     return pltpu.CompilerParams(vmem_limit_bytes=VMEM_LIMIT, collective_id=cid, has_side_effects=True)
 
 
-def cost(us, nbytes):
-    return pl.CostEstimate(flops=int(us * 9 * 10**8), bytes_accessed=nbytes, transcendentals=0)
+def cost(us):
+    return pl.CostEstimate(flops=int(us * 9e8), bytes_accessed=2**23, transcendentals=0)
 
 
 def shape_of(shape, dtype):
@@ -62,8 +67,72 @@
     return lax.rsqrt(jnp.mean(x_f * x_f, axis=-1, keepdims=True) + EPS)
 
 
-def token_kernel(body, tile, tokens, ins, weights, outs, scratch, us):
+def pair_at(index):
+    return pl.ds(pl.multiple_of(index, 2), 2)
+
+
+def owner_gather(ids, served, which, n_src):
+    work = gather_step(served, which, n_src)
+
+    def kernel(ids_ref, served_ref, out_ref, *scratch):
+        work((ids_ref, served_ref), out_ref, scratch)
+
+    return pl.pallas_call(
+        kernel, out_shape=gathered(served, n_src), in_specs=[SMEM_SPEC, ANY_SPEC], out_specs=VMEM_SPEC,
+        scratch_shapes=gather_scratch(served), compiler_params=local_params(), name="owner_gather", cost_estimate=cost(14),
+    )(ids, served)
+
+
+def gathered(served, n_src):
+    return shape_of((n_src * SLOTS, served.shape[3] // LANES, LANES), BF16)
+
+
+def gather_scratch(served):
+    blk, width = served.shape[2:]
+    return [pltpu.VMEM((PLANE, blk, width), BF16), pltpu.VMEM((PLANE * blk * width // LANES + 8, LANES), F32),
+            pltpu.SemaphoreType.DMA((PLANE,))]
+
+
+def gather_step(served, which, n_src):
+    blk, width = served.shape[2:]
+    pieces = width // LANES
+
+    def work(ins, out_ref, scratch):
+        ids_ref, served_ref = ins
+        native, flat, isem = scratch
+        reads = [pltpu.make_async_copy(served_ref.at[b, which], native.at[b], isem.at[b]) for b in range(PLANE)]
+        for c in reads:
+            c.start()
+        for b in range(PLANE):
+            reads[b].wait()
+            for c in range(pieces):
+                flat[pl.ds(b * blk * pieces + c, blk, stride=pieces), :] = native[b, :, c * LANES:(c + 1) * LANES].astype(F32)
+
+        def src(s, c):
+            def part(b, c):
+                for j in range(UNROLL):
+                    r = b * UNROLL + j
+                    out_ref[s * SLOTS + r] = flat[pair_at(ids_ref[s * IDW + r]), :].astype(BF16)
+                return c
+
+            lax.fori_loop(0, SLOTS // UNROLL, part, 0)
+            return c
+
+        lax.fori_loop(0, n_src, src, 0)
+
+    return work
+
+
+def token_kernel(body, tile, tokens, ins, weights, outs, scratch, us, extra_ins=(), extra_outs=(), first_step=None, mirror=None):
+    steps = tokens // tile
+    if mirror is not None:
+        extra_outs = list(extra_outs) + [mirror[0]] * 2
+        scratch = list(scratch) + [pltpu.VMEM((2, tile * mirror[1]) + mirror[0].shape[1:], mirror[0].dtype)] + [
+            pltpu.SemaphoreType.DMA((steps,))] * 3
+    ins = list(ins) + [(a, spec) for a, spec in extra_ins]
+    outs = list(outs) + [(s, ANY_SPEC) for s in extra_outs]
     n_in, n_w, n_out = len(ins), len(weights), len(outs)
+    n_own_in, n_own_out = n_in - len(extra_ins), n_out - len(extra_outs)
 
     def kernel(*refs):
         in_refs = refs[:n_in]
@@ -79,6 +148,8 @@
         def _():
             for c in copies:
                 c.start()
+            if first_step is not None:
+                first_step(in_refs[n_own_in:], out_refs[n_own_out:], rest)
 
         def need(*which):
             @pl.when(opening)
@@ -86,9 +157,47 @@
                 for i in which:
                     copies[i].wait()
 
-        body(need, in_refs, w_vmem, out_refs, rest)
+        if mirror is None:
+            body(need, in_refs[:n_own_in], w_vmem, out_refs[:n_own_out], rest)
+            return
+        i = pl.program_id(0)
+        other = lax.axis_index('emb') ^ 1
+        barrier = pltpu.get_barrier_semaphore()
+        own, pair = out_refs[-2:]
+        stage, keep_sem, send_sem, recv_sem = rest[-4:]
+        per = tile * mirror[1]
+
+        def keep(j):
+            return pltpu.make_async_copy(stage.at[lax.rem(j, 2)], own.at[pl.ds(j * per, per)], keep_sem.at[j])
+
+        def send(j):
+            return pltpu.make_async_remote_copy(
+                src_ref=own.at[pl.ds(j * per, per)], dst_ref=pair.at[pl.ds(j * per, per)], send_sem=send_sem.at[j],
+                recv_sem=recv_sem.at[j], device_id=(other,), device_id_type=MESH)
+
+        @pl.when(opening)
+        def _():
+            pl.semaphore_signal(barrier, inc=1, device_id=(other,), device_id_type=MESH)
+            pl.semaphore_wait(barrier, 1)
+
+        body(need, in_refs[:n_own_in], w_vmem, out_refs[:n_own_out], list(rest[:-4]) + [stage.at[lax.rem(i, 2)]])
+        keep(i).start()
+
+        @pl.when(i > 0)
+        def _():
+            keep(i - 1).wait()
+            send(i - 1).start()
+
+        @pl.when(i == steps - 1)
+        def _():
+            keep(i).wait()
+            send(i).start()
+            for j in range(steps):
+                send(j).wait()
 
     def tiled(shape, per):
+        if isinstance(per, pl.BlockSpec):
+            return per
         return pl.BlockSpec((tile * per,) + shape[1:], lambda i: (i,) + (0,) * (len(shape) - 1))
 
     in_specs = [tiled(a.shape, per) for a, per in ins] + [ANY_SPEC] * n_w
@@ -96,12 +205,12 @@
     w_scratch = [pltpu.VMEM(w.shape[1:], w.dtype) for w, _ in weights]
     return pl.pallas_call(
         kernel, grid=(tokens // tile,), out_shape=[s for s, _ in outs], in_specs=in_specs, out_specs=out_specs,
-        scratch_shapes=w_scratch + [pltpu.SemaphoreType.DMA((n_w,))] + scratch,
-        compiler_params=local_params(), cost_estimate=cost(us, 2**25),
+        scratch_shapes=w_scratch + [pltpu.SemaphoreType.DMA((n_w,))] + list(scratch),
+        compiler_params=local_params() if mirror is None else remote_params(mirror[2]), cost_estimate=cost(us),
     )(*[a for a, _ in ins], *[w for w, _ in weights])
 
 
-def mlp_up(u, w_up, act, h_ref, chunk=512):
+def mlp_up(u, w_up, act, h_ref, chunk=CHUNK):
     for j in range(w_up.shape[1] // chunk):
         cols = slice(j * chunk, (j + 1) * chunk)
         h = dot_nn(u, w_up[:, cols]).astype(BF16)
@@ -113,12 +222,12 @@
 
 def store_rows(ref, value):
     tokens, width = value.shape
-    n = width // 128
+    n = width // LANES
     for c in range(n):
-        ref[pl.ds(c, tokens, stride=n), :] = value[:, c * 128:(c + 1) * 128]
-
-
-def layer_plain(x, w_up, w_down, layer, tile=512):
+        ref[pl.ds(c, tokens, stride=n), :] = value[:, c * LANES:(c + 1) * LANES]
+
+
+def layer_plain(x, w_up, w_down, layer, tile=WIDE_TILE):
     tokens, d = x.shape
 
     def body(need, ins, w, outs, rest):
@@ -126,8 +235,8 @@
         x_f = ins[0][...].astype(F32)
         u = (x_f * rms(x_f)).astype(BF16)
         mlp_up(u, w[0], rest[0], None)
-        for q in range(d // 256):
-            cols = slice(q * 256, (q + 1) * 256)
+        for q in range(d // COLS):
+            cols = slice(q * COLS, (q + 1) * COLS)
             m = dot_nn(rest[0][...], w[1][:, cols]).astype(BF16)
             outs[0][:, cols] = (ins[0][:, cols].astype(F32) + m.astype(F32)).astype(BF16)
 
@@ -135,8 +244,17 @@
                         [(shape_of(x.shape, BF16), 1)], [pltpu.VMEM((tile, w_up.shape[2]), BF16)], 44)[0]
 
 
-def layer_table_head(x, w_up, w_down, w_gate, layer, which, tile=512):
+def layer_table_head(x, w_up, w_down, w_gate, layer, which, ids, served, n_src, tile=WIDE_TILE):
     tokens, d = x.shape
+    gather = gather_step(served, 1, n_src)
+    sent = gathered(served, n_src)
+
+    def first_step(ins, outs, rest):
+        stage, sem = rest[-2:]
+        gather(ins, stage, rest[1:-2])
+        done = pltpu.make_async_copy(stage, outs[0], sem)
+        done.start()
+        done.wait()
 
     def body(need, ins, w, outs, rest):
         need(0, 1, 2)
@@ -145,23 +263,25 @@
         mlp_up(u, w[0], rest[0], None)
         a = dot_nn(u, w[2][...]).astype(BF16)
         outs[1][...] = gelu(a.astype(F32)).astype(BF16)
-        for q in range(d // 256):
-            cols = slice(q * 256, (q + 1) * 256)
+        for q in range(d // COLS):
+            cols = slice(q * COLS, (q + 1) * COLS)
             outs[0][:, cols] = dot_nn(rest[0][...], w[1][:, cols]).astype(BF16)
 
     return token_kernel(body, tile, tokens, [(x, 1)],
                         [(w_up, layer), (w_down, layer), (w_gate, which)],
                         [(shape_of(x.shape, BF16), 1), (shape_of(x.shape, BF16), 1)],
-                        [pltpu.VMEM((tile, w_up.shape[2]), BF16)], 50)
-
-
-def layer_middle(x, m, g, e, d_out, w_up, w_down, w_gate, w_proj, layer, tile=256):
+                        [pltpu.VMEM((tile, w_up.shape[2]), BF16)] + gather_scratch(served) +
+                        [pltpu.VMEM(sent.shape, BF16), pltpu.SemaphoreType.DMA], 60,
+                        [(ids, SMEM_SPEC), (served, ANY_SPEC)], [sent], first_step)
+
+
+def layer_middle(x, m, g, e, d_out, w_up, w_down, w_gate, w_proj, layer, tile=TILE):
     tokens, d = x.shape
     ff = w_up.shape[2]
 
     def body(need, ins, w, outs, rest):
         x_ref, m_ref, g_ref, e_ref, c_ref = ins
-        x2_ref, h_ref, x3_ref, a_ref, dz_ref, row_ref = outs
+        x2_ref, h_ref, x3_ref, a_ref, dz_ref, h3_ref = outs
         act = rest[0]
         need(4, 0)
         z = (g_ref[...].astype(F32) * e_ref[...].astype(F32)).astype(BF16)
@@ -172,42 +292,31 @@
         u = (x_f * rms(x_f)).astype(BF16)
         need(1)
         mlp_up(u, w[0], act, h_ref)
-        for n in range(d // 256):
-            cols = slice(n * 256, (n + 1) * 256)
+        for n in range(d // COLS):
+            cols = slice(n * COLS, (n + 1) * COLS)
             mm = dot_nn(act[...], w[1][:, cols]).astype(BF16)
             x3_ref[:, cols] = (x2_ref[:, cols].astype(F32) + mm.astype(F32)).astype(BF16)
         x_f = x3_ref[...].astype(F32)
         u = (x_f * rms(x_f)).astype(BF16)
-        need(2, 3)
+        need(2, 3, 5)
+        mlp_up(u, w[5], None, h3_ref)
         a = dot_nn(u, w[2][...]).astype(BF16)
         a_ref[...] = a
         gate = gelu(a.astype(F32)).astype(BF16)
         dz = dot_nt(c_ref[...], w[3][...])
         dz_ref[...] = dz
-        store_rows(row_ref, gate.astype(F32) * dz)
+        store_rows(rest[-1], gate.astype(F32) * dz)
 
     vec = (shape_of((tokens, d), BF16), 1)
     return token_kernel(body, tile, tokens, [(x, 1), (m, 1), (g, 1), (e, 1), (d_out, 1)],
-                        [(w_up, layer), (w_down, layer), (w_gate, 1), (w_proj, 1), (w_proj, 0)],
+                        [(w_up, layer), (w_down, layer), (w_gate, 1), (w_proj, 1), (w_proj, 0), (w_up, layer + 1)],
                         [vec, (shape_of((tokens, ff), BF16), 1), vec, vec, (shape_of((tokens, d), F32), 1),
-                         (shape_of((tokens * d // 128, 128), F32), d // 128)],
-                        [pltpu.VMEM((tile, ff), BF16)], 62)
-
-
-def last_up(x, w_up, layer, tile=512):
-    tokens, ff = x.shape[0], w_up.shape[2]
-
-    def body(need, ins, w, outs, rest):
-        need(0)
-        x_f = ins[0][...].astype(F32)
-        u = (x_f * rms(x_f)).astype(BF16)
-        mlp_up(u, w[0], None, outs[0])
-
-    return token_kernel(body, tile, tokens, [(x, 1)], [(w_up, layer)],
-                        [(shape_of((tokens, ff), BF16), 1)], [], 22)[0]
-
-
-def last_down(x, h, a, e, w_down, w_proj, layer, which, tile=256):
+                         (shape_of((tokens, ff), BF16), 1)],
+                        [pltpu.VMEM((tile, ff), BF16)], 90,
+                        mirror=(shape_of((tokens * d // LANES, LANES), F32), d // LANES, 10))
+
+
+def last_down(x, h, a, e, w_down, w_proj, layer, which, tile=TILE):
     tokens, d = x.shape
     ff = h.shape[1]
 
@@ -217,11 +326,11 @@
         need(0, 1)
         gate = gelu(a_ref[...].astype(F32)).astype(BF16)
         z = (gate.astype(F32) * e_ref[...].astype(F32)).astype(BF16)
-        for j in range(ff // 512):
-            cols = slice(j * 512, (j + 1) * 512)
+        for j in range(ff // CHUNK):
+            cols = slice(j * CHUNK, (j + 1) * CHUNK)
             act[:, cols] = gelu(h_ref[:, cols].astype(F32)).astype(BF16)
-        for n in range(d // 256):
-            cols = slice(n * 256, (n + 1) * 256)
+        for n in range(d // COLS):
+            cols = slice(n * COLS, (n + 1) * COLS)
             m = dot_nn(act[...], w[0][:, cols]).astype(BF16)
             q = dot_nn(z, w[1][:, cols]).astype(BF16)
             outs[0][:, cols] = ((x_ref[:, cols].astype(F32) + m.astype(F32)) + q.astype(F32)).astype(BF16)
@@ -232,12 +341,12 @@
 
 
 def back_mlp(c_b, h_ref, w_up, w_down, dh):
-    chunk = 512
+    chunk = CHUNK
     for j in range(h_ref.shape[1] // chunk):
         cols = slice(j * chunk, (j + 1) * chunk)
         d_act = dot_nt(c_b, w_down[cols, :])
         dh[:, cols] = gelu_bwd(h_ref[:, cols].astype(F32), d_act).astype(BF16)
-    return jnp.concatenate([dot_nt(dh[...], w_up[n * 256:(n + 1) * 256, :]) for n in range(w_up.shape[0] // 256)], axis=1)
+    return jnp.concatenate([dot_nt(dh[...], w_up[n * COLS:(n + 1) * COLS, :]) for n in range(w_up.shape[0] // COLS)], axis=1)
 
 
 def back_norm(c_f, x_ref, du):
@@ -246,7 +355,7 @@
     return c_f + (s * du - x_f * (s * s * s) * jnp.mean(x_f * du, axis=-1, keepdims=True))
 
 
-def back_table(c, h, x, a, dz, e, w_up, w_down, w_gate, layer, which, tile=256):
+def back_table(c, h, x, a, dz, e, w_up, w_down, w_gate, layer, which, tile=TILE):
     tokens, d = x.shape
     ff = h.shape[1]
 
@@ -265,7 +374,7 @@
                         [pltpu.VMEM((tile, ff), BF16), pltpu.VMEM((tile, d), F32)], 58)[0]
 
 
-def back_plain(c, h, x, g, w_up, w_down, w_proj, layer, which, tile=256):
+def back_plain(c, h, x, g, w_up, w_down, w_proj, layer, which, tile=TILE):
     tokens, d = x.shape
     ff = h.shape[1]
 
@@ -274,12 +383,12 @@
         need(0, 1, 2)
         du = back_mlp(c_ref[...].astype(BF16), h_ref, w[0], w[1], rest[0])
         c_low = back_norm(c_ref[...], x_ref, du).astype(BF16)
-        store_rows(outs[0], g_ref[...].astype(F32) * dot_nt(c_low, w[2][...]))
+        store_rows(rest[-1], g_ref[...].astype(F32) * dot_nt(c_low, w[2][...]))
 
     return token_kernel(body, tile, tokens, [(c, 1), (h, 1), (x, 1), (g, 1)],
-                        [(w_up, layer), (w_down, layer), (w_proj, which)],
-                        [(shape_of((tokens * d // 128, 128), F32), d // 128)],
-                        [pltpu.VMEM((tile, ff), BF16)], 58)[0]
+                        [(w_up, layer), (w_down, layer), (w_proj, which)], [],
+                        [pltpu.VMEM((tile, ff), BF16)], 58,
+                        mirror=(shape_of((tokens * d // LANES, LANES), F32), d // LANES, 11))
 
 
 def split_rows(tables, place):
@@ -303,76 +412,37 @@
         kernel, out_shape=shape_of((PLANE, n_tab, blk, width), tables.dtype), in_specs=[SMEM_SPEC, ANY_SPEC], out_specs=ANY_SPEC,
         scratch_shapes=[pltpu.VMEM(tables.shape, tables.dtype), pltpu.SemaphoreType.DMA((n_tab,)),
                         pltpu.SemaphoreType.DMA((n_tab * PLANE,))],
-        compiler_params=local_params(), name="split_rows", cost_estimate=cost(4, 2**23))(place, tables)
+        compiler_params=local_params(), name="split_rows", cost_estimate=cost(4))(place, tables)
 
 
 def make_ids(uid, start, count, peak, rnd, blank):
     n_tgt = count.shape[0]
-    rows = -(-SLOTS // 128)
+    rows = -(-SLOTS // LANES)
 
     def kernel(uid_ref, start_ref, count_ref, peak_ref, rnd_ref, out_ref):
-        lane = lax.broadcasted_iota(jnp.int32, (1, 128), 1)
+        lane = lax.broadcasted_iota(jnp.int32, (1, LANES), 1)
         out_ref[...] = jnp.full(out_ref.shape, peak_ref[0], jnp.int32)
         for g in range(n_tgt):
             shift = rnd_ref[0] * SLOTS
             left = jnp.clip(count_ref[g] - shift, 0, SLOTS)
-            at = jnp.minimum(start_ref[g] + shift, (uid_ref.shape[0] - rows - 1) * 128)
-            row, off = at // 128, lax.rem(at, 128)
-            turned = [pltpu.roll(uid_ref[row + i], lax.rem(128 - off, 128), axis=1) for i in range(rows + 1)]
+            at = jnp.minimum(start_ref[g] + shift, (uid_ref.shape[0] - rows - 1) * LANES)
+            row, off = at // LANES, lax.rem(at, LANES)
+            turned = [pltpu.roll(uid_ref[row + i], lax.rem(LANES - off, LANES), axis=1) for i in range(rows + 1)]
             for i in range(rows):
-                ids = jnp.where(lane < 128 - off, turned[i], turned[i + 1])
-                out_ref[g, i:i + 1, :] = jnp.where(i * 128 + lane < left, ids, blank)
+                ids = jnp.where(lane < LANES - off, turned[i], turned[i + 1])
+                out_ref[g, i:i + 1, :] = jnp.where(i * LANES + lane < left, ids, blank)
 
     return pl.pallas_call(
-        kernel, out_shape=shape_of((n_tgt, IDW // 128, 128), jnp.int32),
+        kernel, out_shape=shape_of((n_tgt, IDW // LANES, LANES), jnp.int32),
         in_specs=[VMEM_SPEC] + [SMEM_SPEC] * 4, out_specs=VMEM_SPEC, compiler_params=local_params(), name="make_ids",
-        cost_estimate=cost(3, 2**18),
+        cost_estimate=cost(3),
     )(uid, start, count, peak, jnp.reshape(rnd, (1,)).astype(jnp.int32))
-
-
-def pair_at(index):
-    return pl.ds(pl.multiple_of(index, 2), 2)
-
-
-def owner_gather(ids, served, which, n_src):
-    blk, width = served.shape[2:]
-    rows = PLANE * blk
-    pieces = width // 128
-
-    def kernel(ids_ref, served_ref, out_ref, native, flat, isem):
-        reads = [pltpu.make_async_copy(served_ref.at[b, which], native.at[b], isem.at[b]) for b in range(PLANE)]
-        for c in reads:
-            c.start()
-        for b in range(PLANE):
-            reads[b].wait()
-            for c in range(pieces):
-                flat[pl.ds(b * blk * pieces + c, blk, stride=pieces), :] = native[b, :, c * 128:(c + 1) * 128].astype(F32)
-
-        def src(s, c):
-            def part(b, c):
-                for j in range(UNROLL):
-                    r = b * UNROLL + j
-                    out_ref[s * SLOTS + r] = flat[pair_at(ids_ref[s * IDW + r]), :].astype(BF16)
-                return c
-
-            lax.fori_loop(0, SLOTS // UNROLL, part, 0)
-            return c
-
-        lax.fori_loop(0, n_src, src, 0)
-
-    return pl.pallas_call(
-        kernel, out_shape=shape_of((n_src * SLOTS, pieces, 128), BF16),
-        in_specs=[SMEM_SPEC, ANY_SPEC], out_specs=VMEM_SPEC,
-        scratch_shapes=[pltpu.VMEM((PLANE, blk, width), BF16), pltpu.VMEM((rows * pieces + 8, 128), F32),
-                        pltpu.SemaphoreType.DMA((PLANE,))],
-        compiler_params=local_params(), name="owner_gather", cost_estimate=cost(14, 2**22),
-    )(ids, served)
 
 
 def unpack_rows(idx, rec_own, rec_pair, heads):
     n = idx.shape[0]
     half, pieces = rec_own.shape[0], rec_own.shape[1]
-    tokens, tile = n // heads, 256
+    tokens, tile = n // heads, TILE
     per = heads * pieces
 
     def kernel(idx_ref, own_ref, pair_ref, out_ref, rec, stage, sem):
@@ -392,16 +462,16 @@
 
             lax.fori_loop(0, tile * heads // UNROLL, blk, 0)
             for c in range(per):
-                out_ref[pl.ds(i * tile, tile), c * 128:(c + 1) * 128] = stage[pl.ds(c, tile, stride=per), :].astype(BF16)
+                out_ref[pl.ds(i * tile, tile), c * LANES:(c + 1) * LANES] = stage[pl.ds(c, tile, stride=per), :].astype(BF16)
             return c
 
         lax.fori_loop(0, tokens // tile, part, 0)
 
     return pl.pallas_call(
-        kernel, out_shape=shape_of((tokens, per * 128), BF16),
+        kernel, out_shape=shape_of((tokens, per * LANES), BF16),
         in_specs=[SMEM_SPEC, ANY_SPEC, ANY_SPEC], out_specs=VMEM_SPEC,
-        scratch_shapes=[pltpu.VMEM((2 * half, pieces, 128), BF16), pltpu.VMEM((tile * per, 128), F32), pltpu.SemaphoreType.DMA((2,))],
-        compiler_params=local_params(), name="unpack_rows", cost_estimate=cost(16, 2**23),
+        scratch_shapes=[pltpu.VMEM((2 * half, pieces, LANES), BF16), pltpu.VMEM((tile * per, LANES), F32), pltpu.SemaphoreType.DMA((2,))],
+        compiler_params=local_params(), name="unpack_rows", cost_estimate=cost(16),
     )(idx, rec_own, rec_pair)
 
 
@@ -422,20 +492,20 @@
             for j in range(UNROLL):
                 p = pos_ref[b * UNROLL + j]
                 row = g_ref[pair_at(p & low), :]
-                acc = row + jnp.where(jnp.full((2, 128), p, jnp.int32) < 0, acc, 0.0)
+                acc = row + jnp.where(jnp.full((2, LANES), p, jnp.int32) < 0, acc, 0.0)
                 stage[pair_at(dst_ref[b * UNROLL + j]), :] = acc
             return acc
 
-        lax.fori_loop(0, (size_ref[0] + UNROLL - 1) // UNROLL, blk, jnp.zeros((2, 128), F32))
+        lax.fori_loop(0, (size_ref[0] + UNROLL - 1) // UNROLL, blk, jnp.zeros((2, LANES), F32))
         done = pltpu.make_async_copy(stage.at[pl.ds(0, n_row)], out_ref, sem.at[0])
         done.start()
         done.wait()
 
     return pl.pallas_call(
-        kernel, out_shape=shape_of((n_row, 128), F32),
+        kernel, out_shape=shape_of((n_row, LANES), F32),
         in_specs=[SMEM_SPEC, SMEM_SPEC, SMEM_SPEC, ANY_SPEC, ANY_SPEC], out_specs=ANY_SPEC,
-        scratch_shapes=[pltpu.VMEM((2 * n, 128), F32), pltpu.VMEM((n_row + 8, 128), F32), pltpu.SemaphoreType.DMA((2,))],
-        compiler_params=local_params(), name="pack_rows", cost_estimate=cost(26, 2**24),
+        scratch_shapes=[pltpu.VMEM((2 * n, LANES), F32), pltpu.VMEM((n_row + 8, LANES), F32), pltpu.SemaphoreType.DMA((2,))],
+        compiler_params=local_params(), name="pack_rows", cost_estimate=cost(26),
     )(pos, dst, size, grad_own, grad_pair)
 
 
@@ -453,10 +523,10 @@
             c.start()
 
         def zero(i, c):
-            acc[pl.ds(i * 128, 128), :] = jnp.zeros((128, 128), F32)
+            acc[pl.ds(i * LANES, LANES), :] = jnp.zeros((LANES, LANES), F32)
             return c
 
-        lax.fori_loop(0, 2 * rows // 128, zero, 0)
+        lax.fori_loop(0, 2 * rows // LANES, zero, 0)
         for c in reads:
             c.wait()
 
@@ -482,18 +552,18 @@
             c.wait()
 
     return pl.pallas_call(
-        kernel, out_shape=[shape_of((blk_rows, 128), F32)] * PLANE, in_specs=[SMEM_SPEC, SMEM_SPEC, ANY_SPEC],
+        kernel, out_shape=[shape_of((blk_rows, LANES), F32)] * PLANE, in_specs=[SMEM_SPEC, SMEM_SPEC, ANY_SPEC],
         out_specs=[ANY_SPEC] * PLANE,
-        scratch_shapes=[pltpu.VMEM((2 * rows + 8, 128), F32), pltpu.VMEM((n_src * 2 * SLOTS, 128), F32),
+        scratch_shapes=[pltpu.VMEM((2 * rows + 8, LANES), F32), pltpu.VMEM((n_src * 2 * SLOTS, LANES), F32),
                         pltpu.SemaphoreType.DMA((n_src,)), pltpu.SemaphoreType.DMA((PLANE,))],
-        compiler_params=local_params(), name="owner_scatter", cost_estimate=cost(20, 2**24),
+        compiler_params=local_params(), name="owner_scatter", cost_estimate=cost(20),
     )(ids, place, rec)
 
 
 def finish_table(blocks, grads, which, n_tab):
     blk_rows = blocks[0].shape[0]
     blk = blk_rows // 2
-    shape = (n_tab, PLANE * blk, 256)
+    shape = (n_tab, PLANE * blk, COLS)
     first = grads is None
 
     def kernel(*refs):
@@ -505,7 +575,7 @@
         for b in range(PLANE):
             reads[b].wait()
             for c in range(2):
-                stage[b, :, c * 128:(c + 1) * 128] = buf[b, pl.ds(c, blk, stride=2), :]
+                stage[b, :, c * LANES:(c + 1) * LANES] = buf[b, pl.ds(c, blk, stride=2), :]
             writes.append(pltpu.make_async_copy(stage.at[b], out.at[which, pl.ds(b * blk, blk)], osem.at[b]))
             writes[-1].start()
         for c in writes:
@@ -514,10 +584,10 @@
     args = list(blocks) + ([] if first else [grads])
     return pl.pallas_call(
         kernel, out_shape=shape_of(shape, F32), in_specs=[ANY_SPEC] * len(args), out_specs=ANY_SPEC,
-        scratch_shapes=[pltpu.VMEM((PLANE, blk_rows, 128), F32), pltpu.VMEM((PLANE, blk, 256), F32),
+        scratch_shapes=[pltpu.VMEM((PLANE, blk_rows, LANES), F32), pltpu.VMEM((PLANE, blk, COLS), F32),
                         pltpu.SemaphoreType.DMA((PLANE,)), pltpu.SemaphoreType.DMA((PLANE,))],
         input_output_aliases={} if first else {PLANE: 0},
-        compiler_params=local_params(), name="finish_table", cost_estimate=cost(8, 2**23))(*args)
+        compiler_params=local_params(), name="finish_table", cost_estimate=cost(8))(*args)
 
 
 def swap_cores(x, n_dev):
@@ -550,7 +620,7 @@
     return pl.pallas_call(
         kernel, out_shape=shape_of(blocks.shape, blocks.dtype), in_specs=[ANY_SPEC], out_specs=ANY_SPEC,
         scratch_shapes=[pltpu.SemaphoreType.DMA((n_chip,)), pltpu.SemaphoreType.DMA((n_chip,)), pltpu.SemaphoreType.DMA],
-        compiler_params=remote_params(cid), name="chip_exchange", cost_estimate=cost(100, 2**23))(blocks)
+        compiler_params=remote_params(cid), name="chip_exchange", cost_estimate=cost(100))(blocks)
 
 
 def plane_trade(x, n_dev):
@@ -582,7 +652,7 @@
     got = pl.pallas_call(
         kernel, out_shape=[shape] * (PLANE - 1), in_specs=[ANY_SPEC] * (PLANE - 1), out_specs=[ANY_SPEC] * (PLANE - 1),
         scratch_shapes=[pltpu.SemaphoreType.DMA((PLANE,)), pltpu.SemaphoreType.DMA((PLANE,))],
-        compiler_params=remote_params(cid), name="place_exchange", cost_estimate=cost(50, 2**22))(*blocks[1:])
+        compiler_params=remote_params(cid), name="place_exchange", cost_estimate=cost(50))(*blocks[1:])
     return [blocks[0]] + list(got)
 
 
@@ -590,15 +660,19 @@
     return lax.optimization_barrier((x,) + deps)[0]
 
 
-def route_plan(ids_pair, n_own, rows_dev, n_dev, me):
+def sort_requests(ids_pair, rows_dev, n_dev):
     n = ids_pair.shape[0]
     n_chip = n_dev // 2
     blk = rows_dev // PLANE
     owner, local = ids_pair // rows_dev, lax.rem(ids_pair, rows_dev)
     server = owner ^ (local // blk)
     name = (lax.rem(server, 2) * n_chip + server // 2) * rows_dev + lax.rem(owner, PLANE) * blk + lax.rem(local, blk)
-    lane = jnp.arange(n, dtype=jnp.int32)
-    key = lax.sort(name * n + lane)
+    return lax.sort(name * n + jnp.arange(n, dtype=jnp.int32))
+
+
+def route_plan(key, n_own, rows_dev, n_dev, me):
+    n = key.shape[0]
+    n_chip = n_dev // 2
     sid, pos = key // n, lax.rem(key, n)
     n_low = jnp.sum((sid < n_chip * rows_dev).astype(jnp.int32))
     first = sid != jnp.concatenate([jnp.full((1,), -1, jnp.int32), sid[:-1]])
@@ -618,10 +692,9 @@
     mine = lax.dynamic_slice(both, (0, begin), (2, n + UNROLL))
     valid = jnp.arange(n + UNROLL, dtype=jnp.int32) < size
     most = jnp.iinfo(jnp.int32).max
-    uid = lax.sort(jnp.where(first & (sid // (n_chip * rows_dev) == core), sid, most))
-    uid = jnp.concatenate([2 * lax.rem(uid, rows_dev), jnp.zeros((512,), jnp.int32)]).reshape((n + 512) // 128, 1, 128)
+    distinct = jnp.where(first & (sid // (n_chip * rows_dev) == core), sid, most)
     start = lax.dynamic_slice(start, (core * n_chip,), (n_chip,))
-    return dict(pos=jnp.where(valid, mine[0], 0), code=jnp.where(valid, mine[1], -1), uid=uid, start=start - start[0],
+    return dict(pos=jnp.where(valid, mine[0], 0), code=jnp.where(valid, mine[1], -1), distinct=distinct, start=start - start[0],
                 size=size.reshape(1), by_pos=jnp.where(pos < n_own, pos * (n_dev * 2 * rows_dev) + code, most),
                 count=lax.dynamic_slice(count, (core * n_chip,), (n_chip,)), peak=jnp.max(count).reshape(1))
 
@@ -642,7 +715,7 @@
         n_tab, n_tok, n_heads = token_ids.shape
         rows_dev, row_width = tables.shape[1], tables.shape[2]
         n_req = n_tok * n_heads
-        tail = (row_width // 128, 128)
+        tail = (row_width // LANES, LANES)
         me = lax.axis_index('emb')
         core = lax.rem(me, 2)
 
@@ -651,10 +724,15 @@
         place = lax.rem(me, PLANE).reshape(1)
         split = split_rows(tables, place)
         served = plane_trade(split, n_dev)
-        plans = [route_plan(after(ids_pair, split)[t], n_req, rows_dev, n_dev, me) for t in range(n_tab)]
-
+        keys = [sort_requests(after(ids_pair, split)[t], rows_dev, n_dev) for t in range(n_tab)]
+
+        plans = [route_plan(keys[t], n_req, rows_dev, n_dev, me) for t in range(n_tab)]
+        distinct = lax.sort(jnp.stack([plan['distinct'] for plan in plans]), dimension=1)
+        x1 = layer_plain(after(x_start, *[plan['distinct'] for plan in plans]), w_up, w_down, 0)
+        margin = jnp.zeros((n_tab, CHUNK), jnp.int32)
+        distinct = jnp.concatenate([2 * lax.rem(distinct, rows_dev), margin], axis=1).reshape(n_tab, -1, 1, LANES)
         span = 2 * rows_dev
-        in_order = lax.sort(jnp.stack([plan['by_pos'] for plan in plans]), dimension=1)
+        in_order = lax.sort(after(jnp.stack([plan['by_pos'] for plan in plans]), distinct), dimension=1)
         code_own = lax.rem(in_order[:, :n_req], n_dev * span)
 
         def half_slot(plan, rnd, width, trash):
@@ -664,13 +742,13 @@
 
         def id_blocks(which, rnd):
             plan = plans[which]
-            return make_ids(plan['uid'], plan['start'], plan['count'], plan['peak'], rnd, 2 * rows_dev)
+            return make_ids(distinct[which], plan['start'], plan['count'], plan['peak'], rnd, 2 * rows_dev)
 
         blocks = jnp.stack([id_blocks(t, jnp.int32(0)) for t in range(n_tab)], axis=1)
-        got = chip_trade(after(blocks, served), n_dev)
+        blocks = blocks.reshape(n_chip, n_tab * IDW // LANES, LANES)
+        got = chip_exchange(after(blocks, served, x1), 9, n_chip).reshape(n_chip, n_tab, IDW)
         first_ids = [got[:, t].reshape(n_chip * IDW) for t in range(n_tab)]
-        got = got.reshape(n_chip, n_tab, IDW)
-        rounds = (jnp.max(got[:, :, IDW - 1], axis=0) + SLOTS - 1) // SLOTS
+        rounds = [(jnp.max(got[:, t, IDW - 1]) + SLOTS - 1) // SLOTS for t in range(n_tab)]
 
         def more_ids(which, rnd, cid):
             return chip_exchange(id_blocks(which, rnd), cid, n_chip).reshape(n_chip * IDW)
@@ -698,42 +776,34 @@
             dst = 2 * half_slot(plan, rnd, SLOTS, n_chip * SLOTS)
             return pack_rows(plan['pos'], dst, plan['size'], grad_own, grad_pair, n_chip)
 
-        def pair_rows(grad_rows):
-            return grad_rows, swap_cores(grad_rows, n_dev)
-
         def return_rest(which, first, pair):
             def more(state):
                 rnd, total = state
                 ids = more_ids(which, rnd, 4 + which)
-                rec = chip_exchange(packed(which, rnd, *pair).reshape(n_chip, 2 * SLOTS, 128), 6 + which, n_chip)
-                new = owner_scatter(ids, rec.reshape(n_chip * 2 * SLOTS, 128), rows_dev, place)
+                rec = chip_exchange(packed(which, rnd, *pair).reshape(n_chip, 2 * SLOTS, LANES), 6 + which, n_chip)
+                new = owner_scatter(ids, rec.reshape(n_chip * 2 * SLOTS, LANES), rows_dev, place)
                 return rnd + 1, [p + q for p, q in zip(total, new)]
 
             return lax.while_loop(lambda s: s[0] < rounds[which], more, (jnp.int32(1), list(first)))[1]
 
-        x1 = layer_plain(x_start, w_up, w_down, 0)
-        sent0 = owner_gather(after(first_ids[0], x1), served, 0, n_chip)
+        sent0 = owner_gather(first_ids[0], served, 0, n_chip)
         fetched0 = chip_trade(sent0, n_dev)
-        sent1 = owner_gather(after(first_ids[1], sent0), served, 1, n_chip)
-        fetched1 = chip_trade(sent1, n_dev)
-        m1, g1 = layer_table_head(after(x1, sent1), w_up, w_down, w_gate, 1, 0)
+        m1, g1, sent1 = layer_table_head(after(x1, sent0), w_up, w_down, w_gate, 1, 0, first_ids[1], served, n_chip)
         e1 = fetch_rest(0, unpack(0, 0, fetched0))
-        x2, h2, x3, a3, dz3, rows3 = layer_middle(x1, m1, g1, e1, d_out, w_up, w_down, w_gate, w_proj, 2)
-        pair1 = pair_rows(rows3)
-        h3 = last_up(x3, w_up, 3)
+        fetched1 = chip_trade(after(sent1, e1), n_dev)
+        x2, h2, x3, a3, dz3, h3, *pair1 = layer_middle(x1, m1, g1, e1, d_out, w_up, w_down, w_gate, w_proj, 2)
         sent1 = packed(1, 0, *pair1)
-        returned1 = chip_trade(sent1, n_dev)
+        returned1 = chip_trade(after(sent1, fetched1), n_dev)
         e3 = unpack(1, 0, after(fetched1, sent1))
         e3 = fetch_rest(1, e3)
         c2 = back_table(after(d_out, sent1), h3, x3, a3, dz3, e3, w_up, w_down, w_gate, 3, 1)
-        rows1 = back_plain(c2, h2, x2, g1, w_up, w_down, w_proj, 2, 0)
-        pair0 = pair_rows(rows1)
-        total1 = owner_scatter(first_ids[1], after(returned1, rows1), rows_dev, place)
+        pair0 = back_plain(c2, h2, x2, g1, w_up, w_down, w_proj, 2, 0)
+        sent0 = packed(0, 0, *pair0)
+        returned0 = chip_trade(after(sent0, returned1), n_dev)
+        total1 = owner_scatter(first_ids[1], after(returned1, sent0), rows_dev, place)
         total1 = return_rest(1, total1, pair1)
         placed1 = place_trade(total1, n_dev)
-        sent0 = packed(0, 0, pair0[0], after(pair0[1], total1[0]))
-        returned0 = chip_trade(sent0, n_dev)
-        x_end = last_down(after(x3, sent0), h3, a3, e3, w_down, w_proj, 3, 1)
+        x_end = last_down(after(x3, *total1), h3, a3, e3, w_down, w_proj, 3, 1)
         grads = finish_table([after(p, x_end) for p in placed1], None, 1, n_tab)
         total0 = owner_scatter(first_ids[0], after(returned0, x_end), rows_dev, place)
         total0 = return_rest(0, total0, pair0)

time: 865 us -> 827 us (0.956)
  the two profiles are of different devices: /device:TPU:25 before, /device:TPU:21 now
where the time goes in v2:
time: 827 us; the launch traced here: 819 us
  Pallas kernels  568 us (69%)
  waiting for transfers between devices  88.2 us (11%)
  local copies, waits for them, and re-layouts  56.5 us (7%)
  starting transfers between devices  39.9 us (5%)
  other arithmetic  36.3 us (4%)
  between operations  20.2 us (2%)
  loops' own time  9.36 us (1%)
    pallas_call x6, Pallas kernels, token_kernel(): pl.pallas_call(kernel, grid=(tokens // tile,), out_shape=[s for s, _ in o...  361 us
    ppermute x7, waiting for transfers between devices, place_trade(): lax.ppermute(blocks[b], 'emb', [(i, i ^ b) for i in range(n_dev)])  66.8 us
    pallas_call x2, Pallas kernels, pack_rows(): pl.pallas_call(kernel, out_shape=shape_of((n_row, LANES), F32), in_specs=...  53.6 us
    pallas_call x1, Pallas kernels, place_exchange(): pl.pallas_call(kernel, out_shape=[shape] * (PLANE - 1), in_specs=[ANY_SPE...  52.2 us
    sort x2, local copies, waits for them, and re-layouts, step(): lax.sort(after(jnp.stack([plan['by_pos'] for plan in plans]), distinct),...  44.2 us
    pallas_call x2, Pallas kernels, unpack_rows(): pl.pallas_call(kernel, out_shape=shape_of((tokens, per * LANES), BF16), i...  34.2 us
    pallas_call x2, Pallas kernels, owner_scatter(): pl.pallas_call(kernel, out_shape=[shape_of((blk_rows, LANES), F32)] * PLA...  31.6 us
    all_to_all x4, starting transfers between devices, chip_trade(): return lax.all_to_all(x, 'emb', 0, 0, axis_index_groups=groups, tiled=True)  26.5 us
  transfers between devices with their start and end apart: 15, of which 6 were waited for; matrix products, arithmetic and copies ran while one was open for 5% of the time, Pallas kernels for 54%

profile of v2, /device:TPU:21, one launch (start us, length us, event | category | flops | bytes accessed | tf_op | source)
XLA Modules:
  0.0 818.7 jit_solution(13848939238974486275)
XLA Ops:
  20.0 7.7 sort.42
  30.0 8.1 sort.43
  49.3 45.7 %shard_map.95.refs_0_ = bf16[2048,1024]{1,0:T(8,128)(2,1)} custom-call(bf16[2048,1024]{1,0:T(8,128)(2,1)} %refs_0_, bf16[4,1024,4096]{2,1,0:T(8,128)(2,1)} %refs_4_.6, bf16[4,4096,1024]{2,1,0:T(8,128)(2,1)} %refs_4_.7), custom_call_target="tpu_custom_call" | custom-call | flops 39600001024 | bytes 8388608 | tf_op jit(solution)/shard_map/pallas_call | solution.py:206
  115.0 12.7 %owner_gather.11 = bf16[5376,2,128]{2,1,0:T(2,128)(2,1)} custom-call(s32[16384]{0:T(1024)} %bitcast.160, bf16[8,2,512,256]{3,2,1,0:T(8,128)(2,1)} %all-to-all-done.served_ref.refs_2_), custom_call_target="tpu_custom_call" | custom-call | flops 12600000512 | bytes 8388608 | tf_op jit(solution)/shard_map/owner_gather/pallas_call | solution.py:80
  137.5 44.1 %sort.49.cloned.1.call-done = s32[2,16384]{1,0:T(2,128)} async-done(((s32[2,16384]{1,0:T(2,128)}), s32[2,16384]{1,0:T(2,128)}) %sort.49.cloned.1.call-update) | async-done | bytes 131088 | tf_op jit(solution)/shard_map/sort | solution.py:735
  186.0 8.5 %all-to-all-done.1.own_ref = bf16[5376,2,128]{2,1,0:T(2,128)(2,1)} async-done(((bf16[5376,2,128]{2,1,0:T(2,128)(2,1)}), bf16[5376,2,128]{2,1,0:T(2,128)(2,1)}, u32[]{:S(2)}, u32[]{:S(2)}) %all-to-all-start.1) | async-done | bytes 2752544 | tf_op jit(solution)/shard_map/all_to_all | solution.py:599
  195.9 63.1 %shard_map.96 = (bf16[2048,1024]{1,0:T(8,128)(2,1)}, bf16[2048,1024]{1,0:T(8,128)(2,1)}, bf16[5376,2,128]{2,1,0:T(2,128)(2,1)}) custom-call(bf16[2048,1024]{1,0:T(8,128)(2,1)} %shard_map.95.refs_0_, s32[16384]{0:T(1024)} %bitcast.162, bf16[8,2,512,256]{3,2,1,0:T(8,128)(2,1)} %all-to-all-done.served_ref.refs_2_, bf16[4,1024,4096]{2,1,0:T(8,128)(2,1)} %refs_4_.6, ...), custom_call_target="tpu_custom_call" | custom-call | flops 54000001024 | bytes 8388608 | tf_op jit(solution)/shard_map/pallas_call | solution.py:206
  259.0 17.0 %unpack_rows.12 = bf16[2048,1024]{1,0:T(8,128)(2,1)} custom-call(s32[8192]{0:T(1024)} %get-tuple-element.1203.idx_ref, bf16[5376,2,128]{2,1,0:T(2,128)(2,1)} %all-to-all-done.1.own_ref, bf16[5376,2,128]{2,1,0:T(2,128)(2,1)} %collective-permute-done.3.pair_ref), custom_call_target="tpu_custom_call" | custom-call | flops 14400000000 | bytes 8388608 | tf_op jit(solution)/shard_map/unpack_rows/pallas_call | solution.py:470
  282.9 94.3 %shard_map.97 = (bf16[2048,1024]{1,0:T(8,128)(2,1)}, bf16[2048,4096]{1,0:T(8,128)(2,1)}, bf16[2048,1024]{1,0:T(8,128)(2,1)}, bf16[2048,1024]{1,0:T(8,128)(2,1)},...) custom-call(bf16[2048,1024]{1,0:T(8,128)(2,1)} %shard_map.95.refs_0_, ...), custom_call_target="tpu_custom_call" | custom-call | flops 80999997440 | bytes 8388608 | tf_op jit(solution)/shard_map/pallas_call | solution.py:206
  377.3 26.9 %pack_rows.10 = f32[10752,128]{1,0:T(8,128)} custom-call(s32[16400]{0:T(1024)S(1)} %copy-done.65, s32[16400]{0:T(1024)} %fusion.45.dst_ref, s32[1]{0:T(128)} %bitcast.47.size_ref, f32[16384,128]{1,0:T(8,128)} %get-tuple-element.1754.own_ref, f32[16384,128]{1,0:T(8,128)} %get-tuple-element.1755.pair_ref), custom_call_target="tpu_custom_call" | custom-call | flops 23399999488 | bytes 8388608 | tf_op jit(solution)/shard_map/pack_rows/pallas_call | solution.py:504
  417.0 17.1 %unpack_rows.13 = bf16[2048,1024]{1,0:T(8,128)(2,1)} custom-call(s32[8192]{0:T(1024)} %get-tuple-element.1200.idx_ref, bf16[5376,2,128]{2,1,0:T(2,128)(2,1)} %all-to-all-done.2.own_ref, bf16[5376,2,128]{2,1,0:T(2,128)(2,1)} %collective-permute-done.4.pair_ref), custom_call_target="tpu_custom_call" | custom-call | flops 14400000000 | bytes 8388608 | tf_op jit(solution)/shard_map/unpack_rows/pallas_call | solution.py:470
  434.1 8.7 %while.79 = (s32[]{:T(128)}, bf16[2048,1024]{1,0:T(8,128)(2,1)}, s32[]{:T(128)}, s32[2,8192]{1,0:T(2,128)}, s32[8192]{0:T(1024)}, /*index=5*/pred[]{:T(512)}, s3...) while((s32[]{:T(128)}, bf16[2048,1024]{1,0:T(8,128)(2,1)}, ...), condition=%wide.region_21.22_spmd, body=%wide.region_20.21_spmd.sunk | while | flops 209702420480 | bytes 75026712 | solution.py:772
  442.8 60.7 %shard_map.98.refs_0_ = f32[2048,1024]{1,0:T(8,128)} custom-call(bf16[2048,1024]{1,0:T(8,128)(2,1)} %refs_0_.1, bf16[2048,4096]{1,0:T(8,128)(2,1)} %get-tuple-element.962.refs_1_, bf16[2048,1024]{1,0:T(8,128)(2,1)} %get-tuple-element.988.refs_2_.refs_0_, bf16[2048,1024]{1,0:T(8,128)(2,1)} %get-tuple-element.963.refs_3_.refs_2_, ...), custom_call_target="tpu_custom_call" | custom-call | flops 52200001536 | bytes 8388608 | tf_op jit(solution)/shard_map/pallas_call | solution.py:206
  503.5 59.4 %shard_map.99 = (f32[16384,128]{1,0:T(8,128)}, f32[16384,128]{1,0:T(8,128)}) custom-call(f32[2048,1024]{1,0:T(8,128)} %shard_map.98.refs_0_, bf16[2048,4096]{1,0:T(8,128)(2,1)} %get-tuple-element.967.refs_1_, bf16[2048,1024]{1,0:T(8,128)(2,1)} %get-tuple-element.968.refs_2_, bf16[2048,1024]{1,0:T(8,128)(2,1)} %get-tuple-element.952.refs_2_.refs_3_, ...), custom_call_target="tpu_custom_call" | custom-call | flops 52200001536 | bytes 8388608 | tf_op jit(solution)/shard_map/pallas_call | solution.py:206
  563.0 26.7 %pack_rows.11 = f32[10752,128]{1,0:T(8,128)} custom-call(s32[16400]{0:T(1024)S(1)} %copy-done.63, s32[16400]{0:T(1024)} %fusion.49.dst_ref, s32[1]{0:T(128)} %bitcast.52.size_ref, f32[16384,128]{1,0:T(8,128)} %get-tuple-element.1823.own_ref, f32[16384,128]{1,0:T(8,128)} %get-tuple-element.1824.pair_ref), custom_call_target="tpu_custom_call" | custom-call | flops 23399999488 | bytes 8388608 | tf_op jit(solution)/shard_map/pack_rows/pallas_call | solution.py:504
  589.7 15.7 %owner_scatter.10 = (f32[1024,128]{1,0:T(8,128)}, f32[1024,128]{1,0:T(8,128)}, f32[1024,128]{1,0:T(8,128)}, f32[1024,128]{1,0:T(8,128)}, f32[1024,128]{1,0:T(8,1...) custom-call(s32[16384]{0:T(1024)} %bitcast.163, s32[1]{0:T(128)} %bitcast.22.place_ref, ...), custom_call_target="tpu_custom_call" | custom-call | flops 17999998976 | bytes 8388608 | tf_op jit(solution)/shard_map/owner_scatter/pallas_call | solution.py:554
  617.4 28.5 %collective-permute-done.6.refs_2_ = f32[1024,128]{1,0:T(8,128)S(1)} collective-permute-done((f32[1024,128]{1,0:T(8,128)}, f32[1024,128]{1,0:T(8,128)S(1)}, u32[]{:S(2)}, u32[]{:S(2)}) %collective-permute-start.6) | collective-permute-done | bytes 524320 | tf_op jit(solution)/shard_map/ppermute | solution.py:632
  647.7 37.9 %shard_map.100 = bf16[2048,1024]{1,0:T(8,128)(2,1)} custom-call(bf16[2048,1024]{1,0:T(8,128)(2,1)} %get-tuple-element.988.refs_2_.refs_0_, bf16[2048,4096]{1,0:T(8,128)(2,1)} %get-tuple-element.962.refs_1_, bf16[2048,1024]{1,0:T(8,128)(2,1)} %get-tuple-element.963.refs_3_.refs_2_, bf16[2048,1024]{1,0:T(8,128)(2,1)} %get-tuple-element.966.refs_5_.refs_3_, ...), custom_call_target="tpu_custom_call" | custom-call | flops 27000000512 | bytes 8388608 | tf_op jit(solution)/shard_map/pallas_call | solution.py:206
  685.7 17.6 %collective-permute-done.9.refs_5_ = f32[1024,128]{1,0:T(8,128)} collective-permute-done((f32[1024,128]{1,0:T(8,128)}, f32[1024,128]{1,0:T(8,128)}, u32[]{:S(2)}, u32[]{:S(2)}) %collective-permute-start.9) | collective-permute-done | bytes 524320 | tf_op jit(solution)/shard_map/ppermute | solution.py:632
  703.3 9.4 %collective-permute-done.10.refs_6_ = f32[1024,128]{1,0:T(8,128)} collective-permute-done((f32[1024,128]{1,0:T(8,128)}, f32[1024,128]{1,0:T(8,128)}, u32[]{:S(2)}, u32[]{:S(2)}) %collective-permute-start.10) | collective-permute-done | bytes 524320 | tf_op jit(solution)/shard_map/ppermute | solution.py:632
  712.7 11.2 %collective-permute-done.11.refs_7_ = f32[1024,128]{1,0:T(8,128)} collective-permute-done((f32[1024,128]{1,0:T(8,128)}, f32[1024,128]{1,0:T(8,128)}, u32[]{:S(2)}, u32[]{:S(2)}) %collective-permute-start.11) | collective-permute-done | bytes 524320 | tf_op jit(solution)/shard_map/ppermute | solution.py:632
  727.2 12.9 %all-to-all-done.4 = f32[16,672,128]{2,1,0:T(8,128)} async-done(((f32[16,672,128]{2,1,0:T(8,128)}), f32[16,672,128]{2,1,0:T(8,128)}, u32[]{:S(2)}, u32[]{:S(2)}) %all-to-all-start.4) | async-done | bytes 5505056 | tf_op jit(solution)/shard_map/all_to_all | solution.py:599
  740.1 15.9 %owner_scatter.11 = (f32[1024,128]{1,0:T(8,128)}, f32[1024,128]{1,0:T(8,128)}, f32[1024,128]{1,0:T(8,128)}, f32[1024,128]{1,0:T(8,128)}, f32[1024,128]{1,0:T(8,1...) custom-call(s32[16384]{0:T(1024)} %bitcast.161, s32[1]{0:T(128)} %bitcast.22.place_ref, ...), custom_call_target="tpu_custom_call" | custom-call | flops 17999998976 | bytes 8388608 | tf_op jit(solution)/shard_map/owner_scatter/pallas_call | solution.py:554
  756.1 52.2 %place_exchange.1 = (f32[1024,128]{1,0:T(8,128)}, f32[1024,128]{1,0:T(8,128)}, f32[1024,128]{1,0:T(8,128)}, f32[1024,128]{1,0:T(8,128)}, f32[1024,128]{1,0:T(8,1...) custom-call(f32[1024,128]{1,0:T(8,128)} %get-tuple-element.1000.refs_0_, f32[1024,128]{1,0:T(8,128)} %get-tuple-element.1001.refs_1_, ...), custom_call_target="tpu_custom_call" | custom-call | flops 44999999488 | bytes 8388608 | tf_op jit(solution)/shard_map/place_exchange/pallas_call | solution.py:652
  (153 shorter events, 96.1 us)
Async XLA Ops:
  10.3 9.3 %collective-permute-start.2 = (s32[2,8192]{1,0:T(2,128)S(1)}, s32[2,8192]{1,0:T(2,128)S(1)}, u32[]{:S(2)}, u32[]{:S(2)}) collective-permute-start(s32[2,8192]{1,0:T(2,128)S(1)} %reshape.160), channel_id=1, source_target_pairs={{0,1},{1,0},{2,3},{3,2},{4,5},{5,4},{6,7},{7,6},{8,9},{9,8},{10,11... | collective-permute-start | bytes 196616 | tf_op jit(solution)/shard_map/ppermute | solution.py:594
  14.8 90.7 %all-to-all-start = ((bf16[8,2,512,256]{3,2,1,0:T(8,128)(2,1)}), bf16[8,2,512,256]{3,2,1,0:T(8,128)(2,1)}, u32[]{:S(2)}, u32[]{:S(2)}) async-start(bf16[8,2,512,256]{3,2,1,0:T(8,128)(2,1)} %split_rows.1), calls=%async_computation | async-start | bytes 8388608 | tf_op jit(solution)/shard_map/all_to_all | solution.py:628
  19.5 78.1 %sort.47.cloned.1.call-start = ((), (), s32[]{:S(2)}) async-start(), calls=%async_computation.5 | async-start | bytes 393248 | tf_op jit(solution)/shard_map/sort | solution.py:730
  127.7 66.8 %all-to-all-start.1 = ((bf16[5376,2,128]{2,1,0:T(2,128)(2,1)}), bf16[5376,2,128]{2,1,0:T(2,128)(2,1)}, u32[]{:S(2)}, u32[]{:S(2)}) async-start(bf16[5376,2,128]{2,1,0:T(2,128)(2,1)} %owner_gather.11), calls=%async_computation.1 | async-start | bytes 5505024 | tf_op jit(solution)/shard_map/all_to_all | solution.py:599
  134.5 47.1 %sort.49.cloned.1.call-start = ((), (), s32[]{:S(2)}) async-start(), calls=%async_computation.6 | async-start | bytes 393248 | tf_op jit(solution)/shard_map/sort | solution.py:735
  194.5 64.5 %collective-permute-start.3 = (bf16[5376,2,128]{2,1,0:T(2,128)(2,1)}, bf16[5376,2,128]{2,1,0:T(2,128)(2,1)}, u32[]{:S(2)}, u32[]{:S(2)}) collective-permute-start(bf16[5376,2,128]{2,1,0:T(2,128)(2,1)} %all-to-all-done.1.own_ref), channel_id=1, source_target_pairs={{0,1},{1,0},{2,3},{3,2},{4,5},{5,4},{6,7},{7,6},{8,9},{9,8},{10,11... | collective-permute-start | bytes 8257544 | tf_op jit(solution)/shard_map/ppermute | solution.py:594
  276.4 127.8 %all-to-all-start.2 = ((bf16[5376,2,128]{2,1,0:T(2,128)(2,1)}), bf16[5376,2,128]{2,1,0:T(2,128)(2,1)}, u32[]{:S(2)}, u32[]{:S(2)}) async-start(bf16[5376,2,128]{2,1,0:T(2,128)(2,1)} %get-tuple-element.959), calls=%async_computation.2 | async-start | bytes 5505024 | tf_op jit(solution)/shard_map/all_to_all | solution.py:599
  282.9 94.3 %copy-start.65 = (s32[16400]{0:T(1024)S(1)}, s32[16400]{0:T(1024)}, u32[]{:S(2)}) copy-start(s32[16400]{0:T(1024)} %fusion.53.pos_ref) | copy-start | bytes 196804
  377.3 32.0 %copy-start.62 = (s32[1,8192]{1,0:T(1,128)S(1)}, s32[1,8192]{1,0:T(1,128)}, u32[]{:S(2)}) copy-start(s32[1,8192]{1,0:T(1,128)} %get-tuple-element.1192) | copy-start | bytes 98308
  404.2 12.8 %collective-permute-start.4 = (bf16[5376,2,128]{2,1,0:T(2,128)(2,1)}, bf16[5376,2,128]{2,1,0:T(2,128)(2,1)}, u32[]{:S(2)}, u32[]{:S(2)}) collective-permute-start(bf16[5376,2,128]{2,1,0:T(2,128)(2,1)} %all-to-all-done.2.own_ref), channel_id=1, source_target_pairs={{0,1},{1,0},{2,3},{3,2},{4,5},{5,4},{6,7},{7,6},{8,9},{9,8},{10,11... | collective-permute-start | bytes 8257544 | tf_op jit(solution)/shard_map/ppermute | solution.py:594
  410.6 179.1 %all-to-all-start.3 = ((f32[16,672,128]{2,1,0:T(8,128)}), f32[16,672,128]{2,1,0:T(8,128)}, u32[]{:S(2)}, u32[]{:S(2)}) async-start(f32[16,672,128]{2,1,0:T(8,128)} %bitcast.139), calls=%async_computation.3 | async-start | bytes 11010048 | tf_op jit(solution)/shard_map/all_to_all | solution.py:599
  503.5 59.5 %copy-start.63 = (s32[16400]{0:T(1024)S(1)}, s32[16400]{0:T(1024)}, u32[]{:S(2)}) copy-start(s32[16400]{0:T(1024)} %fusion.51.pos_ref) | copy-start | bytes 196804
  605.5 134.7 %all-to-all-start.4 = ((f32[16,672,128]{2,1,0:T(8,128)}), f32[16,672,128]{2,1,0:T(8,128)}, u32[]{:S(2)}, u32[]{:S(2)}) async-start(f32[16,672,128]{2,1,0:T(8,128)} %bitcast.138), calls=%async_computation.4 | async-start | bytes 11010048 | tf_op jit(solution)/shard_map/all_to_all | solution.py:599
  612.6 3.7 collective-permute-start.5
  612.7 33.2 %collective-permute-start.6 = (f32[1024,128]{1,0:T(8,128)}, f32[1024,128]{1,0:T(8,128)S(1)}, u32[]{:S(2)}, u32[]{:S(2)}) collective-permute-start(f32[1024,128]{1,0:T(8,128)} %get-tuple-element.982), channel_id=1, source_target_pairs={{0,2},{1,3},{2,0},{3,1},{4,6},{5,7},{6,4},{7,5},{8,10},{9,11},{10,... | collective-permute-start | bytes 1572872 | tf_op jit(solution)/shard_map/ppermute | solution.py:632
  613.9 71.7 %collective-permute-start.7 = (f32[1024,128]{1,0:T(8,128)}, f32[1024,128]{1,0:T(8,128)}, u32[]{:S(2)}, u32[]{:S(2)}) collective-permute-start(f32[1024,128]{1,0:T(8,128)} %get-tuple-element.983), channel_id=1, source_target_pairs={{0,3},{1,2},{2,1},{3,0},{4,7},{5,6},{6,5},{7,4},{8,11},{9,10},{10,... | collective-permute-start | bytes 1572872 | tf_op jit(solution)/shard_map/ppermute | solution.py:632
  614.8 70.9 %collective-permute-start.8 = (f32[1024,128]{1,0:T(8,128)}, f32[1024,128]{1,0:T(8,128)}, u32[]{:S(2)}, u32[]{:S(2)}) collective-permute-start(f32[1024,128]{1,0:T(8,128)} %get-tuple-element.984), channel_id=1, source_target_pairs={{0,4},{1,5},{2,6},{3,7},{4,0},{5,1},{6,2},{7,3},{8,12},{9,13},{10,... | collective-permute-start | bytes 1572872 | tf_op jit(solution)/shard_map/ppermute | solution.py:632
  615.1 88.2 %collective-permute-start.9 = (f32[1024,128]{1,0:T(8,128)}, f32[1024,128]{1,0:T(8,128)}, u32[]{:S(2)}, u32[]{:S(2)}) collective-permute-start(f32[1024,128]{1,0:T(8,128)} %get-tuple-element.985), channel_id=1, source_target_pairs={{0,5},{1,4},{2,7},{3,6},{4,1},{5,0},{6,3},{7,2},{8,13},{9,12},{10,... | collective-permute-start | bytes 1572872 | tf_op jit(solution)/shard_map/ppermute | solution.py:632
  616.2 107.7 %copy-start.2 = (f32[1024,128]{1,0:T(8,128)S(1)}, f32[1024,128]{1,0:T(8,128)}, u32[]{:S(2)}) copy-start(f32[1024,128]{1,0:T(8,128)} %get-tuple-element.1014.refs_0_) | copy-start | bytes 1572868
  616.2 69.4 %copy-start.69 = (f32[1024,128]{1,0:T(8,128)}, f32[1024,128]{1,0:T(8,128)S(1)}, u32[]{:S(2)}) copy-start(f32[1024,128]{1,0:T(8,128)S(1)} %collective-permute-done.5.refs_1_) | copy-start | bytes 1572868
  616.2 96.4 %collective-permute-start.10 = (f32[1024,128]{1,0:T(8,128)}, f32[1024,128]{1,0:T(8,128)}, u32[]{:S(2)}, u32[]{:S(2)}) collective-permute-start(f32[1024,128]{1,0:T(8,128)} %get-tuple-element.986), channel_id=1, source_target_pairs={{0,6},{1,7},{2,4},{3,5},{4,2},{5,3},{6,0},{7,1},{8,14},{9,15},{10,... | collective-permute-start | bytes 1572872 | tf_op jit(solution)/shard_map/ppermute | solution.py:632
  645.9 39.7 %copy-start.70 = (f32[1024,128]{1,0:T(8,128)}, f32[1024,128]{1,0:T(8,128)S(1)}, u32[]{:S(2)}) copy-start(f32[1024,128]{1,0:T(8,128)S(1)} %collective-permute-done.6.refs_2_) | copy-start | bytes 1572868
  645.9 78.0 %collective-permute-start.11 = (f32[1024,128]{1,0:T(8,128)}, f32[1024,128]{1,0:T(8,128)}, u32[]{:S(2)}, u32[]{:S(2)}) collective-permute-start(f32[1024,128]{1,0:T(8,128)} %get-tuple-element.987), channel_id=1, source_target_pairs={{0,7},{1,6},{2,5},{3,4},{4,3},{5,2},{6,1},{7,0},{8,15},{9,14},{10,... | collective-permute-start | bytes 1572872 | tf_op jit(solution)/shard_map/ppermute | solution.py:632
  756.1 52.2 %copy-start.23 = (f32[1024,128]{1,0:T(8,128)S(1)}, f32[1024,128]{1,0:T(8,128)}, u32[]{:S(2)}) copy-start(f32[1024,128]{1,0:T(8,128)} %get-tuple-element.999.refs_0_) | copy-start | bytes 1572868
  (16 other events, 186.2 us)
Sparse Core Ops, SparseCore 0:
  43.6 41.9 sort.51.cloned.1.call-done
  137.8 43.5 sort.53.cloned.1.call-done
  (2 shorter events, 0.0 us)

commit v3 on v2

--- a/solution.py
+++ b/solution.py
@@ -10,6 +10,7 @@
 C1 = 0.7978845608028654
 C2 = C1 * 0.044715
 BF16 = jnp.bfloat16
+I32 = jnp.iinfo(jnp.int32)
 F32 = jnp.float32
 VMEM_LIMIT = 62 * 1024 * 1024
 MESH = pl.DeviceIdType.MESH
@@ -75,7 +76,7 @@
     work = gather_step(served, which, n_src)
 
     def kernel(ids_ref, served_ref, out_ref, *scratch):
-        work((ids_ref, served_ref), out_ref, scratch)
+        work((ids_ref, served_ref), out_ref, scratch, lambda: None)
 
     return pl.pallas_call(
         kernel, out_shape=gathered(served, n_src), in_specs=[SMEM_SPEC, ANY_SPEC], out_specs=VMEM_SPEC,
@@ -97,7 +98,7 @@
     blk, width = served.shape[2:]
     pieces = width // LANES
 
-    def work(ins, out_ref, scratch):
+    def work(ins, out_ref, scratch, then):
         ids_ref, served_ref = ins
         native, flat, isem = scratch
         reads = [pltpu.make_async_copy(served_ref.at[b, which], native.at[b], isem.at[b]) for b in range(PLANE)]
@@ -107,6 +108,7 @@
             reads[b].wait()
             for c in range(pieces):
                 flat[pl.ds(b * blk * pieces + c, blk, stride=pieces), :] = native[b, :, c * LANES:(c + 1) * LANES].astype(F32)
+        then()
 
         def src(s, c):
             def part(b, c):
@@ -119,6 +121,70 @@
             return c
 
         lax.fori_loop(0, n_src, src, 0)
+
+    return work
+
+
+def unpacked(idx, rec, heads):
+    return shape_of((idx.shape[0] // heads, heads * rec.shape[1] * LANES), BF16)
+
+
+def unpack_scratch(rec, heads):
+    half, pieces = rec.shape[0], rec.shape[1]
+    rows = pltpu.VMEM((TILE * heads * pieces, LANES), F32)
+    return [pltpu.VMEM((2 * half + 8, pieces, LANES), BF16), rows, pltpu.SemaphoreType.DMA((2,)), rows,
+            pltpu.VMEM((TILE, heads * pieces * LANES), BF16)]
+
+
+def unpack_step(idx, rec_own, rec_pair, heads):
+    n = idx.shape[0]
+    half, pieces = rec_own.shape[0], rec_own.shape[1]
+    per = heads * pieces
+
+    def work(ins, out_ref, scratch, then):
+        idx_ref, own_ref, pair_ref = ins[:3]
+        rec, stage, sem, more, native = scratch
+        copies = [pltpu.make_async_copy(own_ref, rec.at[pl.ds(0, half)], sem.at[0]),
+                  pltpu.make_async_copy(pair_ref, rec.at[pl.ds(half, half)], sem.at[1])]
+        for c in copies:
+            c.start()
+        for c in copies:
+            c.wait()
+        then()
+
+        def part(i, c):
+            first = i * (TILE * heads)
+
+            def blk(b, c):
+                for j in range(UNROLL):
+                    row = rec[idx_ref[first + b * UNROLL + j]]
+                    stage[pl.ds(pl.multiple_of(b * UNROLL * pieces, UNROLL * pieces) + pieces * j, pieces), :] = row.astype(F32)
+                return c
+
+            lax.fori_loop(0, TILE * heads // UNROLL, blk, 0)
+            if len(ins) > 3:
+                late_ref, rounds_ref = ins[3:]
+
+                @pl.when(rounds_ref[0] > 1)
+                def _():
+                    fetch = pltpu.make_async_copy(late_ref.at[pl.ds(i * TILE, TILE)], native, sem.at[0])
+                    fetch.start()
+                    fetch.wait()
+                    store_rows(more, native[...].astype(F32))
+
+                    def patch(r, c):
+                        @pl.when(idx_ref[first + r] == 2 * half)
+                        def _():
+                            stage[pair_at(2 * r), :] = more[pair_at(2 * r), :]
+
+                        return c
+
+                    lax.fori_loop(0, TILE * heads, patch, 0)
+            for c in range(per):
+                out_ref[pl.ds(i * TILE, TILE), c * LANES:(c + 1) * LANES] = stage[pl.ds(c, TILE, stride=per), :].astype(BF16)
+            return c
+
+        lax.fori_loop(0, n // heads // TILE, part, 0)
 
     return work
 
@@ -146,15 +212,19 @@
 
         @pl.when(opening)
         def _():
-            for c in copies:
-                c.start()
-            if first_step is not None:
-                first_step(in_refs[n_own_in:], out_refs[n_own_out:], rest)
+            def start_weights():
+                for c in copies:
+                    c.start()
+
+            if first_step is None:
+                start_weights()
+            else:
+                first_step(in_refs[n_own_in:], out_refs[n_own_out:], rest, start_weights)
 
         def need(*which):
             @pl.when(opening)
             def _():
-                for i in which:
+                for i in which or range(n_w):
                     copies[i].wait()
 
         if mirror is None:
@@ -227,17 +297,26 @@
         ref[pl.ds(c, tokens, stride=n), :] = value[:, c * LANES:(c + 1) * LANES]
 
 
+def tile_of(ref, tile):
+    return ref.at[pl.ds(pl.multiple_of(pl.program_id(0) * tile, tile), tile), :]
+
+
+def unpack_ins(rows):
+    return list(zip(rows, [SMEM_SPEC, ANY_SPEC, ANY_SPEC, ANY_SPEC, SMEM_SPEC]))
+
+
 def layer_plain(x, w_up, w_down, layer, tile=WIDE_TILE):
     tokens, d = x.shape
 
     def body(need, ins, w, outs, rest):
-        need(0, 1)
+        need()
+        up, down = w
         x_f = ins[0][...].astype(F32)
         u = (x_f * rms(x_f)).astype(BF16)
-        mlp_up(u, w[0], rest[0], None)
+        mlp_up(u, up, rest[0], None)
         for q in range(d // COLS):
             cols = slice(q * COLS, (q + 1) * COLS)
-            m = dot_nn(rest[0][...], w[1][:, cols]).astype(BF16)
+            m = dot_nn(rest[0][...], down[:, cols]).astype(BF16)
             outs[0][:, cols] = (ins[0][:, cols].astype(F32) + m.astype(F32)).astype(BF16)
 
     return token_kernel(body, tile, tokens, [(x, 1)], [(w_up, layer), (w_down, layer)],
@@ -249,23 +328,24 @@
     gather = gather_step(served, 1, n_src)
     sent = gathered(served, n_src)
 
-    def first_step(ins, outs, rest):
+    def first_step(ins, outs, rest, then):
         stage, sem = rest[-2:]
-        gather(ins, stage, rest[1:-2])
+        gather(ins, stage, rest[1:-2], then)
         done = pltpu.make_async_copy(stage, outs[0], sem)
         done.start()
         done.wait()
 
     def body(need, ins, w, outs, rest):
-        need(0, 1, 2)
+        need()
+        up, down, gate = w
         x_f = ins[0][...].astype(F32)
         u = (x_f * rms(x_f)).astype(BF16)
-        mlp_up(u, w[0], rest[0], None)
-        a = dot_nn(u, w[2][...]).astype(BF16)
+        mlp_up(u, up, rest[0], None)
+        a = dot_nn(u, gate[...]).astype(BF16)
         outs[1][...] = gelu(a.astype(F32)).astype(BF16)
         for q in range(d // COLS):
             cols = slice(q * COLS, (q + 1) * COLS)
-            outs[0][:, cols] = dot_nn(rest[0][...], w[1][:, cols]).astype(BF16)
+            outs[0][:, cols] = dot_nn(rest[0][...], down[:, cols]).astype(BF16)
 
     return token_kernel(body, tile, tokens, [(x, 1)],
                         [(w_up, layer), (w_down, layer), (w_gate, which)],
@@ -275,16 +355,17 @@
                         [(ids, SMEM_SPEC), (served, ANY_SPEC)], [sent], first_step)
 
 
-def layer_middle(x, m, g, e, d_out, w_up, w_down, w_gate, w_proj, layer, tile=TILE):
+def layer_middle(x, m, g, rows, d_out, w_up, w_down, w_gate, w_proj, layer, heads, tile=TILE):
     tokens, d = x.shape
     ff = w_up.shape[2]
+    unpack = unpack_step(*rows[:3], heads)
 
     def body(need, ins, w, outs, rest):
-        x_ref, m_ref, g_ref, e_ref, c_ref = ins
-        x2_ref, h_ref, x3_ref, a_ref, dz_ref, h3_ref = outs
-        act = rest[0]
+        x_ref, m_ref, g_ref, c_ref = ins
+        x2_ref, h_ref, x3_ref, a_ref, dz_ref, row_ref = outs
+        act, e = rest[:2]
         need(4, 0)
-        z = (g_ref[...].astype(F32) * e_ref[...].astype(F32)).astype(BF16)
+        z = (g_ref[...].astype(F32) * tile_of(e, tile)[...].astype(F32)).astype(BF16)
         q = dot_nn(z, w[4][...]).astype(BF16)
         x2 = ((x_ref[...].astype(F32) + m_ref[...].astype(F32)) + q.astype(F32)).astype(BF16)
         x2_ref[...] = x2
@@ -298,22 +379,35 @@
             x3_ref[:, cols] = (x2_ref[:, cols].astype(F32) + mm.astype(F32)).astype(BF16)
         x_f = x3_ref[...].astype(F32)
         u = (x_f * rms(x_f)).astype(BF16)
-        need(2, 3, 5)
-        mlp_up(u, w[5], None, h3_ref)
+        need(2, 3)
         a = dot_nn(u, w[2][...]).astype(BF16)
         a_ref[...] = a
         gate = gelu(a.astype(F32)).astype(BF16)
         dz = dot_nt(c_ref[...], w[3][...])
         dz_ref[...] = dz
-        store_rows(rest[-1], gate.astype(F32) * dz)
+        store_rows(row_ref, gate.astype(F32) * dz)
 
     vec = (shape_of((tokens, d), BF16), 1)
-    return token_kernel(body, tile, tokens, [(x, 1), (m, 1), (g, 1), (e, 1), (d_out, 1)],
-                        [(w_up, layer), (w_down, layer), (w_gate, 1), (w_proj, 1), (w_proj, 0), (w_up, layer + 1)],
+    return token_kernel(body, tile, tokens, [(x, 1), (m, 1), (g, 1), (d_out, 1)],
+                        [(w_up, layer), (w_down, layer), (w_gate, 1), (w_proj, 1), (w_proj, 0)],
                         [vec, (shape_of((tokens, ff), BF16), 1), vec, vec, (shape_of((tokens, d), F32), 1),
-                         (shape_of((tokens, ff), BF16), 1)],
-                        [pltpu.VMEM((tile, ff), BF16)], 90,
-                        mirror=(shape_of((tokens * d // LANES, LANES), F32), d // LANES, 10))
+                         (shape_of((tokens * d // LANES, LANES), F32), d // LANES)],
+                        [pltpu.VMEM((tile, ff), BF16), pltpu.VMEM((tokens, d), BF16)] + unpack_scratch(rows[1], heads), 76,
+                        unpack_ins(rows), (), lambda ins, outs, rest, then: unpack(ins, rest[1], rest[2:], then))
+
+
+def last_up(x, w_up, layer, tile=WIDE_TILE):
+    tokens, ff = x.shape[0], w_up.shape[2]
+
+    def body(need, ins, w, outs, rest):
+        need()
+        up, = w
+        x_f = ins[0][...].astype(F32)
+        u = (x_f * rms(x_f)).astype(BF16)
+        mlp_up(u, up, None, outs[0])
+
+    return token_kernel(body, tile, tokens, [(x, 1)], [(w_up, layer)],
+                        [(shape_of((tokens, ff), BF16), 1)], [], 22)[0]
 
 
 def last_down(x, h, a, e, w_down, w_proj, layer, which, tile=TILE):
@@ -323,7 +417,8 @@
     def body(need, ins, w, outs, rest):
         x_ref, h_ref, a_ref, e_ref = ins
         act = rest[0]
-        need(0, 1)
+        need()
+        down, proj = w
         gate = gelu(a_ref[...].astype(F32)).astype(BF16)
         z = (gate.astype(F32) * e_ref[...].astype(F32)).astype(BF16)
         for j in range(ff // CHUNK):
@@ -331,8 +426,8 @@
             act[:, cols] = gelu(h_ref[:, cols].astype(F32)).astype(BF16)
         for n in range(d // COLS):
             cols = slice(n * COLS, (n + 1) * COLS)
-            m = dot_nn(act[...], w[0][:, cols]).astype(BF16)
-            q = dot_nn(z, w[1][:, cols]).astype(BF16)
+            m = dot_nn(act[...], down[:, cols]).astype(BF16)
+            q = dot_nn(z, proj[:, cols]).astype(BF16)
             outs[0][:, cols] = ((x_ref[:, cols].astype(F32) + m.astype(F32)) + q.astype(F32)).astype(BF16)
 
     return token_kernel(body, tile, tokens, [(x, 1), (h, 1), (a, 1), (e, 1)],
@@ -355,23 +450,34 @@
     return c_f + (s * du - x_f * (s * s * s) * jnp.mean(x_f * du, axis=-1, keepdims=True))
 
 
-def back_table(c, h, x, a, dz, e, w_up, w_down, w_gate, layer, which, tile=TILE):
+def back_table(c, h, x, a, dz, rows, w_up, w_down, w_gate, layer, which, heads, tile=TILE):
     tokens, d = x.shape
     ff = h.shape[1]
+    unpack = unpack_step(*rows[:3], heads)
+
+    def first_step(ins, outs, rest, then):
+        unpack(ins, rest[2], rest[4:], then)
+        done = pltpu.make_async_copy(rest[2], outs[0], rest[3])
+        done.start()
+        done.wait()
 
     def body(need, ins, w, outs, rest):
-        c_ref, h_ref, x_ref, a_ref, dz_ref, e_ref = ins
-        need(0, 1, 2)
-        d_gate = gelu_bwd(a_ref[...].astype(F32), dz_ref[...] * e_ref[...].astype(F32)).astype(BF16)
-        rest[1][...] = dot_nt(d_gate, w[2][...])
-        du = back_mlp(c_ref[...], h_ref, w[0], w[1], rest[0]) + rest[1][...]
+        c_ref, h_ref, x_ref, a_ref, dz_ref = ins
+        need()
+        up, down, w_g = w
+        e = tile_of(rest[2], tile)[...].astype(F32)
+        d_gate = gelu_bwd(a_ref[...].astype(F32), dz_ref[...] * e).astype(BF16)
+        rest[1][...] = dot_nt(d_gate, w_g[...])
+        du = back_mlp(c_ref[...], h_ref, up, down, rest[0]) + rest[1][...]
         outs[0][...] = back_norm(c_ref[...].astype(F32), x_ref, du)
 
     return token_kernel(body, tile, tokens,
-                        [(c, 1), (h, 1), (x, 1), (a, 1), (dz, 1), (e, 1)],
+                        [(c, 1), (h, 1), (x, 1), (a, 1), (dz, 1)],
                         [(w_up, layer), (w_down, layer), (w_gate, which)],
                         [(shape_of((tokens, d), F32), 1)],
-                        [pltpu.VMEM((tile, ff), BF16), pltpu.VMEM((tile, d), F32)], 58)[0]
+                        [pltpu.VMEM((tile, ff), BF16), pltpu.VMEM((tile, d), F32), pltpu.VMEM((tokens, d), BF16),
+                         pltpu.SemaphoreType.DMA] + unpack_scratch(rows[1], heads), 72,
+                        unpack_ins(rows), [shape_of((tokens, d), BF16)], first_step)
 
 
 def back_plain(c, h, x, g, w_up, w_down, w_proj, layer, which, tile=TILE):
@@ -380,10 +486,11 @@
 
     def body(need, ins, w, outs, rest):
         c_ref, h_ref, x_ref, g_ref = ins
-        need(0, 1, 2)
-        du = back_mlp(c_ref[...].astype(BF16), h_ref, w[0], w[1], rest[0])
+        need()
+        up, down, proj = w
+        du = back_mlp(c_ref[...].astype(BF16), h_ref, up, down, rest[0])
         c_low = back_norm(c_ref[...], x_ref, du).astype(BF16)
-        store_rows(rest[-1], g_ref[...].astype(F32) * dot_nt(c_low, w[2][...]))
+        store_rows(rest[-1], g_ref[...].astype(F32) * dot_nt(c_low, proj[...]))
 
     return token_kernel(body, tile, tokens, [(c, 1), (h, 1), (x, 1), (g, 1)],
                         [(w_up, layer), (w_down, layer), (w_proj, which)], [],
@@ -415,72 +522,51 @@
         compiler_params=local_params(), name="split_rows", cost_estimate=cost(4))(place, tables)
 
 
-def make_ids(uid, start, count, peak, rnd, blank):
-    n_tgt = count.shape[0]
-    rows = -(-SLOTS // LANES)
-
-    def kernel(uid_ref, start_ref, count_ref, peak_ref, rnd_ref, out_ref):
+def make_ids(distinct, start, count, peak, rnd, rows):
+    n_tab, n_row = distinct.shape[:2]
+    n_tgt = count.shape[0] // n_tab
+    depth, per = -(-SLOTS // LANES), IDW // LANES
+
+    def kernel(name_ref, start_ref, count_ref, peak_ref, rnd_ref, out_ref):
         lane = lax.broadcasted_iota(jnp.int32, (1, LANES), 1)
-        out_ref[...] = jnp.full(out_ref.shape, peak_ref[0], jnp.int32)
-        for g in range(n_tgt):
-            shift = rnd_ref[0] * SLOTS
-            left = jnp.clip(count_ref[g] - shift, 0, SLOTS)
-            at = jnp.minimum(start_ref[g] + shift, (uid_ref.shape[0] - rows - 1) * LANES)
-            row, off = at // LANES, lax.rem(at, LANES)
-            turned = [pltpu.roll(uid_ref[row + i], lax.rem(LANES - off, LANES), axis=1) for i in range(rows + 1)]
-            for i in range(rows):
-                ids = jnp.where(lane < LANES - off, turned[i], turned[i + 1])
-                out_ref[g, i:i + 1, :] = jnp.where(i * LANES + lane < left, ids, blank)
+        shift = rnd_ref[0] * SLOTS
+        for t in range(n_tab):
+            out_ref[:, t * per:(t + 1) * per, :] = jnp.full((n_tgt, per, LANES), peak_ref[t], jnp.int32)
+            for g in range(n_tgt):
+                left = jnp.clip(count_ref[t * n_tgt + g] - shift, 0, SLOTS)
+                at = start_ref[t * n_tgt + g] + shift
+                row, off = at // LANES, lax.rem(at, LANES)
+                turned = [pltpu.roll(name_ref[t, jnp.minimum(row + i, n_row - 1)], lax.rem(LANES - off, LANES), axis=1)
+                          for i in range(depth + 1)]
+                for i in range(depth):
+                    ids = 2 * (jnp.where(lane < LANES - off, turned[i], turned[i + 1]) & (rows - 1))
+                    out_ref[g, t * per + i:t * per + i + 1, :] = jnp.where(i * LANES + lane < left, ids, 2 * rows)
 
     return pl.pallas_call(
-        kernel, out_shape=shape_of((n_tgt, IDW // LANES, LANES), jnp.int32),
+        kernel, out_shape=shape_of((n_tgt, n_tab * per, LANES), jnp.int32),
         in_specs=[VMEM_SPEC] + [SMEM_SPEC] * 4, out_specs=VMEM_SPEC, compiler_params=local_params(), name="make_ids",
         cost_estimate=cost(3),
-    )(uid, start, count, peak, jnp.reshape(rnd, (1,)).astype(jnp.int32))
+    )(distinct, start, count, peak, jnp.reshape(rnd, (1,)).astype(jnp.int32))
 
 
 def unpack_rows(idx, rec_own, rec_pair, heads):
-    n = idx.shape[0]
-    half, pieces = rec_own.shape[0], rec_own.shape[1]
-    tokens, tile = n // heads, TILE
-    per = heads * pieces
-
-    def kernel(idx_ref, own_ref, pair_ref, out_ref, rec, stage, sem):
-        copies = [pltpu.make_async_copy(own_ref, rec.at[pl.ds(0, half)], sem.at[0]),
-                  pltpu.make_async_copy(pair_ref, rec.at[pl.ds(half, half)], sem.at[1])]
-        for c in copies:
-            c.start()
-        for c in copies:
-            c.wait()
-
-        def part(i, c):
-            def blk(b, c):
-                for j in range(UNROLL):
-                    row = rec[idx_ref[i * (tile * heads) + b * UNROLL + j]]
-                    stage[pl.ds(pl.multiple_of(b * UNROLL * pieces, UNROLL * pieces) + pieces * j, pieces), :] = row.astype(F32)
-                return c
-
-            lax.fori_loop(0, tile * heads // UNROLL, blk, 0)
-            for c in range(per):
-                out_ref[pl.ds(i * tile, tile), c * LANES:(c + 1) * LANES] = stage[pl.ds(c, tile, stride=per), :].astype(BF16)
-            return c
-
-        lax.fori_loop(0, tokens // tile, part, 0)
+    step = unpack_step(idx, rec_own, rec_pair, heads)
+
+    def kernel(idx_ref, own_ref, pair_ref, out_ref, *scratch):
+        step((idx_ref, own_ref, pair_ref), out_ref, scratch, lambda: None)
 
     return pl.pallas_call(
-        kernel, out_shape=shape_of((tokens, per * LANES), BF16),
-        in_specs=[SMEM_SPEC, ANY_SPEC, ANY_SPEC], out_specs=VMEM_SPEC,
-        scratch_shapes=[pltpu.VMEM((2 * half, pieces, LANES), BF16), pltpu.VMEM((tile * per, LANES), F32), pltpu.SemaphoreType.DMA((2,))],
-        compiler_params=local_params(), name="unpack_rows", cost_estimate=cost(16),
+        kernel, out_shape=unpacked(idx, rec_own, heads), in_specs=[SMEM_SPEC, ANY_SPEC, ANY_SPEC], out_specs=VMEM_SPEC,
+        scratch_shapes=unpack_scratch(rec_own, heads), compiler_params=local_params(), name="unpack_rows", cost_estimate=cost(16),
     )(idx, rec_own, rec_pair)
 
 
-def pack_rows(pos, dst, size, grad_own, grad_pair, n_tgt):
+def pack_rows(pos, dst, span, grad_own, grad_pair, n_tgt):
     n = grad_own.shape[0]
     n_row = 2 * n_tgt * SLOTS
-    low = jnp.iinfo(jnp.int32).max
-
-    def kernel(pos_ref, dst_ref, size_ref, own_ref, pair_ref, out_ref, g_ref, stage, sem):
+    low = I32.max
+
+    def kernel(pos_ref, dst_ref, span_ref, own_ref, pair_ref, out_ref, g_ref, stage, sem):
         first = pltpu.make_async_copy(own_ref, g_ref.at[pl.ds(0, n)], sem.at[0])
         second = pltpu.make_async_copy(pair_ref, g_ref.at[pl.ds(n, n)], sem.at[1])
         first.start()
@@ -488,15 +574,18 @@
         first.wait()
         second.wait()
 
+        begin, size = span_ref[0], span_ref[1]
+
         def blk(b, acc):
+            base = begin + b * UNROLL
             for j in range(UNROLL):
-                p = pos_ref[b * UNROLL + j]
+                p = pos_ref[base + j]
                 row = g_ref[pair_at(p & low), :]
                 acc = row + jnp.where(jnp.full((2, LANES), p, jnp.int32) < 0, acc, 0.0)
-                stage[pair_at(dst_ref[b * UNROLL + j]), :] = acc
+                stage[pair_at(dst_ref[base + j]), :] = acc
             return acc
 
-        lax.fori_loop(0, (size_ref[0] + UNROLL - 1) // UNROLL, blk, jnp.zeros((2, LANES), F32))
+        lax.fori_loop(0, (size + UNROLL - 1) // UNROLL, blk, jnp.zeros((2, LANES), F32))
         done = pltpu.make_async_copy(stage.at[pl.ds(0, n_row)], out_ref, sem.at[0])
         done.start()
         done.wait()
@@ -506,7 +595,7 @@
         in_specs=[SMEM_SPEC, SMEM_SPEC, SMEM_SPEC, ANY_SPEC, ANY_SPEC], out_specs=ANY_SPEC,
         scratch_shapes=[pltpu.VMEM((2 * n, LANES), F32), pltpu.VMEM((n_row + 8, LANES), F32), pltpu.SemaphoreType.DMA((2,))],
         compiler_params=local_params(), name="pack_rows", cost_estimate=cost(26),
-    )(pos, dst, size, grad_own, grad_pair)
+    )(pos, dst, span, grad_own, grad_pair)
 
 
 def owner_scatter(ids, rec, rows, place):
@@ -527,10 +616,9 @@
             return c
 
         lax.fori_loop(0, 2 * rows // LANES, zero, 0)
-        for c in reads:
-            c.wait()
-
-        def src(s, c):
+        for s in range(n_src):
+            reads[s].wait()
+
             def blk(b, c):
                 at = [pair_at(ids_ref[s * IDW + b * per + j]) for j in range(per)]
                 base = pl.multiple_of((s * SLOTS + b * per) * 2, 2 * per)
@@ -540,9 +628,6 @@
                 return c
 
             lax.fori_loop(0, SLOTS // per, blk, 0)
-            return c
-
-        lax.fori_loop(0, n_src, src, 0)
         writes = []
         for b in range(PLANE):
             at = pl.multiple_of((place_ref[0] ^ b) * blk_rows, blk_rows)
@@ -628,32 +713,12 @@
     return lax.all_to_all(x, 'emb', 0, 0, axis_index_groups=groups, tiled=True)
 
 
+def empty_array(shape, dtype):
+    return pl.pallas_call(lambda o: None, out_shape=shape_of(shape, dtype), out_specs=ANY_SPEC, name="empty")()
+
+
 def place_trade(blocks, n_dev):
     return [blocks[0]] + [lax.ppermute(blocks[b], 'emb', [(i, i ^ b) for i in range(n_dev)]) for b in range(1, PLANE)]
-
-
-def place_exchange(blocks, cid):
-    def kernel(*refs):
-        srcs, outs, (ssem, rsem) = refs[:PLANE - 1], refs[PLANE - 1:2 * (PLANE - 1)], refs[-2:]
-        me = lax.axis_index('emb')
-        barrier = pltpu.get_barrier_semaphore()
-        for b in range(1, PLANE):
-            pl.semaphore_signal(barrier, inc=1, device_id=(me ^ b,), device_id_type=MESH)
-        pl.semaphore_wait(barrier, PLANE - 1)
-        copies = [pltpu.make_async_remote_copy(
-            src_ref=srcs[b - 1], dst_ref=outs[b - 1], send_sem=ssem.at[b], recv_sem=rsem.at[b],
-            device_id=(me ^ b,), device_id_type=MESH) for b in range(1, PLANE)]
-        for c in copies:
-            c.start()
-        for c in copies:
-            c.wait()
-
-    shape = shape_of(blocks[0].shape, blocks[0].dtype)
-    got = pl.pallas_call(
-        kernel, out_shape=[shape] * (PLANE - 1), in_specs=[ANY_SPEC] * (PLANE - 1), out_specs=[ANY_SPEC] * (PLANE - 1),
-        scratch_shapes=[pltpu.SemaphoreType.DMA((PLANE,)), pltpu.SemaphoreType.DMA((PLANE,))],
-        compiler_params=remote_params(cid), name="place_exchange", cost_estimate=cost(50))(*blocks[1:])
-    return [blocks[0]] + list(got)
 
 
 def after(x, *deps):
@@ -686,17 +751,13 @@
     core = lax.rem(me, 2)
     size = jnp.where(core == 0, n_low, n - n_low)
     begin = jnp.where(core == 0, 0, n_low)
-    low = jnp.iinfo(jnp.int32).min
-    both = jnp.stack([2 * pos + jnp.where(first, 0, low), code])
-    both = jnp.concatenate([both, both, both[:, :UNROLL]], axis=1)
-    mine = lax.dynamic_slice(both, (0, begin), (2, n + UNROLL))
-    valid = jnp.arange(n + UNROLL, dtype=jnp.int32) < size
-    most = jnp.iinfo(jnp.int32).max
-    distinct = jnp.where(first & (sid // (n_chip * rows_dev) == core), sid, most)
+    mine = sid // (n_chip * rows_dev) == core
     start = lax.dynamic_slice(start, (core * n_chip,), (n_chip,))
-    return dict(pos=jnp.where(valid, mine[0], 0), code=jnp.where(valid, mine[1], -1), distinct=distinct, start=start - start[0],
-                size=size.reshape(1), by_pos=jnp.where(pos < n_own, pos * (n_dev * 2 * rows_dev) + code, most),
-                count=lax.dynamic_slice(count, (core * n_chip,), (n_chip,)), peak=jnp.max(count).reshape(1))
+    return dict(pos=jnp.pad(2 * pos + jnp.where(first, 0, I32.min), (0, UNROLL)),
+                code=jnp.pad(jnp.where(mine, code, -1), (0, UNROLL), constant_values=-1),
+                span=jnp.stack([begin, size]), distinct=jnp.where(first & mine, sid, I32.max), start=start - start[0],
+                by_pos=jnp.where(pos < n_own, pos * (n_dev * 2 * rows_dev) + code, I32.max),
+                count=lax.dynamic_slice(count, (core * n_chip,), (n_chip,)), peak=jnp.max(count))
 
 
 def round_slot(code, span, rnd, trash, width):
@@ -729,8 +790,7 @@
         plans = [route_plan(keys[t], n_req, rows_dev, n_dev, me) for t in range(n_tab)]
         distinct = lax.sort(jnp.stack([plan['distinct'] for plan in plans]), dimension=1)
         x1 = layer_plain(after(x_start, *[plan['distinct'] for plan in plans]), w_up, w_down, 0)
-        margin = jnp.zeros((n_tab, CHUNK), jnp.int32)
-        distinct = jnp.concatenate([2 * lax.rem(distinct, rows_dev), margin], axis=1).reshape(n_tab, -1, 1, LANES)
+        distinct = distinct.reshape(n_tab, -1, 1, LANES)
         span = 2 * rows_dev
         in_order = lax.sort(after(jnp.stack([plan['by_pos'] for plan in plans]), distinct), dimension=1)
         code_own = lax.rem(in_order[:, :n_req], n_dev * span)
@@ -740,41 +800,47 @@
             code = jnp.where(code >= 0, lax.rem(code, n_chip * span), code)
             return round_slot(code, span, rnd, trash, width)
 
-        def id_blocks(which, rnd):
-            plan = plans[which]
-            return make_ids(distinct[which], plan['start'], plan['count'], plan['peak'], rnd, 2 * rows_dev)
-
-        blocks = jnp.stack([id_blocks(t, jnp.int32(0)) for t in range(n_tab)], axis=1)
-        blocks = blocks.reshape(n_chip, n_tab * IDW // LANES, LANES)
+        def id_blocks(tabs, rnd):
+            start, count = (jnp.concatenate([plans[t][key] for t in tabs]) for key in ('start', 'count'))
+            peak = jnp.stack([plans[t]['peak'] for t in tabs])
+            return make_ids(distinct[tabs[0]:tabs[-1] + 1], start, count, peak, rnd, rows_dev)
+
+        blocks = id_blocks(range(n_tab), jnp.int32(0))
         got = chip_exchange(after(blocks, served, x1), 9, n_chip).reshape(n_chip, n_tab, IDW)
         first_ids = [got[:, t].reshape(n_chip * IDW) for t in range(n_tab)]
         rounds = [(jnp.max(got[:, t, IDW - 1]) + SLOTS - 1) // SLOTS for t in range(n_tab)]
 
         def more_ids(which, rnd, cid):
-            return chip_exchange(id_blocks(which, rnd), cid, n_chip).reshape(n_chip * IDW)
+            return chip_exchange(id_blocks([which], rnd), cid, n_chip).reshape(n_chip * IDW)
 
         def own_slot(which, rnd):
-            slot = round_slot(code_own[which], span, rnd, 0, SLOTS)
-            return jnp.where(core == 0, slot, lax.rem(slot + n_chip * SLOTS, 2 * n_chip * SLOTS))
+            half = n_chip * SLOTS
+            slot = round_slot(code_own[which], span, rnd, 2 * half, SLOTS)
+            return jnp.where((core == 0) | (slot == 2 * half), slot, lax.rem(slot + half, 2 * half))
 
         def unpack(which, rnd, own):
             return unpack_rows(own_slot(which, rnd), own, swap_cores(own, n_dev), n_heads)
 
-        def fetch_rest(which, first):
+        def late_rows(start):
             def more(state):
-                rnd, rows = state
-                ids = more_ids(which, rnd, which)
-                sent = owner_gather(ids, served, which, n_chip).reshape((n_chip, SLOTS) + tail)
-                new = unpack(which, rnd, chip_exchange(sent, 2 + which, n_chip).reshape((n_chip * SLOTS,) + tail))
-                now = lax.rem(code_own[which], span) // SLOTS == rnd
-                return rnd + 1, jnp.where(jnp.repeat(now, row_width).reshape(rows.shape), new, rows)
-
-            return lax.while_loop(lambda s: s[0] < rounds[which], more, (jnp.int32(1), first))[1]
+                rnd, now = state[0], []
+                for t in range(n_tab):
+                    sent = owner_gather(more_ids(t, rnd, t), served, t, n_chip).reshape((n_chip, SLOTS) + tail)
+                    new = unpack(t, rnd, chip_exchange(sent, 2 + t, n_chip).reshape((n_chip * SLOTS,) + tail))
+                    mine = lax.rem(code_own[t], span) // SLOTS == rnd
+                    now.append(jnp.where(jnp.repeat(mine, row_width).reshape(new.shape), new, state[1 + t]))
+                return (rnd + 1, *now)
+
+            most = jnp.maximum(*rounds)
+            return lax.while_loop(lambda s: s[0] < most, more, (jnp.int32(1), *start))[1:]
+
+        def parts(which, own):
+            return own_slot(which, 0), own, swap_cores(own, n_dev), late[which], rounds[which].reshape(1)
 
         def packed(which, rnd, grad_own, grad_pair):
             plan = plans[which]
             dst = 2 * half_slot(plan, rnd, SLOTS, n_chip * SLOTS)
-            return pack_rows(plan['pos'], dst, plan['size'], grad_own, grad_pair, n_chip)
+            return pack_rows(plan['pos'], dst, plan['span'], grad_own, grad_pair, n_chip)
 
         def return_rest(which, first, pair):
             def more(state):
@@ -789,14 +855,16 @@
         sent0 = owner_gather(first_ids[0], served, 0, n_chip)
         fetched0 = chip_trade(sent0, n_dev)
         m1, g1, sent1 = layer_table_head(after(x1, sent0), w_up, w_down, w_gate, 1, 0, first_ids[1], served, n_chip)
-        e1 = fetch_rest(0, unpack(0, 0, fetched0))
-        fetched1 = chip_trade(after(sent1, e1), n_dev)
-        x2, h2, x3, a3, dz3, h3, *pair1 = layer_middle(x1, m1, g1, e1, d_out, w_up, w_down, w_gate, w_proj, 2)
-        sent1 = packed(1, 0, *pair1)
+        late = late_rows([after(empty_array((n_tok, n_heads * row_width), BF16), m1, fetched0) for _ in range(n_tab)])
+        rows0 = parts(0, after(fetched0, m1))
+        fetched1 = chip_trade(after(sent1, fetched0, *late), n_dev)
+        x2, h2, x3, a3, dz3, rows3 = layer_middle(x1, m1, g1, rows0, d_out, w_up, w_down, w_gate, w_proj, 2, n_heads)
+        pair1 = rows3, swap_cores(rows3, n_dev)
+        h3 = last_up(x3, w_up, 3)
+        rows1 = parts(1, after(fetched1, h3))
+        sent1 = packed(1, 0, pair1[0], after(pair1[1], h3))
         returned1 = chip_trade(after(sent1, fetched1), n_dev)
-        e3 = unpack(1, 0, after(fetched1, sent1))
-        e3 = fetch_rest(1, e3)
-        c2 = back_table(after(d_out, sent1), h3, x3, a3, dz3, e3, w_up, w_down, w_gate, 3, 1)
+        c2, e3 = back_table(after(d_out, sent1), h3, x3, a3, dz3, rows1, w_up, w_down, w_gate, 3, 1, n_heads)
         pair0 = back_plain(c2, h2, x2, g1, w_up, w_down, w_proj, 2, 0)
         sent0 = packed(0, 0, *pair0)
         returned0 = chip_trade(after(sent0, returned1), n_dev)
@@ -804,10 +872,11 @@
         total1 = return_rest(1, total1, pair1)
         placed1 = place_trade(total1, n_dev)
         x_end = last_down(after(x3, *total1), h3, a3, e3, w_down, w_proj, 3, 1)
-        grads = finish_table([after(p, x_end) for p in placed1], None, 1, n_tab)
         total0 = owner_scatter(first_ids[0], after(returned0, x_end), rows_dev, place)
         total0 = return_rest(0, total0, pair0)
-        grads = finish_table(place_exchange(total0, 8), grads, 0, n_tab)
+        placed0 = place_trade(total0, n_dev)
+        grads = finish_table([after(p, *total0) for p in placed1], None, 1, n_tab)
+        grads = finish_table(placed0, grads, 0, n_tab)
         return x_end, grads
 
     return jax.shard_map(step, mesh=mesh, in_specs=(tok_spec, tok_spec, tab_spec, P(), P(), P(), P(), tab_spec),

time: 827 us -> 829 us (level)
  Pallas kernels: 568 us -> 487 us
  waiting for transfers between devices: 88.2 us -> 169 us
  starting transfers between devices: 39.9 us -> 50.4 us
    all_to_all x4, waiting for transfers between devices: 21.4 us -> 112 us  [chip_trade(): return lax.all_to_all(x, 'emb', 0, 0, axis_index_groups=groups, tiled=True)]
    pallas_call x5 -> x3, Pallas kernels: 91 us -> 2.01 us  [the longest x1 2 us: make_ids(): pl.pallas_call(kernel, out_shape=shape_of((n_tgt, n_tab * per, LANES), jn...]
    pallas_call x6 -> x7, Pallas kernels: 361 us -> 372 us  [token_kernel(): pl.pallas_call(kernel, grid=(tokens // tile,), out_shape=[s for s, _ in o...]
    ppermute x7 -> x14, waiting for transfers between devices: 66.8 us -> 56.6 us  [place_trade(): lax.ppermute(blocks[b], 'emb', [(i, i ^ b) for i in range(n_dev)])]
  transfers between devices with their start and end apart: 15 -> 23, of which waited for: 6 -> 9; matrix products, arithmetic and copies ran while one was open for 5% -> 5% of each run, Pallas kernels for 54% -> 45%
where the time goes in v3:
time: 829 us; the launch traced here: 822 us
  Pallas kernels  487 us (59%)
  waiting for transfers between devices  169 us (20%)
  local copies, waits for them, and re-layouts  52.7 us (6%)
  starting transfers between devices  50.4 us (6%)
  other arithmetic  34.9 us (4%)
  between operations  20 us (2%)
    pallas_call x7, Pallas kernels, token_kernel(): pl.pallas_call(kernel, grid=(tokens // tile,), out_shape=[s for s, _ in o...  372 us
    all_to_all x4, waiting for transfers between devices, chip_trade(): return lax.all_to_all(x, 'emb', 0, 0, axis_index_groups=groups, tiled=True)  112 us
    ppermute x14, waiting for transfers between devices, place_trade(): lax.ppermute(blocks[b], 'emb', [(i, i ^ b) for i in range(n_dev)])  56.6 us
    pallas_call x2, Pallas kernels, pack_rows(): pl.pallas_call(kernel, out_shape=shape_of((n_row, LANES), F32), in_specs=...  54.3 us
    sort x2, local copies, waits for them, and re-layouts, step(): lax.sort(after(jnp.stack([plan['by_pos'] for plan in plans]), distinct),...  42 us
    pallas_call x2, Pallas kernels, owner_scatter(): pl.pallas_call(kernel, out_shape=[shape_of((blk_rows, LANES), F32)] * PLA...  27.4 us
    all_to_all x4, starting transfers between devices, chip_trade(): return lax.all_to_all(x, 'emb', 0, 0, axis_index_groups=groups, tiled=True)  26.7 us
  transfers between devices with their start and end apart: 23, of which 9 were waited for; matrix products, arithmetic and copies ran while one was open for 5% of the time, Pallas kernels for 45%

profile of v3, /device:TPU:21, one launch (start us, length us, event | category | flops | bytes accessed | tf_op | source)
XLA Modules:
  0.0 821.9 jit_solution(8365528118705061752)
XLA Ops:
  20.0 7.7 sort.42
  29.8 8.1 sort.43
  49.4 45.7 %shard_map.95.refs_0_ = bf16[2048,1024]{1,0:T(8,128)(2,1)} custom-call(bf16[2048,1024]{1,0:T(8,128)(2,1)} %refs_0_, bf16[4,1024,4096]{2,1,0:T(8,128)(2,1)} %refs_4_.4, bf16[4,4096,1024]{2,1,0:T(8,128)(2,1)} %refs_4_.5), custom_call_target="tpu_custom_call" | custom-call | flops 39600001024 | bytes 8388608 | tf_op jit(solution)/shard_map/pallas_call | solution.py:276
  102.1 42.0 %sort.49.cloned.1.call-done = s32[2,16384]{1,0:T(2,128)} async-done(((s32[2,16384]{1,0:T(2,128)}), s32[2,16384]{1,0:T(2,128)}) %sort.49.cloned.1.call-update) | async-done | bytes 131088 | tf_op jit(solution)/shard_map/sort | solution.py:795
  147.1 7.8 chip_exchange.37
  156.6 12.7 %owner_gather.11 = bf16[5376,2,128]{2,1,0:T(2,128)(2,1)} custom-call(s32[16384]{0:T(1024)} %bitcast.143, bf16[8,2,512,256]{3,2,1,0:T(8,128)(2,1)} %all-to-all-done.served_ref.refs_2_), custom_call_target="tpu_custom_call" | custom-call | flops 12600000512 | bytes 8388608 | tf_op jit(solution)/shard_map/owner_gather/pallas_call | solution.py:81
  178.1 58.2 %shard_map.96 = (bf16[2048,1024]{1,0:T(8,128)(2,1)}, bf16[2048,1024]{1,0:T(8,128)(2,1)}, bf16[5376,2,128]{2,1,0:T(2,128)(2,1)}) custom-call(bf16[2048,1024]{1,0:T(8,128)(2,1)} %shard_map.95.refs_0_, s32[16384]{0:T(1024)} %bitcast.145, bf16[8,2,512,256]{3,2,1,0:T(8,128)(2,1)} %all-to-all-done.served_ref.refs_2_, bf16[4,1024,4096]{2,1,0:T(8,128)(2,1)} %refs_4_.4, ...), custom_call_target="tpu_custom_call" | custom-call | flops 54000001024 | bytes 8388608 | tf_op jit(solution)/shard_map/pallas_call | solution.py:276
  238.6 8.1 while.67
  246.7 76.5 %shard_map.97 = (bf16[2048,1024]{1,0:T(8,128)(2,1)}, bf16[2048,4096]{1,0:T(8,128)(2,1)}, bf16[2048,1024]{1,0:T(8,128)(2,1)}, bf16[2048,1024]{1,0:T(8,128)(2,1)},...) custom-call(bf16[2048,1024]{1,0:T(8,128)(2,1)} %shard_map.95.refs_0_, bf16[2048,1024]{1,0:T(8,128)(2,1)} %get-tuple-element.846.refs_1_, ...), custom_call_target="tpu_custom_call" | custom-call | flops 68400001024 | bytes 8388608 | tf_op jit(solution)/shard_map/pallas_call | solution.py:276
  334.7 25.3 %shard_map.98.refs_1_ = bf16[2048,4096]{1,0:T(8,128)(2,1)} custom-call(bf16[2048,1024]{1,0:T(8,128)(2,1)} %get-tuple-element.886.refs_0_.refs_2_, bf16[4,1024,4096]{2,1,0:T(8,128)(2,1)} %refs_4_.4), custom_call_target="tpu_custom_call" | custom-call | flops 19800000512 | bytes 8388608 | tf_op jit(solution)/shard_map/pallas_call | solution.py:276
  360.1 30.0 %all-to-all-done.2.refs_6_ = bf16[5376,2,128]{2,1,0:T(2,128)(2,1)} async-done(((bf16[5376,2,128]{2,1,0:T(2,128)(2,1)}), bf16[5376,2,128]{2,1,0:T(2,128)(2,1)}, u32[]{:S(2)}, u32[]{:S(2)}) %all-to-all-start.2) | async-done | bytes 2752544 | tf_op jit(solution)/shard_map/all_to_all | solution.py:684
  392.4 27.0 %pack_rows.10 = f32[10752,128]{1,0:T(8,128)} custom-call(s32[16400]{0:T(1024)S(1)} %pad.13.pos_ref, s32[16400]{0:T(1024)} %get-tuple-element.1070.dst_ref, s32[2]{0:T(128)S(1)} %pad_add_fusion.8.span_ref, f32[16384,128]{1,0:T(8,128)} %get-tuple-element.1583.own_ref, f32[16384,128]{1,0:T(8,128)} %collective-permute-done.4.pair_ref), custom_call_target="tpu_custom_call" | custom-call | flops 23399999488 | bytes 8388608 | tf_op jit(solution)/shard_map/pack_rows/pallas_call | solution.py:593
  419.4 6.9 all-to-all-start.3
  426.3 69.9 %shard_map.99 = (f32[2048,1024]{1,0:T(8,128)}, bf16[2048,1024]{1,0:T(8,128)(2,1)}) custom-call(bf16[2048,1024]{1,0:T(8,128)(2,1)} %refs_0_.1, bf16[2048,4096]{1,0:T(8,128)(2,1)} %shard_map.98.refs_1_, bf16[2048,1024]{1,0:T(8,128)(2,1)} %get-tuple-element.886.refs_0_.refs_2_, bf16[2048,1024]{1,0:T(8,128)(2,1)} %get-tuple-element.861.refs_3_.refs_2_, ...), custom_call_target="tpu_custom_call" | custom-call | flops 64799997952 | bytes 8388608 | tf_op jit(solution)/shard_map/pallas_call | solution.py:276
  496.2 58.7 %shard_map.100 = (f32[16384,128]{1,0:T(8,128)}, f32[16384,128]{1,0:T(8,128)}) custom-call(f32[2048,1024]{1,0:T(8,128)} %get-tuple-element.864.refs_0_, bf16[2048,4096]{1,0:T(8,128)(2,1)} %get-tuple-element.865.refs_1_, bf16[2048,1024]{1,0:T(8,128)(2,1)} %get-tuple-element.866.refs_2_, bf16[2048,1024]{1,0:T(8,128)(2,1)} %get-tuple-element.847.refs_2_.refs_3_, ...), custom_call_target="tpu_custom_call" | custom-call | flops 52200001536 | bytes 8388608 | tf_op jit(solution)/shard_map/pallas_call | solution.py:276
  555.0 27.3 %pack_rows.11 = f32[10752,128]{1,0:T(8,128)} custom-call(s32[16400]{0:T(1024)S(1)} %copy-done.55, s32[16400]{0:T(1024)} %get-tuple-element.1067.dst_ref, s32[2]{0:T(128)S(1)} %pad_add_fusion.9.span_ref, f32[16384,128]{1,0:T(8,128)} %get-tuple-element.1652.own_ref, f32[16384,128]{1,0:T(8,128)} %get-tuple-element.1653.pair_ref), custom_call_target="tpu_custom_call" | custom-call | flops 23399999488 | bytes 8388608 | tf_op jit(solution)/shard_map/pack_rows/pallas_call | solution.py:593
  582.3 13.6 %owner_scatter.10 = (f32[1024,128]{1,0:T(8,128)}, f32[1024,128]{1,0:T(8,128)}, f32[1024,128]{1,0:T(8,128)}, f32[1024,128]{1,0:T(8,128)}, f32[1024,128]{1,0:T(8,1...) custom-call(s32[16384]{0:T(1024)} %bitcast.146, s32[1]{0:T(128)} %bitcast.21.place_ref, ...), custom_call_target="tpu_custom_call" | custom-call | flops 17999998976 | bytes 8388608 | tf_op jit(solution)/shard_map/owner_scatter/pallas_call | solution.py:639
  606.4 37.9 %shard_map.101 = bf16[2048,1024]{1,0:T(8,128)(2,1)} custom-call(bf16[2048,1024]{1,0:T(8,128)(2,1)} %get-tuple-element.886.refs_0_.refs_2_, bf16[2048,4096]{1,0:T(8,128)(2,1)} %shard_map.98.refs_1_, bf16[2048,1024]{1,0:T(8,128)(2,1)} %get-tuple-element.861.refs_3_.refs_2_, bf16[2048,1024]{1,0:T(8,128)(2,1)} %get-tuple-element.887.refs_3_, ...), custom_call_target="tpu_custom_call" | custom-call | flops 27000000512 | bytes 8388608 | tf_op jit(solution)/shard_map/pallas_call | solution.py:276
  644.3 82.0 %all-to-all-done.4 = f32[16,672,128]{2,1,0:T(8,128)} async-done(((f32[16,672,128]{2,1,0:T(8,128)}), f32[16,672,128]{2,1,0:T(8,128)}, u32[]{:S(2)}, u32[]{:S(2)}) %all-to-all-start.4) | async-done | bytes 5505056 | tf_op jit(solution)/shard_map/all_to_all | solution.py:684
  726.3 13.8 %owner_scatter.11 = (f32[1024,128]{1,0:T(8,128)}, f32[1024,128]{1,0:T(8,128)}, f32[1024,128]{1,0:T(8,128)}, f32[1024,128]{1,0:T(8,128)}, f32[1024,128]{1,0:T(8,1...) custom-call(s32[16384]{0:T(1024)} %bitcast.144, s32[1]{0:T(128)} %bitcast.21.place_ref, ...), custom_call_target="tpu_custom_call" | custom-call | flops 17999998976 | bytes 8388608 | tf_op jit(solution)/shard_map/owner_scatter/pallas_call | solution.py:639
  745.7 8.5 %collective-permute-done.18.refs_6_ = f32[1024,128]{1,0:T(8,128)} collective-permute-done((f32[1024,128]{1,0:T(8,128)}, f32[1024,128]{1,0:T(8,128)}, u32[]{:S(2)}, u32[]{:S(2)}) %collective-permute-start.18) | collective-permute-done | bytes 524320 | tf_op jit(solution)/shard_map/ppermute | solution.py:721
  754.3 13.1 %collective-permute-done.19.refs_7_ = f32[1024,128]{1,0:T(8,128)S(1)} collective-permute-done((f32[1024,128]{1,0:T(8,128)}, f32[1024,128]{1,0:T(8,128)S(1)}, u32[]{:S(2)}, u32[]{:S(2)}) %collective-permute-start.19) | collective-permute-done | bytes 524320 | tf_op jit(solution)/shard_map/ppermute | solution.py:721
  790.0 9.3 %collective-permute-done.11.refs_6_ = f32[1024,128]{1,0:T(8,128)} collective-permute-done((f32[1024,128]{1,0:T(8,128)}, f32[1024,128]{1,0:T(8,128)}, u32[]{:S(2)}, u32[]{:S(2)}) %collective-permute-start.11) | collective-permute-done | bytes 524320 | tf_op jit(solution)/shard_map/ppermute | solution.py:721
  799.3 12.1 %collective-permute-done.12.refs_7_ = f32[1024,128]{1,0:T(8,128)} collective-permute-done((f32[1024,128]{1,0:T(8,128)}, f32[1024,128]{1,0:T(8,128)}, u32[]{:S(2)}, u32[]{:S(2)}) %collective-permute-start.12) | collective-permute-done | bytes 524320 | tf_op jit(solution)/shard_map/ppermute | solution.py:721
  (157 shorter events, 99.4 us)
Async XLA Ops:
  10.3 9.4 %collective-permute-start.2 = (s32[2,8192]{1,0:T(2,128)S(1)}, s32[2,8192]{1,0:T(2,128)S(1)}, u32[]{:S(2)}, u32[]{:S(2)}) collective-permute-start(s32[2,8192]{1,0:T(2,128)S(1)} %reshape.145), channel_id=1, source_target_pairs={{0,1},{1,0},{2,3},{3,2},{4,5},{5,4},{6,7},{7,6},{8,9},{9,8},{10,11... | collective-permute-start | bytes 196616 | tf_op jit(solution)/shard_map/ppermute | solution.py:679
  14.8 132.2 %all-to-all-start = ((bf16[8,2,512,256]{3,2,1,0:T(8,128)(2,1)}), bf16[8,2,512,256]{3,2,1,0:T(8,128)(2,1)}, u32[]{:S(2)}, u32[]{:S(2)}) async-start(bf16[8,2,512,256]{3,2,1,0:T(8,128)(2,1)} %split_rows.1), calls=%async_computation | async-start | bytes 8388608 | tf_op jit(solution)/shard_map/all_to_all | solution.py:713
  169.3 67.0 %all-to-all-start.1 = ((bf16[5376,2,128]{2,1,0:T(2,128)(2,1)}), bf16[5376,2,128]{2,1,0:T(2,128)(2,1)}, u32[]{:S(2)}, u32[]{:S(2)}) async-start(bf16[5376,2,128]{2,1,0:T(2,128)(2,1)} %owner_gather.11), calls=%async_computation.1 | async-start | bytes 5505024 | tf_op jit(solution)/shard_map/all_to_all | solution.py:684
  236.3 10.4 %collective-permute-start.3 = (bf16[5376,2,128]{2,1,0:T(2,128)(2,1)}, bf16[5376,2,128]{2,1,0:T(2,128)(2,1)}, u32[]{:S(2)}, u32[]{:S(2)}) collective-permute-start(bf16[5376,2,128]{2,1,0:T(2,128)(2,1)} %all-to-all-done.1.refs_5_), channel_id=1, source_target_pairs={{0,1},{1,0},{2,3},{3,2},{4,5},{5,4},{6,7},{7,6},{8,9},{9,8},{10,11... | collective-permute-start | bytes 8257544 | tf_op jit(solution)/shard_map/ppermute | solution.py:679
  323.2 69.1 %collective-permute-start.4 = (f32[16384,128]{1,0:T(8,128)}, f32[16384,128]{1,0:T(8,128)}, u32[]{:S(2)}, u32[]{:S(2)}) collective-permute-start(f32[16384,128]{1,0:T(8,128)} %get-tuple-element.1583.own_ref), channel_id=1, source_target_pairs={{0,1},{1,0},{2,3},{3,2},{4,5},{5,4},{6,7},{7,6},{8,9},{9,8},{10,11... | collective-permute-start | bytes 25165832 | tf_op jit(solution)/shard_map/ppermute | solution.py:679
  323.4 66.7 %all-to-all-start.2 = ((bf16[5376,2,128]{2,1,0:T(2,128)(2,1)}), bf16[5376,2,128]{2,1,0:T(2,128)(2,1)}, u32[]{:S(2)}, u32[]{:S(2)}) async-start(bf16[5376,2,128]{2,1,0:T(2,128)(2,1)} %get-tuple-element.858), calls=%async_computation.2 | async-start | bytes 5505024 | tf_op jit(solution)/shard_map/all_to_all | solution.py:684
  390.1 36.2 %collective-permute-start.5 = (bf16[5376,2,128]{2,1,0:T(2,128)(2,1)}, bf16[5376,2,128]{2,1,0:T(2,128)(2,1)}, u32[]{:S(2)}, u32[]{:S(2)}) collective-permute-start(bf16[5376,2,128]{2,1,0:T(2,128)(2,1)} %all-to-all-done.2.refs_6_), channel_id=1, source_target_pairs={{0,1},{1,0},{2,3},{3,2},{4,5},{5,4},{6,7},{7,6},{8,9},{9,8},{10,11... | collective-permute-start | bytes 8257544 | tf_op jit(solution)/shard_map/ppermute | solution.py:679
  391.6 163.3 %copy-start.63 = (s32[2]{0:T(128)}, s32[2]{0:T(128)S(1)}, u32[]{:S(2)}) copy-start(s32[2]{0:T(128)S(1)} %pad_add_fusion.9.span_ref) | copy-start | bytes 28
  419.4 162.8 %all-to-all-start.3 = ((f32[16,672,128]{2,1,0:T(8,128)}), f32[16,672,128]{2,1,0:T(8,128)}, u32[]{:S(2)}, u32[]{:S(2)}) async-start(f32[16,672,128]{2,1,0:T(8,128)} %bitcast.130), calls=%async_computation.3 | async-start | bytes 11010048 | tf_op jit(solution)/shard_map/all_to_all | solution.py:684
  595.9 130.4 %all-to-all-start.4 = ((f32[16,672,128]{2,1,0:T(8,128)}), f32[16,672,128]{2,1,0:T(8,128)}, u32[]{:S(2)}, u32[]{:S(2)}) async-start(f32[16,672,128]{2,1,0:T(8,128)} %bitcast.129), calls=%async_computation.4 | async-start | bytes 11010048 | tf_op jit(solution)/shard_map/all_to_all | solution.py:684
  602.7 137.4 %collective-permute-start.13 = (f32[1024,128]{1,0:T(8,128)}, f32[1024,128]{1,0:T(8,128)S(1)}, u32[]{:S(2)}, u32[]{:S(2)}) collective-permute-start(f32[1024,128]{1,0:T(8,128)} %get-tuple-element.879), channel_id=1, source_target_pairs={{0,1},{1,0},{2,3},{3,2},{4,5},{5,4},{6,7},{7,6},{8,9},{9,8},{10,11... | collective-permute-start | bytes 1572872 | tf_op jit(solution)/shard_map/ppermute | solution.py:721
  602.9 138.2 %collective-permute-start.14 = (f32[1024,128]{1,0:T(8,128)}, f32[1024,128]{1,0:T(8,128)}, u32[]{:S(2)}, u32[]{:S(2)}) collective-permute-start(f32[1024,128]{1,0:T(8,128)} %get-tuple-element.880), channel_id=1, source_target_pairs={{0,2},{1,3},{2,0},{3,1},{4,6},{5,7},{6,4},{7,5},{8,10},{9,11},{10,... | collective-permute-start | bytes 1572872 | tf_op jit(solution)/shard_map/ppermute | solution.py:721
  604.1 139.5 %collective-permute-start.15 = (f32[1024,128]{1,0:T(8,128)}, f32[1024,128]{1,0:T(8,128)}, u32[]{:S(2)}, u32[]{:S(2)}) collective-permute-start(f32[1024,128]{1,0:T(8,128)} %get-tuple-element.881), channel_id=1, source_target_pairs={{0,3},{1,2},{2,1},{3,0},{4,7},{5,6},{6,5},{7,4},{8,11},{9,10},{10,... | collective-permute-start | bytes 1572872 | tf_op jit(solution)/shard_map/ppermute | solution.py:721
  604.9 138.6 %collective-permute-start.16 = (f32[1024,128]{1,0:T(8,128)}, f32[1024,128]{1,0:T(8,128)}, u32[]{:S(2)}, u32[]{:S(2)}) collective-permute-start(f32[1024,128]{1,0:T(8,128)} %get-tuple-element.882), channel_id=1, source_target_pairs={{0,4},{1,5},{2,6},{3,7},{4,0},{5,1},{6,2},{7,3},{8,12},{9,13},{10,... | collective-permute-start | bytes 1572872 | tf_op jit(solution)/shard_map/ppermute | solution.py:721
  605.2 138.6 %collective-permute-start.17 = (f32[1024,128]{1,0:T(8,128)}, f32[1024,128]{1,0:T(8,128)}, u32[]{:S(2)}, u32[]{:S(2)}) collective-permute-start(f32[1024,128]{1,0:T(8,128)} %get-tuple-element.883), channel_id=1, source_target_pairs={{0,5},{1,4},{2,7},{3,6},{4,1},{5,0},{6,3},{7,2},{8,13},{9,12},{10,... | collective-permute-start | bytes 1572872 | tf_op jit(solution)/shard_map/ppermute | solution.py:721
  740.2 14.1 %collective-permute-start.18 = (f32[1024,128]{1,0:T(8,128)}, f32[1024,128]{1,0:T(8,128)}, u32[]{:S(2)}, u32[]{:S(2)}) collective-permute-start(f32[1024,128]{1,0:T(8,128)} %get-tuple-element.884), channel_id=1, source_target_pairs={{0,6},{1,7},{2,4},{3,5},{4,2},{5,3},{6,0},{7,1},{8,14},{9,15},{10,... | collective-permute-start | bytes 1572872 | tf_op jit(solution)/shard_map/ppermute | solution.py:721
  741.1 26.3 %collective-permute-start.19 = (f32[1024,128]{1,0:T(8,128)}, f32[1024,128]{1,0:T(8,128)S(1)}, u32[]{:S(2)}, u32[]{:S(2)}) collective-permute-start(f32[1024,128]{1,0:T(8,128)} %get-tuple-element.885), channel_id=1, source_target_pairs={{0,7},{1,6},{2,5},{3,4},{4,3},{5,2},{6,1},{7,0},{8,15},{9,14},{10,... | collective-permute-start | bytes 1572872 | tf_op jit(solution)/shard_map/ppermute | solution.py:721
  743.6 23.9 %collective-permute-start.6 = (f32[1024,128]{1,0:T(8,128)}, f32[1024,128]{1,0:T(8,128)S(1)}, u32[]{:S(2)}, u32[]{:S(2)}) collective-permute-start(f32[1024,128]{1,0:T(8,128)} %get-tuple-element.899), channel_id=1, source_target_pairs={{0,1},{1,0},{2,3},{3,2},{4,5},{5,4},{6,7},{7,6},{8,9},{9,8},{10,11... | collective-permute-start | bytes 1572872 | tf_op jit(solution)/shard_map/ppermute | solution.py:721
  743.6 31.3 %collective-permute-start.7 = (f32[1024,128]{1,0:T(8,128)}, f32[1024,128]{1,0:T(8,128)S(1)}, u32[]{:S(2)}, u32[]{:S(2)}) collective-permute-start(f32[1024,128]{1,0:T(8,128)} %get-tuple-element.900), channel_id=1, source_target_pairs={{0,2},{1,3},{2,0},{3,1},{4,6},{5,7},{6,4},{7,5},{8,10},{9,11},{10,... | collective-permute-start | bytes 1572872 | tf_op jit(solution)/shard_map/ppermute | solution.py:721
  743.8 44.0 %collective-permute-start.8 = (f32[1024,128]{1,0:T(8,128)}, f32[1024,128]{1,0:T(8,128)}, u32[]{:S(2)}, u32[]{:S(2)}) collective-permute-start(f32[1024,128]{1,0:T(8,128)} %get-tuple-element.901), channel_id=1, source_target_pairs={{0,3},{1,2},{2,1},{3,0},{4,7},{5,6},{6,5},{7,4},{8,11},{9,10},{10,... | collective-permute-start | bytes 1572872 | tf_op jit(solution)/shard_map/ppermute | solution.py:721
  754.3 33.5 %collective-permute-start.9 = (f32[1024,128]{1,0:T(8,128)}, f32[1024,128]{1,0:T(8,128)}, u32[]{:S(2)}, u32[]{:S(2)}) collective-permute-start(f32[1024,128]{1,0:T(8,128)} %get-tuple-element.902), channel_id=1, source_target_pairs={{0,4},{1,5},{2,6},{3,7},{4,0},{5,1},{6,2},{7,3},{8,12},{9,13},{10,... | collective-permute-start | bytes 1572872 | tf_op jit(solution)/shard_map/ppermute | solution.py:721
  767.4 22.6 %collective-permute-start.10 = (f32[1024,128]{1,0:T(8,128)}, f32[1024,128]{1,0:T(8,128)}, u32[]{:S(2)}, u32[]{:S(2)}) collective-permute-start(f32[1024,128]{1,0:T(8,128)} %get-tuple-element.903), channel_id=1, source_target_pairs={{0,5},{1,4},{2,7},{3,6},{4,1},{5,0},{6,3},{7,2},{8,13},{9,12},{10,... | collective-permute-start | bytes 1572872 | tf_op jit(solution)/shard_map/ppermute | solution.py:721
  767.4 31.8 %collective-permute-start.11 = (f32[1024,128]{1,0:T(8,128)}, f32[1024,128]{1,0:T(8,128)}, u32[]{:S(2)}, u32[]{:S(2)}) collective-permute-start(f32[1024,128]{1,0:T(8,128)} %get-tuple-element.904), channel_id=1, source_target_pairs={{0,6},{1,7},{2,4},{3,5},{4,2},{5,3},{6,0},{7,1},{8,14},{9,15},{10,... | collective-permute-start | bytes 1572872 | tf_op jit(solution)/shard_map/ppermute | solution.py:721
  774.8 36.5 %collective-permute-start.12 = (f32[1024,128]{1,0:T(8,128)}, f32[1024,128]{1,0:T(8,128)}, u32[]{:S(2)}, u32[]{:S(2)}) collective-permute-start(f32[1024,128]{1,0:T(8,128)} %get-tuple-element.905), channel_id=1, source_target_pairs={{0,7},{1,6},{2,5},{3,4},{4,3},{5,2},{6,1},{7,0},{8,15},{9,14},{10,... | collective-permute-start | bytes 1572872 | tf_op jit(solution)/shard_map/ppermute | solution.py:721
  (23 other events, 597.0 us)
Sparse Core Ops, SparseCore 0:
  45.5 41.9 sort.51.cloned.1.call-done
  100.3 43.5 sort.53.cloned.1.call-done
  (2 shorter events, 0.0 us)

commit v4 on v3

--- a/solution.py
+++ b/solution.py
@@ -18,6 +18,7 @@
 SLOTS = 336
 IDW = 1024
 UNROLL = 16
+UNPACK = 32
 LANES = 128
 COLS = 256
 CHUNK = 512
@@ -156,12 +157,12 @@
             first = i * (TILE * heads)
 
             def blk(b, c):
-                for j in range(UNROLL):
-                    row = rec[idx_ref[first + b * UNROLL + j]]
-                    stage[pl.ds(pl.multiple_of(b * UNROLL * pieces, UNROLL * pieces) + pieces * j, pieces), :] = row.astype(F32)
+                for j in range(UNPACK):
+                    row = rec[idx_ref[first + b * UNPACK + j]]
+                    stage[pl.ds(pl.multiple_of(b * UNPACK * pieces, UNPACK * pieces) + pieces * j, pieces), :] = row.astype(F32)
                 return c
 
-            lax.fori_loop(0, TILE * heads // UNROLL, blk, 0)
+            lax.fori_loop(0, TILE * heads // UNPACK, blk, 0)
             if len(ins) > 3:
                 late_ref, rounds_ref = ins[3:]
 
@@ -522,19 +523,24 @@
         compiler_params=local_params(), name="split_rows", cost_estimate=cost(4))(place, tables)
 
 
-def make_ids(distinct, start, count, peak, rnd, rows):
+def make_ids(distinct, marks, rnd, rows):
     n_tab, n_row = distinct.shape[:2]
-    n_tgt = count.shape[0] // n_tab
+    n_mark = marks.shape[0] // n_tab
+    n_tgt = (n_mark - 3) // 2
     depth, per = -(-SLOTS // LANES), IDW // LANES
 
-    def kernel(name_ref, start_ref, count_ref, peak_ref, rnd_ref, out_ref):
+    def kernel(name_ref, mark_ref, rnd_ref, out_ref):
         lane = lax.broadcasted_iota(jnp.int32, (1, LANES), 1)
         shift = rnd_ref[0] * SLOTS
         for t in range(n_tab):
-            out_ref[:, t * per:(t + 1) * per, :] = jnp.full((n_tgt, per, LANES), peak_ref[t], jnp.int32)
+            base = t * n_mark
+            half = mark_ref[base + n_mark - 2]
+            origin = mark_ref[base + half]
+            out_ref[:, t * per:(t + 1) * per, :] = jnp.full((n_tgt, per, LANES), mark_ref[base + n_mark - 1], jnp.int32)
             for g in range(n_tgt):
-                left = jnp.clip(count_ref[t * n_tgt + g] - shift, 0, SLOTS)
-                at = start_ref[t * n_tgt + g] + shift
+                begin = mark_ref[base + half + g]
+                left = jnp.clip(mark_ref[base + half + g + 1] - begin - shift, 0, SLOTS)
+                at = begin - origin + shift
                 row, off = at // LANES, lax.rem(at, LANES)
                 turned = [pltpu.roll(name_ref[t, jnp.minimum(row + i, n_row - 1)], lax.rem(LANES - off, LANES), axis=1)
                           for i in range(depth + 1)]
@@ -544,9 +550,9 @@
 
     return pl.pallas_call(
         kernel, out_shape=shape_of((n_tgt, n_tab * per, LANES), jnp.int32),
-        in_specs=[VMEM_SPEC] + [SMEM_SPEC] * 4, out_specs=VMEM_SPEC, compiler_params=local_params(), name="make_ids",
+        in_specs=[VMEM_SPEC, SMEM_SPEC, SMEM_SPEC], out_specs=VMEM_SPEC, compiler_params=local_params(), name="make_ids",
         cost_estimate=cost(3),
-    )(distinct, start, count, peak, jnp.reshape(rnd, (1,)).astype(jnp.int32))
+    )(distinct, marks, jnp.reshape(rnd, (1,)).astype(jnp.int32))
 
 
 def unpack_rows(idx, rec_own, rec_pair, heads):
@@ -752,12 +758,11 @@
     size = jnp.where(core == 0, n_low, n - n_low)
     begin = jnp.where(core == 0, 0, n_low)
     mine = sid // (n_chip * rows_dev) == core
-    start = lax.dynamic_slice(start, (core * n_chip,), (n_chip,))
+    marks = jnp.concatenate([start, jnp.stack([core * n_chip, jnp.max(count)])])
     return dict(pos=jnp.pad(2 * pos + jnp.where(first, 0, I32.min), (0, UNROLL)),
                 code=jnp.pad(jnp.where(mine, code, -1), (0, UNROLL), constant_values=-1),
-                span=jnp.stack([begin, size]), distinct=jnp.where(first & mine, sid, I32.max), start=start - start[0],
-                by_pos=jnp.where(pos < n_own, pos * (n_dev * 2 * rows_dev) + code, I32.max),
-                count=lax.dynamic_slice(count, (core * n_chip,), (n_chip,)), peak=jnp.max(count))
+                span=jnp.stack([begin, size]), distinct=jnp.where(first & mine, sid, I32.max), marks=marks,
+                by_pos=jnp.where(pos < n_own, pos * (n_dev * 2 * rows_dev) + code, I32.max))
 
 
 def round_slot(code, span, rnd, trash, width):
@@ -801,9 +806,8 @@
             return round_slot(code, span, rnd, trash, width)
 
         def id_blocks(tabs, rnd):
-            start, count = (jnp.concatenate([plans[t][key] for t in tabs]) for key in ('start', 'count'))
-            peak = jnp.stack([plans[t]['peak'] for t in tabs])
-            return make_ids(distinct[tabs[0]:tabs[-1] + 1], start, count, peak, rnd, rows_dev)
+            marks = jnp.concatenate([plans[t]['marks'] for t in tabs])
+            return make_ids(distinct[tabs[0]:tabs[-1] + 1], marks, rnd, rows_dev)
 
         blocks = id_blocks(range(n_tab), jnp.int32(0))
         got = chip_exchange(after(blocks, served, x1), 9, n_chip).reshape(n_chip, n_tab, IDW)
@@ -832,7 +836,14 @@
                 return (rnd + 1, *now)
 
             most = jnp.maximum(*rounds)
-            return lax.while_loop(lambda s: s[0] < most, more, (jnp.int32(1), *start))[1:]
+
+            def nothing():
+                return tuple(empty_array((n_tok, n_heads * row_width), BF16) for _ in range(n_tab))
+
+            def loop():
+                return lax.while_loop(lambda s: s[0] < most, more, (jnp.int32(1), *nothing()))[1:]
+
+            return lax.cond(after(most, *start) > 1, loop, nothing)
 
         def parts(which, own):
             return own_slot(which, 0), own, swap_cores(own, n_dev), late[which], rounds[which].reshape(1)
@@ -855,8 +866,8 @@
         sent0 = owner_gather(first_ids[0], served, 0, n_chip)
         fetched0 = chip_trade(sent0, n_dev)
         m1, g1, sent1 = layer_table_head(after(x1, sent0), w_up, w_down, w_gate, 1, 0, first_ids[1], served, n_chip)
-        late = late_rows([after(empty_array((n_tok, n_heads * row_width), BF16), m1, fetched0) for _ in range(n_tab)])
-        rows0 = parts(0, after(fetched0, m1))
+        late = late_rows((m1, fetched0))
+        rows0 = parts(0, after(fetched0, *late))
         fetched1 = chip_trade(after(sent1, fetched0, *late), n_dev)
         x2, h2, x3, a3, dz3, rows3 = layer_middle(x1, m1, g1, rows0, d_out, w_up, w_down, w_gate, w_proj, 2, n_heads)
         pair1 = rows3, swap_cores(rows3, n_dev)

time: 829 us -> 828 us (level)
  transfers between devices with their start and end apart: 23 -> 23, of which waited for: 9 -> 10; matrix products, arithmetic and copies ran while one was open for 5% -> 5% of each run, Pallas kernels for 45% -> 45%
where the time goes in v4:
time: 828 us; the launch traced here: 822 us
  Pallas kernels  484 us (58%)
  waiting for transfers between devices  173 us (21%)
  local copies, waits for them, and re-layouts  52.2 us (6%)
  starting transfers between devices  50.2 us (6%)
  other arithmetic  33.5 us (4%)
  between operations  20.3 us (2%)
  loops' own time  8.35 us (1%)
    pallas_call x7, Pallas kernels, token_kernel(): pl.pallas_call(kernel, grid=(tokens // tile,), out_shape=[s for s, _ in o...  369 us
    all_to_all x4, waiting for transfers between devices, chip_trade(): return lax.all_to_all(x, 'emb', 0, 0, axis_index_groups=groups, tiled=True)  112 us
    ppermute x14, waiting for transfers between devices, place_trade(): lax.ppermute(blocks[b], 'emb', [(i, i ^ b) for i in range(n_dev)])  56.8 us
    pallas_call x2, Pallas kernels, pack_rows(): pl.pallas_call(kernel, out_shape=shape_of((n_row, LANES), F32), in_specs=...  54.3 us
    sort x2, local copies, waits for them, and re-layouts, step(): lax.sort(after(jnp.stack([plan['by_pos'] for plan in plans]), distinct),...  42.3 us
    pallas_call x2, Pallas kernels, owner_scatter(): pl.pallas_call(kernel, out_shape=[shape_of((blk_rows, LANES), F32)] * PLA...  27.4 us
    all_to_all x4, starting transfers between devices, chip_trade(): return lax.all_to_all(x, 'emb', 0, 0, axis_index_groups=groups, tiled=True)  26.6 us
  transfers between devices with their start and end apart: 23, of which 10 were waited for; matrix products, arithmetic and copies ran while one was open for 5% of the time, Pallas kernels for 45%

profile of v4, /device:TPU:21, one launch (start us, length us, event | category | flops | bytes accessed | tf_op | source)
XLA Modules:
  0.0 821.5 jit_solution(11637419316263336353)
XLA Ops:
  20.0 7.7 sort.42
  28.6 8.1 sort.43
  45.4 45.8 %shard_map.95.refs_0_ = bf16[2048,1024]{1,0:T(8,128)(2,1)} custom-call(bf16[2048,1024]{1,0:T(8,128)(2,1)} %refs_0_, bf16[4,1024,4096]{2,1,0:T(8,128)(2,1)} %refs_4_.4, bf16[4,4096,1024]{2,1,0:T(8,128)(2,1)} %refs_4_.5), custom_call_target="tpu_custom_call" | custom-call | flops 39600001024 | bytes 8388608 | tf_op jit(solution)/shard_map/pallas_call | solution.py:277
  99.3 42.2 %sort.49.cloned.1.call-done = s32[2,16384]{1,0:T(2,128)} async-done(((s32[2,16384]{1,0:T(2,128)}), s32[2,16384]{1,0:T(2,128)}) %sort.49.cloned.1.call-update) | async-done | bytes 131088 | tf_op jit(solution)/shard_map/sort | solution.py:800
  143.0 7.8 chip_exchange.37
  152.5 12.7 %owner_gather.11 = bf16[5376,2,128]{2,1,0:T(2,128)(2,1)} custom-call(s32[16384]{0:T(1024)} %bitcast.136, bf16[8,2,512,256]{3,2,1,0:T(8,128)(2,1)} %all-to-all-done.served_ref.refs_2_), custom_call_target="tpu_custom_call" | custom-call | flops 12600000512 | bytes 8388608 | tf_op jit(solution)/shard_map/owner_gather/pallas_call | solution.py:82
  174.1 58.3 %shard_map.96 = (bf16[2048,1024]{1,0:T(8,128)(2,1)}, bf16[2048,1024]{1,0:T(8,128)(2,1)}, bf16[5376,2,128]{2,1,0:T(2,128)(2,1)}) custom-call(bf16[2048,1024]{1,0:T(8,128)(2,1)} %shard_map.95.refs_0_, s32[16384]{0:T(1024)} %bitcast.138, bf16[8,2,512,256]{3,2,1,0:T(8,128)(2,1)} %all-to-all-done.served_ref.refs_2_, bf16[4,1024,4096]{2,1,0:T(8,128)(2,1)} %refs_4_.4, ...), custom_call_target="tpu_custom_call" | custom-call | flops 54000001024 | bytes 8388608 | tf_op jit(solution)/shard_map/pallas_call | solution.py:277
  232.4 8.3 %conditional.1 = (bf16[2048,1024]{1,0:T(8,128)(2,1)}, bf16[2048,1024]{1,0:T(8,128)(2,1)}) conditional(s32[]{:T(128)} %convert_element_type.19, () %tuple.85, (s32[2,8192]{1,0:T(2,128)S(1)}, s32[]{:T(128)}, s32[]{:T(128)}, s32[2,128,1,128]{3,2,1,0:T(1,128)}, s32[35]{0:T(128)}, /*index=5*/bf16[8,2,512,256]{3,2,1,0:T(8,128)(2,1)}, ...), branch_computations={%region_16.17_spmd, %region_17.20_spmd} | conditional | flops 419404906496 | bytes 151814928 | solution.py:846
  248.1 74.9 %shard_map.97 = (bf16[2048,1024]{1,0:T(8,128)(2,1)}, bf16[2048,4096]{1,0:T(8,128)(2,1)}, bf16[2048,1024]{1,0:T(8,128)(2,1)}, bf16[2048,1024]{1,0:T(8,128)(2,1)},...) custom-call(bf16[2048,1024]{1,0:T(8,128)(2,1)} %shard_map.95.refs_0_, bf16[2048,1024]{1,0:T(8,128)(2,1)} %get-tuple-element.768.refs_1_, ...), custom_call_target="tpu_custom_call" | custom-call | flops 68400001024 | bytes 8388608 | tf_op jit(solution)/shard_map/pallas_call | solution.py:277
  335.8 25.4 %shard_map.98.refs_1_ = bf16[2048,4096]{1,0:T(8,128)(2,1)} custom-call(bf16[2048,1024]{1,0:T(8,128)(2,1)} %get-tuple-element.807.refs_0_.refs_2_, bf16[4,1024,4096]{2,1,0:T(8,128)(2,1)} %refs_4_.4), custom_call_target="tpu_custom_call" | custom-call | flops 19800000512 | bytes 8388608 | tf_op jit(solution)/shard_map/pallas_call | solution.py:277
  361.2 29.8 %all-to-all-done.2.refs_6_ = bf16[5376,2,128]{2,1,0:T(2,128)(2,1)} async-done(((bf16[5376,2,128]{2,1,0:T(2,128)(2,1)}), bf16[5376,2,128]{2,1,0:T(2,128)(2,1)}, u32[]{:S(2)}, u32[]{:S(2)}) %all-to-all-start.2) | async-done | bytes 2752544 | tf_op jit(solution)/shard_map/all_to_all | solution.py:690
  393.6 27.0 %pack_rows.10 = f32[10752,128]{1,0:T(8,128)} custom-call(s32[16400]{0:T(1024)S(1)} %pad.13.pos_ref, s32[16400]{0:T(1024)} %get-tuple-element.975.dst_ref, s32[2]{0:T(128)S(1)} %pad_add_fusion.7.span_ref, f32[16384,128]{1,0:T(8,128)} %get-tuple-element.1424.own_ref, f32[16384,128]{1,0:T(8,128)} %collective-permute-done.4.pair_ref), custom_call_target="tpu_custom_call" | custom-call | flops 23399999488 | bytes 8388608 | tf_op jit(solution)/shard_map/pack_rows/pallas_call | solution.py:599
  427.4 68.2 %shard_map.99 = (f32[2048,1024]{1,0:T(8,128)}, bf16[2048,1024]{1,0:T(8,128)(2,1)}) custom-call(bf16[2048,1024]{1,0:T(8,128)(2,1)} %refs_0_.1, bf16[2048,4096]{1,0:T(8,128)(2,1)} %shard_map.98.refs_1_, bf16[2048,1024]{1,0:T(8,128)(2,1)} %get-tuple-element.807.refs_0_.refs_2_, bf16[2048,1024]{1,0:T(8,128)(2,1)} %get-tuple-element.782.refs_3_.refs_2_, ...), custom_call_target="tpu_custom_call" | custom-call | flops 64799997952 | bytes 8388608 | tf_op jit(solution)/shard_map/pallas_call | solution.py:277
  495.7 58.9 %shard_map.100 = (f32[16384,128]{1,0:T(8,128)}, f32[16384,128]{1,0:T(8,128)}) custom-call(f32[2048,1024]{1,0:T(8,128)} %get-tuple-element.785.refs_0_, bf16[2048,4096]{1,0:T(8,128)(2,1)} %get-tuple-element.786.refs_1_, bf16[2048,1024]{1,0:T(8,128)(2,1)} %get-tuple-element.787.refs_2_, bf16[2048,1024]{1,0:T(8,128)(2,1)} %get-tuple-element.769.refs_2_.refs_3_, ...), custom_call_target="tpu_custom_call" | custom-call | flops 52200001536 | bytes 8388608 | tf_op jit(solution)/shard_map/pallas_call | solution.py:277
  554.5 27.3 %pack_rows.11 = f32[10752,128]{1,0:T(8,128)} custom-call(s32[16400]{0:T(1024)S(1)} %copy-done.64, s32[16400]{0:T(1024)} %get-tuple-element.972.dst_ref, s32[2]{0:T(128)S(1)} %copy-done.72, f32[16384,128]{1,0:T(8,128)} %get-tuple-element.1487.own_ref, f32[16384,128]{1,0:T(8,128)} %get-tuple-element.1488.pair_ref), custom_call_target="tpu_custom_call" | custom-call | flops 23399999488 | bytes 8388608 | tf_op jit(solution)/shard_map/pack_rows/pallas_call | solution.py:599
  581.8 13.6 %owner_scatter.10 = (f32[1024,128]{1,0:T(8,128)}, f32[1024,128]{1,0:T(8,128)}, f32[1024,128]{1,0:T(8,128)}, f32[1024,128]{1,0:T(8,128)}, f32[1024,128]{1,0:T(8,1...) custom-call(s32[16384]{0:T(1024)} %bitcast.139, s32[1]{0:T(128)} %bitcast.21.place_ref, ...), custom_call_target="tpu_custom_call" | custom-call | flops 17999998976 | bytes 8388608 | tf_op jit(solution)/shard_map/owner_scatter/pallas_call | solution.py:645
  595.5 6.8 all-to-all-start.4
  606.0 37.9 %shard_map.101 = bf16[2048,1024]{1,0:T(8,128)(2,1)} custom-call(bf16[2048,1024]{1,0:T(8,128)(2,1)} %get-tuple-element.807.refs_0_.refs_2_, bf16[2048,4096]{1,0:T(8,128)(2,1)} %shard_map.98.refs_1_, bf16[2048,1024]{1,0:T(8,128)(2,1)} %get-tuple-element.782.refs_3_.refs_2_, bf16[2048,1024]{1,0:T(8,128)(2,1)} %get-tuple-element.808.refs_3_, ...), custom_call_target="tpu_custom_call" | custom-call | flops 27000000512 | bytes 8388608 | tf_op jit(solution)/shard_map/pallas_call | solution.py:277
  643.9 82.0 %all-to-all-done.4 = f32[16,672,128]{2,1,0:T(8,128)} async-done(((f32[16,672,128]{2,1,0:T(8,128)}), f32[16,672,128]{2,1,0:T(8,128)}, u32[]{:S(2)}, u32[]{:S(2)}) %all-to-all-start.4) | async-done | bytes 5505056 | tf_op jit(solution)/shard_map/all_to_all | solution.py:690
  726.0 13.8 %owner_scatter.11 = (f32[1024,128]{1,0:T(8,128)}, f32[1024,128]{1,0:T(8,128)}, f32[1024,128]{1,0:T(8,128)}, f32[1024,128]{1,0:T(8,128)}, f32[1024,128]{1,0:T(8,1...) custom-call(s32[16384]{0:T(1024)} %bitcast.137, s32[1]{0:T(128)} %bitcast.21.place_ref, ...), custom_call_target="tpu_custom_call" | custom-call | flops 17999998976 | bytes 8388608 | tf_op jit(solution)/shard_map/owner_scatter/pallas_call | solution.py:645
  745.3 8.6 %collective-permute-done.18.refs_6_ = f32[1024,128]{1,0:T(8,128)} collective-permute-done((f32[1024,128]{1,0:T(8,128)}, f32[1024,128]{1,0:T(8,128)}, u32[]{:S(2)}, u32[]{:S(2)}) %collective-permute-start.18) | collective-permute-done | bytes 524320 | tf_op jit(solution)/shard_map/ppermute | solution.py:727
  753.9 13.0 %collective-permute-done.19.refs_7_ = f32[1024,128]{1,0:T(8,128)S(1)} collective-permute-done((f32[1024,128]{1,0:T(8,128)}, f32[1024,128]{1,0:T(8,128)S(1)}, u32[]{:S(2)}, u32[]{:S(2)}) %collective-permute-start.19) | collective-permute-done | bytes 524320 | tf_op jit(solution)/shard_map/ppermute | solution.py:727
  789.6 9.4 %collective-permute-done.11.refs_6_ = f32[1024,128]{1,0:T(8,128)} collective-permute-done((f32[1024,128]{1,0:T(8,128)}, f32[1024,128]{1,0:T(8,128)}, u32[]{:S(2)}, u32[]{:S(2)}) %collective-permute-start.11) | collective-permute-done | bytes 524320 | tf_op jit(solution)/shard_map/ppermute | solution.py:727
  798.9 12.0 %collective-permute-done.12.refs_7_ = f32[1024,128]{1,0:T(8,128)} collective-permute-done((f32[1024,128]{1,0:T(8,128)}, f32[1024,128]{1,0:T(8,128)}, u32[]{:S(2)}, u32[]{:S(2)}) %collective-permute-start.12) | collective-permute-done | bytes 524320 | tf_op jit(solution)/shard_map/ppermute | solution.py:727
  (156 shorter events, 101.5 us)
Async XLA Ops:
  10.3 9.3 %collective-permute-start.2 = (s32[2,8192]{1,0:T(2,128)S(1)}, s32[2,8192]{1,0:T(2,128)S(1)}, u32[]{:S(2)}, u32[]{:S(2)}) collective-permute-start(s32[2,8192]{1,0:T(2,128)S(1)} %reshape.149), channel_id=1, source_target_pairs={{0,1},{1,0},{2,3},{3,2},{4,5},{5,4},{6,7},{7,6},{8,9},{9,8},{10,11... | collective-permute-start | bytes 196616 | tf_op jit(solution)/shard_map/ppermute | solution.py:685
  14.8 128.2 %all-to-all-start = ((bf16[8,2,512,256]{3,2,1,0:T(8,128)(2,1)}), bf16[8,2,512,256]{3,2,1,0:T(8,128)(2,1)}, u32[]{:S(2)}, u32[]{:S(2)}) async-start(bf16[8,2,512,256]{3,2,1,0:T(8,128)(2,1)} %split_rows.1), calls=%async_computation | async-start | bytes 8388608 | tf_op jit(solution)/shard_map/all_to_all | solution.py:719
  45.3 96.1 %sort.49.cloned.1.call-start = ((), (), s32[]{:S(2)}) async-start(), calls=%async_computation.6 | async-start | bytes 393248 | tf_op jit(solution)/shard_map/sort | solution.py:800
  165.3 67.1 %all-to-all-start.1 = ((bf16[5376,2,128]{2,1,0:T(2,128)(2,1)}), bf16[5376,2,128]{2,1,0:T(2,128)(2,1)}, u32[]{:S(2)}, u32[]{:S(2)}) async-start(bf16[5376,2,128]{2,1,0:T(2,128)(2,1)} %owner_gather.11), calls=%async_computation.1 | async-start | bytes 5505024 | tf_op jit(solution)/shard_map/all_to_all | solution.py:690
  240.8 7.3 collective-permute-start.3
  323.1 70.5 %collective-permute-start.4 = (f32[16384,128]{1,0:T(8,128)}, f32[16384,128]{1,0:T(8,128)}, u32[]{:S(2)}, u32[]{:S(2)}) collective-permute-start(f32[16384,128]{1,0:T(8,128)} %get-tuple-element.1424.own_ref), channel_id=1, source_target_pairs={{0,1},{1,0},{2,3},{3,2},{4,5},{5,4},{6,7},{7,6},{8,9},{9,8},{10,11... | collective-permute-start | bytes 25165832 | tf_op jit(solution)/shard_map/ppermute | solution.py:685
  323.5 67.4 %all-to-all-start.2 = ((bf16[5376,2,128]{2,1,0:T(2,128)(2,1)}), bf16[5376,2,128]{2,1,0:T(2,128)(2,1)}, u32[]{:S(2)}, u32[]{:S(2)}) async-start(bf16[5376,2,128]{2,1,0:T(2,128)(2,1)} %get-tuple-element.779), calls=%async_computation.2 | async-start | bytes 5505024 | tf_op jit(solution)/shard_map/all_to_all | solution.py:690
  390.9 36.5 %collective-permute-start.5 = (bf16[5376,2,128]{2,1,0:T(2,128)(2,1)}, bf16[5376,2,128]{2,1,0:T(2,128)(2,1)}, u32[]{:S(2)}, u32[]{:S(2)}) collective-permute-start(bf16[5376,2,128]{2,1,0:T(2,128)(2,1)} %all-to-all-done.2.refs_6_), channel_id=1, source_target_pairs={{0,1},{1,0},{2,3},{3,2},{4,5},{5,4},{6,7},{7,6},{8,9},{9,8},{10,11... | collective-permute-start | bytes 8257544 | tf_op jit(solution)/shard_map/ppermute | solution.py:685
  420.6 161.2 %all-to-all-start.3 = ((f32[16,672,128]{2,1,0:T(8,128)}), f32[16,672,128]{2,1,0:T(8,128)}, u32[]{:S(2)}, u32[]{:S(2)}) async-start(f32[16,672,128]{2,1,0:T(8,128)} %bitcast.119), calls=%async_computation.3 | async-start | bytes 11010048 | tf_op jit(solution)/shard_map/all_to_all | solution.py:690
  595.5 130.5 %all-to-all-start.4 = ((f32[16,672,128]{2,1,0:T(8,128)}), f32[16,672,128]{2,1,0:T(8,128)}, u32[]{:S(2)}, u32[]{:S(2)}) async-start(f32[16,672,128]{2,1,0:T(8,128)} %bitcast.118), calls=%async_computation.4 | async-start | bytes 11010048 | tf_op jit(solution)/shard_map/all_to_all | solution.py:690
  602.3 137.5 %collective-permute-start.13 = (f32[1024,128]{1,0:T(8,128)}, f32[1024,128]{1,0:T(8,128)S(1)}, u32[]{:S(2)}, u32[]{:S(2)}) collective-permute-start(f32[1024,128]{1,0:T(8,128)} %get-tuple-element.800), channel_id=1, source_target_pairs={{0,1},{1,0},{2,3},{3,2},{4,5},{5,4},{6,7},{7,6},{8,9},{9,8},{10,11... | collective-permute-start | bytes 1572872 | tf_op jit(solution)/shard_map/ppermute | solution.py:727
  602.4 138.2 %collective-permute-start.14 = (f32[1024,128]{1,0:T(8,128)}, f32[1024,128]{1,0:T(8,128)}, u32[]{:S(2)}, u32[]{:S(2)}) collective-permute-start(f32[1024,128]{1,0:T(8,128)} %get-tuple-element.801), channel_id=1, source_target_pairs={{0,2},{1,3},{2,0},{3,1},{4,6},{5,7},{6,4},{7,5},{8,10},{9,11},{10,... | collective-permute-start | bytes 1572872 | tf_op jit(solution)/shard_map/ppermute | solution.py:727
  603.6 139.5 %collective-permute-start.15 = (f32[1024,128]{1,0:T(8,128)}, f32[1024,128]{1,0:T(8,128)}, u32[]{:S(2)}, u32[]{:S(2)}) collective-permute-start(f32[1024,128]{1,0:T(8,128)} %get-tuple-element.802), channel_id=1, source_target_pairs={{0,3},{1,2},{2,1},{3,0},{4,7},{5,6},{6,5},{7,4},{8,11},{9,10},{10,... | collective-permute-start | bytes 1572872 | tf_op jit(solution)/shard_map/ppermute | solution.py:727
  604.5 138.6 %collective-permute-start.16 = (f32[1024,128]{1,0:T(8,128)}, f32[1024,128]{1,0:T(8,128)}, u32[]{:S(2)}, u32[]{:S(2)}) collective-permute-start(f32[1024,128]{1,0:T(8,128)} %get-tuple-element.803), channel_id=1, source_target_pairs={{0,4},{1,5},{2,6},{3,7},{4,0},{5,1},{6,2},{7,3},{8,12},{9,13},{10,... | collective-permute-start | bytes 1572872 | tf_op jit(solution)/shard_map/ppermute | solution.py:727
  604.8 138.6 %collective-permute-start.17 = (f32[1024,128]{1,0:T(8,128)}, f32[1024,128]{1,0:T(8,128)}, u32[]{:S(2)}, u32[]{:S(2)}) collective-permute-start(f32[1024,128]{1,0:T(8,128)} %get-tuple-element.804), channel_id=1, source_target_pairs={{0,5},{1,4},{2,7},{3,6},{4,1},{5,0},{6,3},{7,2},{8,13},{9,12},{10,... | collective-permute-start | bytes 1572872 | tf_op jit(solution)/shard_map/ppermute | solution.py:727
  739.8 14.1 %collective-permute-start.18 = (f32[1024,128]{1,0:T(8,128)}, f32[1024,128]{1,0:T(8,128)}, u32[]{:S(2)}, u32[]{:S(2)}) collective-permute-start(f32[1024,128]{1,0:T(8,128)} %get-tuple-element.805), channel_id=1, source_target_pairs={{0,6},{1,7},{2,4},{3,5},{4,2},{5,3},{6,0},{7,1},{8,14},{9,15},{10,... | collective-permute-start | bytes 1572872 | tf_op jit(solution)/shard_map/ppermute | solution.py:727
  740.6 26.3 %collective-permute-start.19 = (f32[1024,128]{1,0:T(8,128)}, f32[1024,128]{1,0:T(8,128)S(1)}, u32[]{:S(2)}, u32[]{:S(2)}) collective-permute-start(f32[1024,128]{1,0:T(8,128)} %get-tuple-element.806), channel_id=1, source_target_pairs={{0,7},{1,6},{2,5},{3,4},{4,3},{5,2},{6,1},{7,0},{8,15},{9,14},{10,... | collective-permute-start | bytes 1572872 | tf_op jit(solution)/shard_map/ppermute | solution.py:727
  743.1 23.9 %collective-permute-start.6 = (f32[1024,128]{1,0:T(8,128)}, f32[1024,128]{1,0:T(8,128)S(1)}, u32[]{:S(2)}, u32[]{:S(2)}) collective-permute-start(f32[1024,128]{1,0:T(8,128)} %get-tuple-element.820), channel_id=1, source_target_pairs={{0,1},{1,0},{2,3},{3,2},{4,5},{5,4},{6,7},{7,6},{8,9},{9,8},{10,11... | collective-permute-start | bytes 1572872 | tf_op jit(solution)/shard_map/ppermute | solution.py:727
  743.1 31.4 %collective-permute-start.7 = (f32[1024,128]{1,0:T(8,128)}, f32[1024,128]{1,0:T(8,128)S(1)}, u32[]{:S(2)}, u32[]{:S(2)}) collective-permute-start(f32[1024,128]{1,0:T(8,128)} %get-tuple-element.821), channel_id=1, source_target_pairs={{0,2},{1,3},{2,0},{3,1},{4,6},{5,7},{6,4},{7,5},{8,10},{9,11},{10,... | collective-permute-start | bytes 1572872 | tf_op jit(solution)/shard_map/ppermute | solution.py:727
  743.4 44.0 %collective-permute-start.8 = (f32[1024,128]{1,0:T(8,128)}, f32[1024,128]{1,0:T(8,128)}, u32[]{:S(2)}, u32[]{:S(2)}) collective-permute-start(f32[1024,128]{1,0:T(8,128)} %get-tuple-element.822), channel_id=1, source_target_pairs={{0,3},{1,2},{2,1},{3,0},{4,7},{5,6},{6,5},{7,4},{8,11},{9,10},{10,... | collective-permute-start | bytes 1572872 | tf_op jit(solution)/shard_map/ppermute | solution.py:727
  753.9 33.5 %collective-permute-start.9 = (f32[1024,128]{1,0:T(8,128)}, f32[1024,128]{1,0:T(8,128)}, u32[]{:S(2)}, u32[]{:S(2)}) collective-permute-start(f32[1024,128]{1,0:T(8,128)} %get-tuple-element.823), channel_id=1, source_target_pairs={{0,4},{1,5},{2,6},{3,7},{4,0},{5,1},{6,2},{7,3},{8,12},{9,13},{10,... | collective-permute-start | bytes 1572872 | tf_op jit(solution)/shard_map/ppermute | solution.py:727
  767.0 22.6 %collective-permute-start.10 = (f32[1024,128]{1,0:T(8,128)}, f32[1024,128]{1,0:T(8,128)}, u32[]{:S(2)}, u32[]{:S(2)}) collective-permute-start(f32[1024,128]{1,0:T(8,128)} %get-tuple-element.824), channel_id=1, source_target_pairs={{0,5},{1,4},{2,7},{3,6},{4,1},{5,0},{6,3},{7,2},{8,13},{9,12},{10,... | collective-permute-start | bytes 1572872 | tf_op jit(solution)/shard_map/ppermute | solution.py:727
  767.0 31.9 %collective-permute-start.11 = (f32[1024,128]{1,0:T(8,128)}, f32[1024,128]{1,0:T(8,128)}, u32[]{:S(2)}, u32[]{:S(2)}) collective-permute-start(f32[1024,128]{1,0:T(8,128)} %get-tuple-element.825), channel_id=1, source_target_pairs={{0,6},{1,7},{2,4},{3,5},{4,2},{5,3},{6,0},{7,1},{8,14},{9,15},{10,... | collective-permute-start | bytes 1572872 | tf_op jit(solution)/shard_map/ppermute | solution.py:727
  774.6 36.4 %collective-permute-start.12 = (f32[1024,128]{1,0:T(8,128)}, f32[1024,128]{1,0:T(8,128)}, u32[]{:S(2)}, u32[]{:S(2)}) collective-permute-start(f32[1024,128]{1,0:T(8,128)} %get-tuple-element.826), channel_id=1, source_target_pairs={{0,7},{1,6},{2,5},{3,4},{4,3},{5,2},{6,1},{7,0},{8,15},{9,14},{10,... | collective-permute-start | bytes 1572872 | tf_op jit(solution)/shard_map/ppermute | solution.py:727
  (25 other events, 658.8 us)
Sparse Core Ops, SparseCore 0:
  45.5 42.7 sort.51.cloned.1.call-done
  97.6 43.5 sort.53.cloned.1.call-done
  (2 shorter events, 0.0 us)
